TPU v7x, 32 devices: a whole 2x2x4 slice. The times are simulated.
32 devices in a mesh: dom: 2 (over x), shard: 16 (over z, y, core).
Axes of the slice: x: 2, y: 2, z: 4, core: 2. Of those that a mesh axis runs over, the one named last changes fastest.
Arguments:
- activations: bfloat16 [4096, 8192], P(('dom', 'shard')), parts along dimension 0, may hold values from -6 to 6
- out_grads: bfloat16 [4096, 28672], P(('dom', 'shard')), parts along dimension 0, may hold values from -6 to 6
- example_ids: int32 [32, 128], P(('dom', 'shard')), parts along dimension 0, may hold values from 0 to 7, never falling along the last dimension, each value on 1 to 32 neighbouring positions
- in_factor: bfloat16 [64, 8192], P(None, 'shard'), may hold values from -0.0625 to 0.0625
- out_factor: bfloat16 [64, 28672], P(None, 'shard'), may hold values from -0.03125 to 0.03125
- query_grads: float32 [128, 4096], P('shard'), may hold values from -6 to 6
- basis_in: float32 [64, 64], replicated, may hold values from -0.75 to 0.75
- basis_out: float32 [64, 64], replicated, may hold values from -0.75 to 0.75
- eigen: float32 [64, 64], replicated, may hold values from 0.5 to 4
Outputs:
- scores: float32 [256, 128], P('dom', 'shard'), parts along dimension 0
There are 2 independent parts, one for each index of `dom`. A program takes and returns all parts, laid end to end along the dimension named above; an argument that names none is the same for every part. Nothing has to cross between parts.
Inputs may be any that keep to these rules, and one draw needn't show every extreme that they name: `example_ids`: in each row (the 128 tokens of one shard) the example numbers never fall, and every number from 0 to 7 covers 1 to 32 tokens.
All inputs are finite; a program needn't handle non-finite values.
Results may differ from a plain program's by a relative error of at most 0.005.
Values may be sent and summed in bfloat16 or wider, within the bound.
No kernel may reach another device: no remote copies, remote signals or barrier semaphores. Data moves between devices by JAX's collectives and lax.ppermute only.
A program may use at most 128 MiB of HBM per device.

v0:
```python
import jax
import jax.numpy as jnp
from jax import lax
from jax.sharding import PartitionSpec as P

EX_DEV = 8


def precondition(query_grads, basis_in, basis_out, eigen):
    rank = basis_in.shape[0]
    grads = query_grads.reshape(-1, rank, rank)
    rotated = jnp.einsum(
        "ai,qab,bj->qij", basis_in, grads, basis_out, precision=lax.Precision.HIGHEST
    )
    scaled = rotated / eigen
    restored = jnp.einsum(
        "ia,qab,jb->qij", basis_in, scaled, basis_out, precision=lax.Precision.HIGHEST
    )
    return restored.reshape(grads.shape[0], -1).astype(jnp.bfloat16)


def fold_columns(features, piece):
    return lax.dot_general(
        features, piece, (((1,), (1,)), ((), ())), preferred_element_type=jnp.float32
    )


def on_device(
    activations,
    out_grads,
    example_ids,
    in_factor,
    out_factor,
    query_grads,
    basis_in,
    basis_out,
    eigen,
):
    rank = in_factor.shape[0]
    proj_in = fold_columns(
        activations, lax.all_gather(in_factor, "shard", axis=1, tiled=True)
    ).astype(jnp.bfloat16)
    proj_out = fold_columns(
        out_grads, lax.all_gather(out_factor, "shard", axis=1, tiled=True)
    ).astype(jnp.bfloat16)
    precond = precondition(query_grads, basis_in, basis_out, eigen)
    total_examples = EX_DEV * lax.axis_size("shard")
    global_ids = example_ids[0] + lax.axis_index("shard") * EX_DEV
    query_mats = precond.reshape(-1, rank, rank)
    rows_in = lax.all_gather(proj_in, "shard", axis=0, tiled=True)
    rows_out = lax.all_gather(proj_out, "shard", axis=0, tiled=True)
    owners = lax.all_gather(global_ids, "shard", axis=0, tiled=True)
    turned = jnp.einsum("ti,qij->tqj", rows_in, query_mats, preferred_element_type=jnp.float32)
    per_token = jnp.sum(turned * rows_out.astype(jnp.float32)[:, None, :], axis=2)
    scores = jax.ops.segment_sum(per_token, owners, num_segments=total_examples)
    return scores * 0.00390625


def solution(mesh):
    placed = (
        P(("dom", "shard"), None),
        P(("dom", "shard"), None),
        P(("dom", "shard"), None),
        P(None, "shard"),
        P(None, "shard"),
        P("shard", None),
        P(),
        P(),
        P(),
    )
    return jax.shard_map(
        on_device, mesh=mesh, in_specs=placed, out_specs=P("dom", "shard"), check_vma=False
    )
```

profile of v0, /device:TPU:0, one launch (start us, length us, event | category | flops | bytes accessed | tf_op | source)
XLA Modules:
  0.0 148.1 jit_solution(9690514091207022177)
XLA Ops:
  6.5 0.0 copy-start
  6.5 0.0 all-gather.4.cloned.1.call-start
  6.5 0.7 all-gather.4.cloned.1.call-update
  7.3 0.0 all-gather.6.cloned.1.call-start
  7.3 0.7 all-gather.6.cloned.1.call-update
  8.0 1.0 reshape.9
  9.0 1.2 fusion.4
  10.2 1.1 convolution_divide_fusion
  11.3 1.1 fusion.2
  12.5 1.1 convolution_convert_fusion
  13.6 0.1 copy.22
  13.7 0.7 broadcast_add_fusion
  14.4 23.1 %all-gather = s32[1,2048]{1,0:T(1,128)S(1)} all-gather(s32[1,128]{1,0:T(1,128)S(1)} %broadcast_add_fusion), channel_id=2, replica_groups=mesh['dom'=2,'shard'=16] {'shard'}, dimensions={1}, use_global_device_ids=true | all-gather | bytes 8704 | tf_op jit(solution)/shard_map/all_gather | solution.py:52
  37.5 11.4 %all-gather.4.cloned.1.call-done = bf16[64,8192]{1,0:T(8,128)(2,1)} async-done(((bf16[64,512]{1,0:T(8,128)(2,1)}), bf16[64,8192]{1,0:T(8,128)(2,1)}) %all-gather.4.cloned.1.call-update) | async-done | bytes 1048592 | tf_op jit(solution)/shard_map/all_gather | solution.py:41
  48.9 0.0 copy-done
  48.9 2.1 %convolution_convert_fusion.2 = bf16[128,64]{0,1:T(8,128)(2,1)S(1)} fusion(bf16[128,8192]{1,0:T(8,128)(2,1)S(1)} %copy-done, bf16[64,8192]{1,0:T(8,128)(2,1)} %all-gather.4.cloned.1.call-done), kind=kOutput, calls=%fused_computation.5 | convolution fusion | flops 134225920 | bytes 3162112 | tf_op jit(solution)/shard_map/dot_general | solution.py:23
  51.0 21.0 %all_gather.17 = bf16[2048,64]{0,1:T(8,128)(2,1)S(1)} all-gather(bf16[128,64]{0,1:T(8,128)(2,1)S(1)} %convolution_convert_fusion.2), channel_id=1, replica_groups=mesh['dom'=2,'shard'=16] {'shard'}, dimensions={0}, use_global_device_ids=true | all-gather | bytes 278528 | tf_op jit(solution)/shard_map/all_gather | solution.py:50
  72.0 27.1 %all-gather.6.cloned.1.call-done = bf16[64,28672]{1,0:T(8,128)(2,1)} async-done(((bf16[64,1792]{1,0:T(8,128)(2,1)}), bf16[64,28672]{1,0:T(8,128)(2,1)}) %all-gather.6.cloned.1.call-update) | async-done | bytes 3670032 | tf_op jit(solution)/shard_map/all_gather | solution.py:44
  99.1 6.8 %convolution_convert_fusion.1 = bf16[128,64]{0,1:T(8,128)(2,1)S(1)} fusion(bf16[128,28672]{1,0:T(8,128)(2,1)} %param.10, bf16[64,28672]{1,0:T(8,128)(2,1)} %all-gather.6.cloned.1.call-done), kind=kOutput, calls=%fused_computation.4 | convolution fusion | flops 469770240 | bytes 11026432 | tf_op jit(solution)/shard_map/dot_general | solution.py:23
  105.9 19.5 %all_gather.19 = bf16[2048,64]{0,1:T(8,128)(2,1)S(1)} all-gather(bf16[128,64]{0,1:T(8,128)(2,1)S(1)} %convolution_convert_fusion.1), channel_id=1, replica_groups=mesh['dom'=2,'shard'=16] {'shard'}, dimensions={0}, use_global_device_ids=true | all-gather | bytes 278528 | tf_op jit(solution)/shard_map/all_gather | solution.py:51
  125.4 0.7 multiply_reduce_fusion
  126.1 0.3 copy.23
  126.4 14.1 %scatter_custom_fusion = f32[128,8]{1,0:T(8,128)S(1)} fusion(s32[2048]{0:T(1024)S(1)} %bitcast.27, f32[2048,8]{1,0:T(8,128)S(1)} %copy.23, f32[]{:T(128)} %constant.4.clone.1), kind=kCustom, calls=%fused_computation.12 | custom fusion | flops 16384 | bytes 4100 | tf_op jit(solution)/shard_map/scatter-add | solution.py:55
  140.6 0.6 broadcast_multiply_fusion
  (2 shorter events, 0.1 us)
Async XLA Ops:
  6.5 42.4 %copy-start = (bf16[128,8192]{1,0:T(8,128)(2,1)S(1)}, bf16[128,8192]{1,0:T(8,128)(2,1)}, u32[]{:S(2)}) copy-start(bf16[128,8192]{1,0:T(8,128)(2,1)} %param.9) | copy-start | bytes 6291460
  6.5 42.4 %all-gather.4.cloned.1.call-start = ((), (), s32[]{:S(2)}) async-start(), calls=%async_computation | async-start | bytes 1114112 | tf_op jit(solution)/shard_map/all_gather | solution.py:41
  7.3 91.9 %all-gather.6.cloned.1.call-start = ((), (), s32[]{:S(2)}) async-start(), calls=%async_computation.1 | async-start | bytes 3899392 | tf_op jit(solution)/shard_map/all_gather | solution.py:44
Sparse Core Ops, SparseCore 0:
  9.5 39.3 all-gather.3
  51.1 47.9 all-gather.5
where the time goes:
time: 149 us; the launch traced here: 148 us
  blocking collectives  63.6 us (43%)
  waiting for transfers between devices  39.9 us (27%)
  other arithmetic  15.4 us (10%)
  matrix products  14.1 us (9%)
  between operations  13.5 us (9%)
  local copies, waits for them, and re-layouts  1.52 us (1%)
    all_gather x1, waiting for transfers between devices, on_device(): lax.all_gather(out_factor, 'shard', axis=1, tiled=True)  27.1 us
    all_gather x1, blocking collectives, on_device(): owners = lax.all_gather(global_ids, 'shard', axis=0, tiled=True)  23.1 us
    all_gather x1, blocking collectives, on_device(): rows_in = lax.all_gather(proj_in, 'shard', axis=0, tiled=True)  21 us
    all_gather x1, blocking collectives, on_device(): rows_out = lax.all_gather(proj_out, 'shard', axis=0, tiled=True)  19.5 us
    scatter-add x1, other arithmetic, on_device(): scores = jax.ops.segment_sum(per_token, owners, num_segments=total_examples)  14.1 us
    all_gather x1, waiting for transfers between devices, on_device(): lax.all_gather(in_factor, 'shard', axis=1, tiled=True)  11.4 us
    dot_general x2, matrix products, fold_columns(): lax.dot_general(features, piece, (((1,), (1,)), ((), ())), preferred_elem...  8.84 us
  transfers between devices with their start and end apart: 2, of which 2 were waited for; matrix products, arithmetic and copies ran while one was open for 6% of the time, Pallas kernels for 0%

commit v1 on v0

v1 whole, which is shorter than its diff:
```python
import functools
import math

import jax
import jax.numpy as jnp
from jax import lax
from jax.experimental import pallas as pl
from jax.experimental.pallas import tpu as pltpu
from jax.sharding import PartitionSpec as P


EX_DEV = 8
SCALE = 0.00390625


def grid_of(n):
    chips = n // 2
    far = 1 << -(-int(math.log2(chips)) // 2)
    return far, chips // far, 2


def moved(value, n, offset):
    return lax.ppermute(value, "shard", [(i, i ^ offset) for i in range(n)])


NT = (((1,), (1,)), ((), ()))
VMEM = pl.BlockSpec(memory_space=pltpu.VMEM)
HBM = pl.BlockSpec(memory_space=pltpu.HBM)
MIB = 1 << 20


def columns(ref, first, width):
    return ref.at[:, pl.ds(pl.multiple_of(first * width, 128), width)]


def run_copies(pairs, sems):
    copies = [pltpu.make_async_copy(src, dst, sems.at[i]) for i, (src, dst) in enumerate(pairs)]
    for copy in copies:
        copy.start()
    for copy in copies:
        copy.wait()


def split_kernel(inner, outer, mine, sems):
    h_in, h_out = inner.shape[1] // 2, outer.shape[1] // 2
    dom = lax.axis_index("dom") % 2
    run_copies(
        [(columns(inner, dom, h_in), mine.at[:, :h_in]), (columns(outer, dom, h_out), mine.at[:, h_in:])], sems
    )


def split(in_factor, out_factor):
    rank = in_factor.shape[0]
    width = (in_factor.shape[1] + out_factor.shape[1]) // 2
    return pl.pallas_call(
        split_kernel,
        out_shape=jax.ShapeDtypeStruct((rank, width), in_factor.dtype),
        in_specs=[HBM, HBM],
        out_specs=VMEM,
        scratch_shapes=[pltpu.SemaphoreType.DMA((2,))],
        cost_estimate=pl.CostEstimate(flops=2 * 10**10, bytes_accessed=0, transcendentals=0),
        compiler_params=pltpu.CompilerParams(vmem_limit_bytes=2 * MIB),
        name="split",
    )(in_factor, out_factor)


INNER, OUTER, CARRIED, CROSSED = range(4)


def project_kernel(keys, h_in, has_part, final, act, grad, *refs):
    count = len(keys)
    pieces = refs[:count]
    out = refs[-1]
    rank = pieces[0].shape[0]
    me = lax.axis_index("shard")
    dom = lax.axis_index("dom") % 2
    part = refs[count][...] if has_part else None
    sums = [part[:, :rank], part[:, rank:]] if has_part else [0.0, 0.0]

    def add(j, piece, place, lo, size):
        rows = (act, grad)[j][:, pl.ds(pl.multiple_of(place * size, 128), size)]
        sums[j] = sums[j] + lax.dot_general(
            rows, piece[:, lo : lo + size], NT, preferred_element_type=jnp.float32
        )

    for piece, (offset, kind) in zip(pieces, keys):
        src = me ^ offset
        width = piece.shape[1]
        if kind in (INNER, OUTER):
            add(kind, piece, src, 0, width)
        else:
            place = 2 * src + (dom if kind == CARRIED else 1 - dom)
            add(INNER, piece, place, 0, h_in)
            add(OUTER, piece, place, h_in, width - h_in)
    total = jnp.concatenate(sums, axis=1)
    if final:
        ids = refs[count + 1]
        out[: 2 * rank] = total.T.astype(jnp.bfloat16)
        out[2 * rank :] = jnp.broadcast_to(ids[...].astype(jnp.float32), (16, ids.shape[1])).astype(jnp.bfloat16)
    else:
        out[...] = total


def project(act, grad, pieces, keys, h_in, part, ids):
    tokens = act.shape[0]
    rank = pieces[0].shape[0]
    extra = (() if part is None else (part,)) + (() if ids is None else (ids,))
    if ids is None:
        shape = jax.ShapeDtypeStruct((tokens, 2 * rank), jnp.float32)
    else:
        shape = jax.ShapeDtypeStruct((2 * rank + 16, tokens), jnp.bfloat16)
    size = sum(piece.size for piece in pieces)
    return pl.pallas_call(
        functools.partial(project_kernel, tuple(keys), h_in, part is not None, ids is not None),
        out_shape=shape,
        in_specs=[VMEM] * (2 + len(pieces) + len(extra)),
        out_specs=VMEM,
        cost_estimate=pl.CostEstimate(
            flops=2 * tokens * size, bytes_accessed=2 * tokens * size // rank, transcendentals=0
        ),
        compiler_params=pltpu.CompilerParams(vmem_limit_bytes=3 * MIB),
    )(act, grad, *pieces, *extra)


def project_halves(n, act, grad, ids, in_factor, out_factor):
    far, near, cores = grid_of(n)
    fars = [k * near * cores for k in range(1, far)]
    nears = [k * cores for k in range(1, near)]
    h_in = in_factor.shape[1] // 2

    def crossed(value):
        return lax.ppermute(value, "dom", [(0, 1), (1, 0)])

    mine = split(in_factor, out_factor)
    held = {(0, INNER): in_factor, (0, OUTER): out_factor}

    def bring(key, source, offset):
        held[key] = moved(held[source] if source in held else mine, n, offset)

    near_keys = []
    for m in nears:
        bring((m, CARRIED), (0, CARRIED), m)
        held[m, CROSSED] = crossed(held[m, CARRIED])
        near_keys += [(m, CARRIED), (m, CROSSED)]
    waves = []
    for i, f in enumerate(fars):
        wave = []
        for kind in (INNER, OUTER) if i == 0 else (CARRIED,):
            bring((f, kind), (0, kind), f)
            wave.append((f, kind))
            for m in nears:
                bring((f ^ m, kind), (f, kind), m)
                wave.append((f ^ m, kind))
        if i:
            for o, _ in list(wave):
                held[o, CROSSED] = crossed(held[o, CARRIED])
            wave += [(o, CROSSED) for o, _ in wave]
        waves.append(wave)
    for o, kind in list(held):
        held[o ^ 1, kind] = moved(held[o, kind], n, 1)
    rest = [key for wave in waves[1:] for key in wave]
    late = [key for key in rest[len(rest) // 2 - len(nears) :] if key != waves[-1][0]]
    groups = [[(0, INNER), (0, OUTER)], near_keys + waves[0], [key for key in rest if key not in late]]
    groups += [late[:-1], late[-1:]]
    part = None
    for i, keys in enumerate(groups):
        keys = [(o ^ c, kind) for o, kind in keys for c in (0, 1)]
        last = ids if i == len(groups) - 1 else None
        part = project(act, grad, [held[key] for key in keys], keys, h_in, part, last)
    return part


def project_plain(n, act, grad, ids, in_factor, out_factor):
    w_in, w_out = in_factor.shape[1], out_factor.shape[1]
    pieces = [jnp.concatenate([in_factor, out_factor], axis=1)]
    offsets = [0]
    step = n // 2
    while step:
        pieces += [moved(piece, n, step) for piece in pieces]
        offsets += [offset ^ step for offset in offsets]
        step //= 2
    me = lax.axis_index("shard")
    sums = [0.0, 0.0]
    for piece, offset in zip(pieces, offsets):
        src = me ^ offset
        for i, (rows, part, width) in enumerate(((act, piece[:, :w_in], w_in), (grad, piece[:, w_in:], w_out))):
            cols = lax.dynamic_slice_in_dim(rows, src * width, width, axis=1)
            sums[i] = sums[i] + lax.dot_general(part, cols, NT, preferred_element_type=jnp.float32)
    numbers = jnp.broadcast_to(ids, (16, ids.shape[1]))
    return jnp.concatenate([s.astype(jnp.bfloat16) for s in (*sums, numbers)], axis=0)


def halves_of(value):
    high = value.astype(jnp.bfloat16)
    return high, (value - high.astype(jnp.float32)).astype(jnp.bfloat16)


def fine_dot(left, right, dims):
    dot = functools.partial(lax.dot_general, dimension_numbers=dims, preferred_element_type=jnp.float32)
    (a, a_rest), (b, b_rest) = halves_of(left), halves_of(right)
    return dot(a, b) + (dot(a, b_rest) + dot(a_rest, b))


def precondition_kernel(grads, basis_in, basis_out, eigen, out, stacked, turned):
    rank = basis_in.shape[0]
    queries = grads.shape[0]
    nn = (((1,), (0,)), ((), ()))
    for a in range(rank):
        stacked[pl.ds(a, queries, stride=rank)] = grads[:, a * rank : (a + 1) * rank]
    inner, outer, weights = basis_in[...], basis_out[...], eigen[...]
    inner_t = inner.T
    right = fine_dot(stacked[...], outer, nn)
    parts = [right[q * rank : (q + 1) * rank] for q in range(queries)]
    scaled = [fine_dot(inner_t, part, nn) / weights for part in parts]
    back = fine_dot(jnp.concatenate(scaled, axis=0), outer, NT)
    for q in range(queries):
        turned[pl.ds(q, rank, stride=queries)] = fine_dot(inner, back[q * rank : (q + 1) * rank], nn)
    out[...] = turned[...].astype(jnp.bfloat16)


def precondition(query_grads, basis_in, basis_out, eigen):
    rank = basis_in.shape[0]
    rows = query_grads.shape[0] * rank
    return pl.pallas_call(
        precondition_kernel,
        out_shape=jax.ShapeDtypeStruct((rows, rank), jnp.bfloat16),
        in_specs=[VMEM] * 4,
        out_specs=VMEM,
        scratch_shapes=[pltpu.VMEM((rows, rank), jnp.float32)] * 2,
        cost_estimate=pl.CostEstimate(
            flops=10**10, bytes_accessed=4 * rows * rank, transcendentals=0
        ),
        compiler_params=pltpu.CompilerParams(vmem_limit_bytes=8 * MIB),
        name="precondition",
    )(query_grads, basis_in, basis_out, eigen)


def score_kernel(offsets, final, has_part, query, *refs):
    count = len(offsets)
    blocks = refs[:count]
    out, stacked, member = refs[-3:]
    rank = query.shape[1]
    queries = query.shape[0] // rank
    tokens = blocks[0].shape[1]
    me = lax.axis_index("shard")
    examples = out.shape[1]
    group = stacked.shape[1] // tokens
    lane = lax.broadcasted_iota(jnp.int32, (examples, tokens), 0)
    total = refs[count][...] if has_part else 0.0
    for first in range(0, count, group):
        for k in range(group):
            block = blocks[first + k]
            turned = jnp.dot(query[...], block[rank : 2 * rank], preferred_element_type=jnp.float32)
            inputs = block[:rank].astype(jnp.float32)
            each = jnp.sum(turned.reshape(rank, queries, tokens) * inputs[:, None, :], axis=0)
            ids = block[2 * rank :].astype(jnp.float32)[:1].astype(jnp.int32)
            owner = ids + (me ^ offsets[first + k]) * EX_DEV
            cols = pl.ds(k * tokens, tokens)
            member[:, cols] = jnp.where(lane == owner, 1.0, 0.0).astype(jnp.bfloat16)
            high = each.astype(jnp.bfloat16).astype(jnp.float32)
            mid = (each - high).astype(jnp.bfloat16).astype(jnp.float32)
            stacked[0:queries, cols] = high
            stacked[queries : 2 * queries, cols] = mid
            stacked[2 * queries :, cols] = each - high - mid
        sums = lax.dot_general(
            stacked[...].astype(jnp.bfloat16), member[...], NT, preferred_element_type=jnp.float32
        )
        total = total + (sums[:queries] + (sums[queries : 2 * queries] + sums[2 * queries :]))
    out[...] = total * SCALE if final else total


def score(query, blocks, offsets, examples, part, final):
    rank2, tokens = blocks[0].shape
    queries = query.shape[0] // query.shape[1]
    group = math.gcd(4, len(offsets))
    parts = () if part is None else (part,)
    return pl.pallas_call(
        functools.partial(score_kernel, tuple(offsets), final, bool(parts)),
        out_shape=jax.ShapeDtypeStruct((queries, examples), jnp.float32),
        in_specs=[VMEM] * (1 + len(blocks) + len(parts)),
        out_specs=VMEM,
        scratch_shapes=[
            pltpu.VMEM((3 * queries, group * tokens), jnp.float32),
            pltpu.VMEM((examples, group * tokens), jnp.bfloat16),
        ],
        cost_estimate=pl.CostEstimate(
            flops=2 * query.size * tokens * len(blocks),
            bytes_accessed=2 * rank2 * tokens * len(blocks),
            transcendentals=0,
        ),
        compiler_params=pltpu.CompilerParams(vmem_limit_bytes=4 * MIB),
    )(query, *blocks, *parts)


def on_device(
    n,
    doms,
    activations,
    out_grads,
    example_ids,
    in_factor,
    out_factor,
    query_grads,
    basis_in,
    basis_out,
    eigen,
):
    far, near, cores = grid_of(n)
    fars = [k * near * cores for k in range(1, far)]
    nears = [k * cores for k in range(1, near)]
    aligned = doms == 2 and in_factor.shape[1] % 256 == 0 and out_factor.shape[1] % 256 == 0
    project_all = project_halves if aligned else project_plain
    mine = project_all(n, activations, out_grads, example_ids, in_factor, out_factor)
    query = precondition(query_grads, basis_in, basis_out, eigen)
    row = {0: mine}
    for i, f in reversed(list(enumerate(fars))):
        row[f] = moved(mine, n, f)
    rest = {o ^ m: moved(block, n, m) for m in nears for o, block in row.items()}
    steps = [row, {o ^ 1: moved(block, n, 1) for o, block in row.items()}]
    cores = {}
    for o, block in rest.items():
        cores[o ^ 1] = moved(block, n, 1)
    steps += [rest, cores]
    total = None
    for i, step in enumerate(steps):
        total = score(query, list(step.values()), list(step), EX_DEV * n, total, i == len(steps) - 1)
    return total.T


def solution(mesh):
    placed = (
        P(("dom", "shard"), None),
        P(("dom", "shard"), None),
        P(("dom", "shard"), None),
        P(None, "shard"),
        P(None, "shard"),
        P("shard", None),
        P(),
        P(),
        P(),
    )
    return jax.shard_map(
        functools.partial(on_device, mesh.shape["shard"], mesh.shape["dom"]),
        mesh=mesh,
        in_specs=placed,
        out_specs=P("dom", "shard"),
        check_vma=False,
    )
```

time: 149 us -> 74 us (0.50)
  blocking collectives: 63.6 us -> 0 us
  starting transfers between devices: 0.04 us -> 33.5 us
  other arithmetic: 15.4 us -> 0 us
  matrix products: 14.1 us -> 0 us
  between operations: 13.5 us -> 0.25 us
  waiting for transfers between devices: 39.9 us -> 30.9 us
  Pallas kernels: 0 us -> 7.33 us
    all_gather x3 -> x0, blocking collectives: 63.6 us -> none  [the longest x1 23.1 us: on_device(): owners = lax.all_gather(global_ids, 'shard', axis=0, tiled=True)]
    all_gather x2 -> x0, waiting for transfers between devices: 38.5 us -> none  [the longest x1 27.1 us: on_device(): lax.all_gather(out_factor, 'shard', axis=1, tiled=True)]
    ppermute x0 -> x45, starting transfers between devices: none -> 33.5 us  [the longest x40 26.9 us: moved(): return lax.ppermute(value, 'shard', [(i, i ^ offset) for i in range(n)])]
    ppermute x0 -> x45, waiting for transfers between devices: none -> 30.9 us  [the longest x40 23.5 us: moved(): return lax.ppermute(value, 'shard', [(i, i ^ offset) for i in range(n)])]
    scatter-add x1 -> x0, other arithmetic: 14.1 us -> none  [on_device(): scores = jax.ops.segment_sum(per_token, owners, num_segments=total_examples)]
    dot_general x6 -> x0, matrix products: 13.4 us -> none  [the longest x2 8.84 us: fold_columns(): lax.dot_general(features, piece, (((1,), (1,)), ((), ())), preferred_elem...]
    pallas_call x0 -> x11, Pallas kernels: none -> 7.33 us  [the longest x5 3.68 us: project(): pl.pallas_call(functools.partial(project_kernel, tuple(keys), h_in, part...]
    unnamed x2 -> x22, local copies, waits for them, and re-layouts: 0.01 us -> 1.82 us
  transfers between devices with their start and end apart: 2 -> 45, of which waited for: 2 -> 13; matrix products, arithmetic and copies ran while one was open for 6% -> 0% of each run, Pallas kernels for 0% -> 8%
where the time goes in v1:
time: 74 us; the launch traced here: 73.8 us
  starting transfers between devices  33.5 us (45%)
  waiting for transfers between devices  30.9 us (42%)
  Pallas kernels  7.33 us (10%)
  local copies, waits for them, and re-layouts  1.82 us (2%)
    ppermute x40, starting transfers between devices, moved(): return lax.ppermute(value, 'shard', [(i, i ^ offset) for i in range(n)])  26.9 us
    ppermute x40, waiting for transfers between devices, moved(): return lax.ppermute(value, 'shard', [(i, i ^ offset) for i in range(n)])  23.5 us
    ppermute x5, waiting for transfers between devices, crossed(): return lax.ppermute(value, 'dom', [(0, 1), (1, 0)])  7.39 us
    ppermute x5, starting transfers between devices, crossed(): return lax.ppermute(value, 'dom', [(0, 1), (1, 0)])  6.64 us
    pallas_call x5, Pallas kernels, project(): pl.pallas_call(functools.partial(project_kernel, tuple(keys), h_in, part...  3.68 us
    pallas_call x4, Pallas kernels, score(): pl.pallas_call(functools.partial(score_kernel, tuple(offsets), final, boo...  2.33 us
    unnamed x22, local copies, waits for them, and re-layouts  1.82 us
  transfers between devices with their start and end apart: 45, of which 13 were waited for; matrix products, arithmetic and copies ran while one was open for 0% of the time, Pallas kernels for 8%

profile of v1, /device:TPU:0, one launch (start us, length us, event | category | flops | bytes accessed | tf_op | source)
XLA Modules:
  0.0 73.8 jit_solution(16623573469287518332)
XLA Ops:
  0.0 3.1 %collective-permute-start.20 = (bf16[64,512]{1,0:T(8,128)(2,1)}, bf16[64,512]{1,0:T(8,128)(2,1)S(1)}, u32[]{:S(2)}, u32[]{:S(2)}) collective-permute-start(bf16[64,512]{1,0:T(8,128)(2,1)} %refs_0_.1), channel_id=1, source_target_pairs={{0,4},{1,5},{2,6},{3,7},{4,0},{5,1},{6,2},{7,3},{8,12},{9,13},{10,... | collective-permute-start | bytes 196616 | tf_op jit(solution)/shard_map/ppermute | solution.py:23
  3.1 0.9 %copy-done.2 = bf16[64,1792]{1,0:T(8,128)(2,1)S(1)} copy-done((bf16[64,1792]{1,0:T(8,128)(2,1)S(1)}, bf16[64,1792]{1,0:T(8,128)(2,1)}, u32[]{:S(2)}) %copy-start.2) | copy-done | bytes 229400
  4.0 0.8 %copy-done.4 = bf16[64,512]{1,0:T(8,128)(2,1)S(1)} copy-done((bf16[64,512]{1,0:T(8,128)(2,1)S(1)}, bf16[64,512]{1,0:T(8,128)(2,1)}, u32[]{:S(2)}) %copy-start.4) | copy-done | bytes 65560
  4.9 2.2 %collective-permute-start.16 = (bf16[64,1152]{1,0:T(8,128)(2,1)S(1)}, bf16[64,1152]{1,0:T(8,128)(2,1)S(1)}, u32[]{:S(2)}, u32[]{:S(2)}) collective-permute-start(bf16[64,1152]{1,0:T(8,128)(2,1)S(1)} %split.1), channel_id=1, source_target_pairs={{0,2},{1,3},{2,0},{3,1},{4,6},{5,7},{6,4},{7,5},{8,10},{9,11},{10,... | collective-permute-start | bytes 442376 | tf_op jit(solution)/shard_map/ppermute | solution.py:23
  7.5 1.6 %collective-permute-start.24 = (bf16[64,1792]{1,0:T(8,128)(2,1)S(1)}, bf16[64,1792]{1,0:T(8,128)(2,1)S(1)}, u32[]{:S(2)}, u32[]{:S(2)}) collective-permute-start(bf16[64,1792]{1,0:T(8,128)(2,1)S(1)} %copy-done.2), channel_id=1, source_target_pairs={{0,4},{1,5},{2,6},{3,7},{4,0},{5,1},{6,2},{7,3},{8,12},{9,13},{10,... | collective-permute-start | bytes 688136 | tf_op jit(solution)/shard_map/ppermute | solution.py:23
  9.3 3.5 %collective-permute-done.22.refs_6_ = bf16[64,512]{1,0:T(8,128)(2,1)S(1)} collective-permute-done((bf16[64,512]{1,0:T(8,128)(2,1)S(1)}, bf16[64,512]{1,0:T(8,128)(2,1)S(1)}, u32[]{:S(2)}, u32[]{:S(2)}) %collective-permute-start.22) | collective-permute-done | bytes 65568 | tf_op jit(solution)/shard_map/ppermute | solution.py:23
  12.8 2.8 %collective-permute-start.4 = (bf16[64,1152]{1,0:T(8,128)(2,1)S(1)}, bf16[64,1152]{1,0:T(8,128)(2,1)S(1)}, u32[]{:S(2)}, u32[]{:S(2)}) collective-permute-start(bf16[64,1152]{1,0:T(8,128)(2,1)S(1)} %split.1), channel_id=1, source_target_pairs={{0,8},{1,9},{2,10},{3,11},{4,12},{5,13},{6,14},{7,15},{8,0},{9,1},... | collective-permute-start | bytes 442376 | tf_op jit(solution)/shard_map/ppermute | solution.py:23
  15.6 0.5 collective-permute-start
  16.1 1.5 %collective-permute-start.18 = (bf16[64,1152]{1,0:T(8,128)(2,1)S(1)}, bf16[64,1152]{1,0:T(8,128)(2,1)S(1)}, u32[]{:S(2)}, u32[]{:S(2)}) collective-permute-start(bf16[64,1152]{1,0:T(8,128)(2,1)S(1)} %collective-permute-done.16.refs_0_), channel_id=1, source_target_pairs={{0,16},{16,0},{1,17},{17,1},{2,18},{18,2},{3,19},{19,3},{4,20},{20... | collective-permute-start | bytes 442376 | tf_op jit(solution)/shard_map/ppermute | solution.py:132
  17.7 9.1 %collective-permute-done.4.refs_0_ = bf16[64,1152]{1,0:T(8,128)(2,1)S(1)} collective-permute-done((bf16[64,1152]{1,0:T(8,128)(2,1)S(1)}, bf16[64,1152]{1,0:T(8,128)(2,1)S(1)}, u32[]{:S(2)}, u32[]{:S(2)}) %collective-permute-start.4) | collective-permute-done | bytes 147488 | tf_op jit(solution)/shard_map/ppermute | solution.py:23
  26.7 0.5 collective-permute-start.23
  27.2 1.0 %collective-permute-done.23.refs_7_ = bf16[64,512]{1,0:T(8,128)(2,1)S(1)} collective-permute-done((bf16[64,512]{1,0:T(8,128)(2,1)S(1)}, bf16[64,512]{1,0:T(8,128)(2,1)S(1)}, u32[]{:S(2)}, u32[]{:S(2)}) %collective-permute-start.23) | collective-permute-done | bytes 65568 | tf_op jit(solution)/shard_map/ppermute | solution.py:23
  28.2 1.6 %collective-permute-start.5 = (bf16[64,1152]{1,0:T(8,128)(2,1)S(1)}, bf16[64,1152]{1,0:T(8,128)(2,1)S(1)}, u32[]{:S(2)}, u32[]{:S(2)}) collective-permute-start(bf16[64,1152]{1,0:T(8,128)(2,1)S(1)} %collective-permute-done.4.refs_0_), channel_id=1, source_target_pairs={{0,2},{1,3},{2,0},{3,1},{4,6},{5,7},{6,4},{7,5},{8,10},{9,11},{10,... | collective-permute-start | bytes 442376 | tf_op jit(solution)/shard_map/ppermute | solution.py:23
  30.2 1.6 %collective-permute-start.13 = (bf16[64,1152]{1,0:T(8,128)(2,1)S(1)}, bf16[64,1152]{1,0:T(8,128)(2,1)S(1)}, u32[]{:S(2)}, u32[]{:S(2)}) collective-permute-start(bf16[64,1152]{1,0:T(8,128)(2,1)S(1)} %collective-permute-done.4.refs_0_), channel_id=1, source_target_pairs={{0,16},{16,0},{1,17},{17,1},{2,18},{18,2},{3,19},{19,3},{4,20},{20... | collective-permute-start | bytes 442376 | tf_op jit(solution)/shard_map/ppermute | solution.py:132
  31.8 0.5 collective-permute-start.15
  32.3 2.6 %collective-permute-done.5.refs_2_ = bf16[64,1152]{1,0:T(8,128)(2,1)S(1)} collective-permute-done((bf16[64,1152]{1,0:T(8,128)(2,1)S(1)}, bf16[64,1152]{1,0:T(8,128)(2,1)S(1)}, u32[]{:S(2)}, u32[]{:S(2)}) %collective-permute-start.5) | collective-permute-done | bytes 147488 | tf_op jit(solution)/shard_map/ppermute | solution.py:23
  34.9 1.6 %collective-permute-start.1 = (bf16[64,1152]{1,0:T(8,128)(2,1)S(1)}, bf16[64,1152]{1,0:T(8,128)(2,1)S(1)}, u32[]{:S(2)}, u32[]{:S(2)}) collective-permute-start(bf16[64,1152]{1,0:T(8,128)(2,1)S(1)} %collective-permute-done.refs_6_), channel_id=1, source_target_pairs={{0,2},{1,3},{2,0},{3,1},{4,6},{5,7},{6,4},{7,5},{8,10},{9,11},{10,... | collective-permute-start | bytes 442376 | tf_op jit(solution)/shard_map/ppermute | solution.py:23
  36.5 1.5 %collective-permute-start.9 = (bf16[64,1152]{1,0:T(8,128)(2,1)S(1)}, bf16[64,1152]{1,0:T(8,128)(2,1)S(1)}, u32[]{:S(2)}, u32[]{:S(2)}) collective-permute-start(bf16[64,1152]{1,0:T(8,128)(2,1)S(1)} %collective-permute-done.refs_6_), channel_id=1, source_target_pairs={{0,16},{16,0},{1,17},{17,1},{2,18},{18,2},{3,19},{19,3},{4,20},{20... | collective-permute-start | bytes 442376 | tf_op jit(solution)/shard_map/ppermute | solution.py:132
  38.1 0.5 collective-permute-start.25
  38.6 1.3 %collective-permute-done.26.refs_10_ = bf16[64,1792]{1,0:T(8,128)(2,1)S(1)} collective-permute-done((bf16[64,1792]{1,0:T(8,128)(2,1)S(1)}, bf16[64,1792]{1,0:T(8,128)(2,1)S(1)}, u32[]{:S(2)}, u32[]{:S(2)}) %collective-permute-start.26) | collective-permute-done | bytes 229408 | tf_op jit(solution)/shard_map/ppermute | solution.py:23
  39.8 2.5 %collective-permute-done.1.refs_2_ = bf16[64,1152]{1,0:T(8,128)(2,1)S(1)} collective-permute-done((bf16[64,1152]{1,0:T(8,128)(2,1)S(1)}, bf16[64,1152]{1,0:T(8,128)(2,1)S(1)}, u32[]{:S(2)}, u32[]{:S(2)}) %collective-permute-start.1) | collective-permute-done | bytes 147488 | tf_op jit(solution)/shard_map/ppermute | solution.py:23
  42.3 1.6 %collective-permute-start.6 = (bf16[64,1152]{1,0:T(8,128)(2,1)S(1)}, bf16[64,1152]{1,0:T(8,128)(2,1)S(1)}, u32[]{:S(2)}, u32[]{:S(2)}) collective-permute-start(bf16[64,1152]{1,0:T(8,128)(2,1)S(1)} %collective-permute-done.5.refs_2_), channel_id=1, source_target_pairs={{0,16},{16,0},{1,17},{17,1},{2,18},{18,2},{3,19},{19,3},{4,20},{20... | collective-permute-start | bytes 442376 | tf_op jit(solution)/shard_map/ppermute | solution.py:132
  43.9 0.4 collective-permute-start.2
  44.4 4.7 %collective-permute-done.6.refs_0_ = bf16[64,1152]{1,0:T(8,128)(2,1)S(1)} collective-permute-done((bf16[64,1152]{1,0:T(8,128)(2,1)S(1)}, bf16[64,1152]{1,0:T(8,128)(2,1)S(1)}, u32[]{:S(2)}, u32[]{:S(2)}) %collective-permute-start.6) | collective-permute-done | bytes 147488 | tf_op jit(solution)/shard_map/ppermute | solution.py:132
  49.1 2.7 %collective-permute-done.2.refs_0_ = bf16[64,1152]{1,0:T(8,128)(2,1)S(1)} collective-permute-done((bf16[64,1152]{1,0:T(8,128)(2,1)S(1)}, bf16[64,1152]{1,0:T(8,128)(2,1)S(1)}, u32[]{:S(2)}, u32[]{:S(2)}) %collective-permute-start.2) | collective-permute-done | bytes 147488 | tf_op jit(solution)/shard_map/ppermute | solution.py:132
  51.8 0.5 collective-permute-start.7
  52.4 0.5 shard_map.91.refs_12_
  52.9 1.2 %shard_map.92.refs_8_ = f32[128,128]{1,0:T(8,128)S(1)} custom-call(bf16[128,8192]{1,0:T(8,128)(2,1)S(1)} %copy-done.1, bf16[128,28672]{1,0:T(8,128)(2,1)S(1)} %copy-done, bf16[64,1152]{1,0:T(8,128)(2,1)S(1)} %collective-permute-done.16.refs_0_, bf16[64,1152]{1,0:T(8,128)(2,1)S(1)} %collective-permute-done.17.refs_1_, ...), custom_call_target="tpu_custom_call" | custom-call | flops 226492416 | bytes 3538944 | tf_op jit(solution)/shard_map/pallas_call | solution.py:113
  54.1 0.8 %shard_map.93.refs_6_ = f32[128,128]{1,0:T(8,128)S(1)} custom-call(bf16[128,8192]{1,0:T(8,128)(2,1)S(1)} %copy-done.1, bf16[128,28672]{1,0:T(8,128)(2,1)S(1)} %copy-done, bf16[64,1152]{1,0:T(8,128)(2,1)S(1)} %collective-permute-done.4.refs_0_, bf16[64,1152]{1,0:T(8,128)(2,1)S(1)} %collective-permute-done.11.refs_1_, ...), custom_call_target="tpu_custom_call" | custom-call | flops 150994944 | bytes 2359296 | tf_op jit(solution)/shard_map/pallas_call | solution.py:113
  55.0 0.7 shard_map.94.refs_2_
  55.7 0.5 shard_map.95.refs_0_
  56.2 2.4 %collective-permute-start.32 = (bf16[144,128]{1,0:T(8,128)(2,1)S(1)}, bf16[144,128]{1,0:T(8,128)(2,1)S(1)}, u32[]{:S(2)}, u32[]{:S(2)}) collective-permute-start(bf16[144,128]{1,0:T(8,128)(2,1)S(1)} %shard_map.95.refs_0_), channel_id=1, source_target_pairs={{0,12},{1,13},{2,14},{3,15},{4,8},{5,9},{6,10},{7,11},{8,4},{9,5},... | collective-permute-start | bytes 110600 | tf_op jit(solution)/shard_map/ppermute | solution.py:23
  58.6 1.3 %collective-permute-start.35 = (bf16[144,128]{1,0:T(8,128)(2,1)S(1)}, bf16[144,128]{1,0:T(8,128)(2,1)S(1)}, u32[]{:S(2)}, u32[]{:S(2)}) collective-permute-start(bf16[144,128]{1,0:T(8,128)(2,1)S(1)} %shard_map.95.refs_0_), channel_id=1, source_target_pairs={{0,8},{1,9},{2,10},{3,11},{4,12},{5,13},{6,14},{7,15},{8,0},{9,1},... | collective-permute-start | bytes 110600 | tf_op jit(solution)/shard_map/ppermute | solution.py:23
  59.9 0.8 %collective-permute-start.38 = (bf16[144,128]{1,0:T(8,128)(2,1)S(1)}, bf16[144,128]{1,0:T(8,128)(2,1)S(1)}, u32[]{:S(2)}, u32[]{:S(2)}) collective-permute-start(bf16[144,128]{1,0:T(8,128)(2,1)S(1)} %shard_map.95.refs_0_), channel_id=1, source_target_pairs={{0,4},{1,5},{2,6},{3,7},{4,0},{5,1},{6,2},{7,3},{8,12},{9,13},{10,... | collective-permute-start | bytes 110600 | tf_op jit(solution)/shard_map/ppermute | solution.py:23
  60.7 1.7 %collective-permute-start.30 = (bf16[144,128]{1,0:T(8,128)(2,1)S(1)}, bf16[144,128]{1,0:T(8,128)(2,1)S(1)}, u32[]{:S(2)}, u32[]{:S(2)}) collective-permute-start(bf16[144,128]{1,0:T(8,128)(2,1)S(1)} %shard_map.95.refs_0_), channel_id=1, source_target_pairs={{0,2},{1,3},{2,0},{3,1},{4,6},{5,7},{6,4},{7,5},{8,10},{9,11},{10,... | collective-permute-start | bytes 110600 | tf_op jit(solution)/shard_map/ppermute | solution.py:23
  62.5 1.0 %collective-permute-done.35.refs_2_ = bf16[144,128]{1,0:T(8,128)(2,1)S(1)} collective-permute-done((bf16[144,128]{1,0:T(8,128)(2,1)S(1)}, bf16[144,128]{1,0:T(8,128)(2,1)S(1)}, u32[]{:S(2)}, u32[]{:S(2)}) %collective-permute-start.35) | collective-permute-done | bytes 36896 | tf_op jit(solution)/shard_map/ppermute | solution.py:23
  63.5 0.6 collective-permute-done.38.refs_3_
  64.1 1.5 %collective-permute-start.33 = (bf16[144,128]{1,0:T(8,128)(2,1)S(1)}, bf16[144,128]{1,0:T(8,128)(2,1)S(1)}, u32[]{:S(2)}, u32[]{:S(2)}) collective-permute-start(bf16[144,128]{1,0:T(8,128)(2,1)S(1)} %collective-permute-done.32.refs_1_), channel_id=1, source_target_pairs={{0,2},{1,3},{2,0},{3,1},{4,6},{5,7},{6,4},{7,5},{8,10},{9,11},{10,... | collective-permute-start | bytes 110600 | tf_op jit(solution)/shard_map/ppermute | solution.py:23
  65.6 0.5 collective-permute-start.36
  66.1 1.5 %collective-permute-start.39 = (bf16[144,128]{1,0:T(8,128)(2,1)S(1)}, bf16[144,128]{1,0:T(8,128)(2,1)S(1)}, u32[]{:S(2)}, u32[]{:S(2)}) collective-permute-start(bf16[144,128]{1,0:T(8,128)(2,1)S(1)} %collective-permute-done.38.refs_3_), channel_id=1, source_target_pairs={{0,2},{1,3},{2,0},{3,1},{4,6},{5,7},{6,4},{7,5},{8,10},{9,11},{10,... | collective-permute-start | bytes 110600 | tf_op jit(solution)/shard_map/ppermute | solution.py:23
  67.6 0.5 collective-permute-start.31
  68.2 1.3 %collective-permute-done.36.refs_2_ = bf16[144,128]{1,0:T(8,128)(2,1)S(1)} collective-permute-done((bf16[144,128]{1,0:T(8,128)(2,1)S(1)}, bf16[144,128]{1,0:T(8,128)(2,1)S(1)}, u32[]{:S(2)}, u32[]{:S(2)}) %collective-permute-start.36) | collective-permute-done | bytes 36896 | tf_op jit(solution)/shard_map/ppermute | solution.py:23
  69.5 0.5 collective-permute-done.39.refs_3_
  70.1 1.3 %precondition.1.query = bf16[512,64]{1,0:T(8,128)(2,1)S(1)} custom-call(f32[8,4096]{1,0:T(8,128)S(1)} %copy-done.7, f32[64,64]{1,0:T(8,128)S(1)} %copy-done.8, f32[64,64]{1,0:T(8,128)S(1)} %copy-done.9, f32[64,64]{1,0:T(8,128)S(1)} %copy-done.10), custom_call_target="tpu_custom_call" | custom-call | flops 10000000000 | bytes 131072 | tf_op jit(solution)/shard_map/precondition/pallas_call | solution.py:224
  71.4 0.4 shard_map.96.refs_4_
  71.8 0.4 shard_map.97.refs_4_
  72.3 0.4 shard_map.98.refs_4_
  72.8 1.0 %shard_map.99 = f32[8,128]{1,0:T(8,128)} custom-call(bf16[512,64]{1,0:T(8,128)(2,1)S(1)} %precondition.1.query, bf16[144,128]{1,0:T(8,128)(2,1)S(1)} %collective-permute-done.31.refs_0_, bf16[144,128]{1,0:T(8,128)(2,1)S(1)} %collective-permute-done.34.refs_1_, bf16[144,128]{1,0:T(8,128)(2,1)S(1)} %collective-permute-done.37.refs_2_, ...), custom_call_target="tpu_custom_call" | custom-call | flops 33554432 | bytes 147456 | tf_op jit(solution)/shard_map/pallas_call | solution.py:277
  (75 shorter events, 1.6 us)
Async XLA Ops:
  0.0 52.3 %copy-start = (bf16[128,28672]{1,0:T(8,128)(2,1)S(1)}, bf16[128,28672]{1,0:T(8,128)(2,1)}, u32[]{:S(2)}) copy-start(bf16[128,28672]{1,0:T(8,128)(2,1)} %grad.9) | copy-start | bytes 22020100
  0.0 52.3 %copy-start.1 = (bf16[128,8192]{1,0:T(8,128)(2,1)S(1)}, bf16[128,8192]{1,0:T(8,128)(2,1)}, u32[]{:S(2)}) copy-start(bf16[128,8192]{1,0:T(8,128)(2,1)} %act.9) | copy-start | bytes 6291460
  0.0 7.1 %collective-permute-start.20 = (bf16[64,512]{1,0:T(8,128)(2,1)}, bf16[64,512]{1,0:T(8,128)(2,1)S(1)}, u32[]{:S(2)}, u32[]{:S(2)}) collective-permute-start(bf16[64,512]{1,0:T(8,128)(2,1)} %refs_0_.1), channel_id=1, source_target_pairs={{0,4},{1,5},{2,6},{3,7},{4,0},{5,1},{6,2},{7,3},{8,12},{9,13},{10,... | collective-permute-start | bytes 196616 | tf_op jit(solution)/shard_map/ppermute | solution.py:23
  3.1 6.0 %collective-permute-start.28 = (bf16[64,512]{1,0:T(8,128)(2,1)}, bf16[64,512]{1,0:T(8,128)(2,1)S(1)}, u32[]{:S(2)}, u32[]{:S(2)}) collective-permute-start(bf16[64,512]{1,0:T(8,128)(2,1)} %refs_0_.1), channel_id=1, source_target_pairs={{0,1},{1,0},{2,3},{3,2},{4,5},{5,4},{6,7},{7,6},{8,9},{9,8},{10,11... | collective-permute-start | bytes 196616 | tf_op jit(solution)/shard_map/ppermute | solution.py:23
  4.8 47.5 %copy-start.5 = (bf16[64,512]{1,0:T(8,128)(2,1)S(1)}, bf16[64,512]{1,0:T(8,128)(2,1)}, u32[]{:S(2)}) copy-start(bf16[64,512]{1,0:T(8,128)(2,1)} %refs_0_.1) | copy-start | bytes 196612
  4.9 11.2 %collective-permute-start.16 = (bf16[64,1152]{1,0:T(8,128)(2,1)S(1)}, bf16[64,1152]{1,0:T(8,128)(2,1)S(1)}, u32[]{:S(2)}, u32[]{:S(2)}) collective-permute-start(bf16[64,1152]{1,0:T(8,128)(2,1)S(1)} %split.1), channel_id=1, source_target_pairs={{0,2},{1,3},{2,0},{3,1},{4,6},{5,7},{6,4},{7,5},{8,10},{9,11},{10,... | collective-permute-start | bytes 442376 | tf_op jit(solution)/shard_map/ppermute | solution.py:23
  7.1 5.7 %collective-permute-start.22 = (bf16[64,512]{1,0:T(8,128)(2,1)S(1)}, bf16[64,512]{1,0:T(8,128)(2,1)S(1)}, u32[]{:S(2)}, u32[]{:S(2)}) collective-permute-start(bf16[64,512]{1,0:T(8,128)(2,1)S(1)} %collective-permute-done.20.refs_4_), channel_id=1, source_target_pairs={{0,2},{1,3},{2,0},{3,1},{4,6},{5,7},{6,4},{7,5},{8,10},{9,11},{10,... | collective-permute-start | bytes 196616 | tf_op jit(solution)/shard_map/ppermute | solution.py:23
  7.5 8.2 %collective-permute-start.21 = (bf16[64,512]{1,0:T(8,128)(2,1)S(1)}, bf16[64,512]{1,0:T(8,128)(2,1)S(1)}, u32[]{:S(2)}, u32[]{:S(2)}) collective-permute-start(bf16[64,512]{1,0:T(8,128)(2,1)S(1)} %collective-permute-done.20.refs_4_), channel_id=1, source_target_pairs={{0,1},{1,0},{2,3},{3,2},{4,5},{5,4},{6,7},{7,6},{8,9},{9,8},{10,11... | collective-permute-start | bytes 196616 | tf_op jit(solution)/shard_map/ppermute | solution.py:23
  7.5 22.3 %collective-permute-start.24 = (bf16[64,1792]{1,0:T(8,128)(2,1)S(1)}, bf16[64,1792]{1,0:T(8,128)(2,1)S(1)}, u32[]{:S(2)}, u32[]{:S(2)}) collective-permute-start(bf16[64,1792]{1,0:T(8,128)(2,1)S(1)} %copy-done.2), channel_id=1, source_target_pairs={{0,4},{1,5},{2,6},{3,7},{4,0},{5,1},{6,2},{7,3},{8,12},{9,13},{10,... | collective-permute-start | bytes 688136 | tf_op jit(solution)/shard_map/ppermute | solution.py:23
  9.1 21.2 %collective-permute-start.29 = (bf16[64,1792]{1,0:T(8,128)(2,1)S(1)}, bf16[64,1792]{1,0:T(8,128)(2,1)S(1)}, u32[]{:S(2)}, u32[]{:S(2)}) collective-permute-start(bf16[64,1792]{1,0:T(8,128)(2,1)S(1)} %copy-done.2), channel_id=1, source_target_pairs={{0,1},{1,0},{2,3},{3,2},{4,5},{5,4},{6,7},{7,6},{8,9},{9,8},{10,11... | collective-permute-start | bytes 688136 | tf_op jit(solution)/shard_map/ppermute | solution.py:23
  12.8 13.9 %collective-permute-start.4 = (bf16[64,1152]{1,0:T(8,128)(2,1)S(1)}, bf16[64,1152]{1,0:T(8,128)(2,1)S(1)}, u32[]{:S(2)}, u32[]{:S(2)}) collective-permute-start(bf16[64,1152]{1,0:T(8,128)(2,1)S(1)} %split.1), channel_id=1, source_target_pairs={{0,8},{1,9},{2,10},{3,11},{4,12},{5,13},{6,14},{7,15},{8,0},{9,1},... | collective-permute-start | bytes 442376 | tf_op jit(solution)/shard_map/ppermute | solution.py:23
  15.6 11.1 %collective-permute-start = (bf16[64,1152]{1,0:T(8,128)(2,1)S(1)}, bf16[64,1152]{1,0:T(8,128)(2,1)S(1)}, u32[]{:S(2)}, u32[]{:S(2)}) collective-permute-start(bf16[64,1152]{1,0:T(8,128)(2,1)S(1)} %split.1), channel_id=1, source_target_pairs={{0,12},{1,13},{2,14},{3,15},{4,8},{5,9},{6,10},{7,11},{8,4},{9,5},... | collective-permute-start | bytes 442376 | tf_op jit(solution)/shard_map/ppermute | solution.py:23
  16.1 15.7 %collective-permute-start.18 = (bf16[64,1152]{1,0:T(8,128)(2,1)S(1)}, bf16[64,1152]{1,0:T(8,128)(2,1)S(1)}, u32[]{:S(2)}, u32[]{:S(2)}) collective-permute-start(bf16[64,1152]{1,0:T(8,128)(2,1)S(1)} %collective-permute-done.16.refs_0_), channel_id=1, source_target_pairs={{0,16},{16,0},{1,17},{17,1},{2,18},{18,2},{3,19},{19,3},{4,20},{20... | collective-permute-start | bytes 442376 | tf_op jit(solution)/shard_map/ppermute | solution.py:132
  26.7 5.1 %collective-permute-start.17 = (bf16[64,1152]{1,0:T(8,128)(2,1)S(1)}, bf16[64,1152]{1,0:T(8,128)(2,1)S(1)}, u32[]{:S(2)}, u32[]{:S(2)}) collective-permute-start(bf16[64,1152]{1,0:T(8,128)(2,1)S(1)} %collective-permute-done.16.refs_0_), channel_id=1, source_target_pairs={{0,1},{1,0},{2,3},{3,2},{4,5},{5,4},{6,7},{7,6},{8,9},{9,8},{10,11... | collective-permute-start | bytes 442376 | tf_op jit(solution)/shard_map/ppermute | solution.py:23
  26.7 1.5 %collective-permute-start.23 = (bf16[64,512]{1,0:T(8,128)(2,1)S(1)}, bf16[64,512]{1,0:T(8,128)(2,1)S(1)}, u32[]{:S(2)}, u32[]{:S(2)}) collective-permute-start(bf16[64,512]{1,0:T(8,128)(2,1)S(1)} %collective-permute-done.22.refs_6_), channel_id=1, source_target_pairs={{0,1},{1,0},{2,3},{3,2},{4,5},{5,4},{6,7},{7,6},{8,9},{9,8},{10,11... | collective-permute-start | bytes 196616 | tf_op jit(solution)/shard_map/ppermute | solution.py:23
  28.2 6.7 %collective-permute-start.5 = (bf16[64,1152]{1,0:T(8,128)(2,1)S(1)}, bf16[64,1152]{1,0:T(8,128)(2,1)S(1)}, u32[]{:S(2)}, u32[]{:S(2)}) collective-permute-start(bf16[64,1152]{1,0:T(8,128)(2,1)S(1)} %collective-permute-done.4.refs_0_), channel_id=1, source_target_pairs={{0,2},{1,3},{2,0},{3,1},{4,6},{5,7},{6,4},{7,5},{8,10},{9,11},{10,... | collective-permute-start | bytes 442376 | tf_op jit(solution)/shard_map/ppermute | solution.py:23
  29.8 10.0 %collective-permute-start.26 = (bf16[64,1792]{1,0:T(8,128)(2,1)S(1)}, bf16[64,1792]{1,0:T(8,128)(2,1)S(1)}, u32[]{:S(2)}, u32[]{:S(2)}) collective-permute-start(bf16[64,1792]{1,0:T(8,128)(2,1)S(1)} %collective-permute-done.24.refs_8_), channel_id=1, source_target_pairs={{0,2},{1,3},{2,0},{3,1},{4,6},{5,7},{6,4},{7,5},{8,10},{9,11},{10,... | collective-permute-start | bytes 688136 | tf_op jit(solution)/shard_map/ppermute | solution.py:23
  30.2 6.3 %collective-permute-start.13 = (bf16[64,1152]{1,0:T(8,128)(2,1)S(1)}, bf16[64,1152]{1,0:T(8,128)(2,1)S(1)}, u32[]{:S(2)}, u32[]{:S(2)}) collective-permute-start(bf16[64,1152]{1,0:T(8,128)(2,1)S(1)} %collective-permute-done.4.refs_0_), channel_id=1, source_target_pairs={{0,16},{16,0},{1,17},{17,1},{2,18},{18,2},{3,19},{19,3},{4,20},{20... | collective-permute-start | bytes 442376 | tf_op jit(solution)/shard_map/ppermute | solution.py:132
  31.8 6.2 %collective-permute-start.11 = (bf16[64,1152]{1,0:T(8,128)(2,1)S(1)}, bf16[64,1152]{1,0:T(8,128)(2,1)S(1)}, u32[]{:S(2)}, u32[]{:S(2)}) collective-permute-start(bf16[64,1152]{1,0:T(8,128)(2,1)S(1)} %collective-permute-done.4.refs_0_), channel_id=1, source_target_pairs={{0,1},{1,0},{2,3},{3,2},{4,5},{5,4},{6,7},{7,6},{8,9},{9,8},{10,11... | collective-permute-start | bytes 442376 | tf_op jit(solution)/shard_map/ppermute | solution.py:23
  31.8 6.2 %collective-permute-start.15 = (bf16[64,1152]{1,0:T(8,128)(2,1)S(1)}, bf16[64,1152]{1,0:T(8,128)(2,1)S(1)}, u32[]{:S(2)}, u32[]{:S(2)}) collective-permute-start(bf16[64,1152]{1,0:T(8,128)(2,1)S(1)} %collective-permute-done.refs_6_), channel_id=1, source_target_pairs={{0,1},{1,0},{2,3},{3,2},{4,5},{5,4},{6,7},{7,6},{8,9},{9,8},{10,11... | collective-permute-start | bytes 442376 | tf_op jit(solution)/shard_map/ppermute | solution.py:23
  34.9 7.4 %collective-permute-start.1 = (bf16[64,1152]{1,0:T(8,128)(2,1)S(1)}, bf16[64,1152]{1,0:T(8,128)(2,1)S(1)}, u32[]{:S(2)}, u32[]{:S(2)}) collective-permute-start(bf16[64,1152]{1,0:T(8,128)(2,1)S(1)} %collective-permute-done.refs_6_), channel_id=1, source_target_pairs={{0,2},{1,3},{2,0},{3,1},{4,6},{5,7},{6,4},{7,5},{8,10},{9,11},{10,... | collective-permute-start | bytes 442376 | tf_op jit(solution)/shard_map/ppermute | solution.py:23
  36.5 5.8 %collective-permute-start.9 = (bf16[64,1152]{1,0:T(8,128)(2,1)S(1)}, bf16[64,1152]{1,0:T(8,128)(2,1)S(1)}, u32[]{:S(2)}, u32[]{:S(2)}) collective-permute-start(bf16[64,1152]{1,0:T(8,128)(2,1)S(1)} %collective-permute-done.refs_6_), channel_id=1, source_target_pairs={{0,16},{16,0},{1,17},{17,1},{2,18},{18,2},{3,19},{19,3},{4,20},{20... | collective-permute-start | bytes 442376 | tf_op jit(solution)/shard_map/ppermute | solution.py:132
  38.0 5.9 %collective-permute-start.19 = (bf16[64,1152]{1,0:T(8,128)(2,1)S(1)}, bf16[64,1152]{1,0:T(8,128)(2,1)S(1)}, u32[]{:S(2)}, u32[]{:S(2)}) collective-permute-start(bf16[64,1152]{1,0:T(8,128)(2,1)S(1)} %collective-permute-done.18.refs_2_), channel_id=1, source_target_pairs={{0,1},{1,0},{2,3},{3,2},{4,5},{5,4},{6,7},{7,6},{8,9},{9,8},{10,11... | collective-permute-start | bytes 442376 | tf_op jit(solution)/shard_map/ppermute | solution.py:23
  38.1 13.7 %collective-permute-start.25 = (bf16[64,1792]{1,0:T(8,128)(2,1)S(1)}, bf16[64,1792]{1,0:T(8,128)(2,1)S(1)}, u32[]{:S(2)}, u32[]{:S(2)}) collective-permute-start(bf16[64,1792]{1,0:T(8,128)(2,1)S(1)} %collective-permute-done.24.refs_8_), channel_id=1, source_target_pairs={{0,1},{1,0},{2,3},{3,2},{4,5},{5,4},{6,7},{7,6},{8,9},{9,8},{10,11... | collective-permute-start | bytes 688136 | tf_op jit(solution)/shard_map/ppermute | solution.py:23
  39.8 12.4 %collective-permute-start.27 = (bf16[64,1792]{1,0:T(8,128)(2,1)S(1)}, bf16[64,1792]{1,0:T(8,128)(2,1)S(1)}, u32[]{:S(2)}, u32[]{:S(2)}) collective-permute-start(bf16[64,1792]{1,0:T(8,128)(2,1)S(1)} %collective-permute-done.26.refs_10_), channel_id=1, source_target_pairs={{0,1},{1,0},{2,3},{3,2},{4,5},{5,4},{6,7},{7,6},{8,9},{9,8},{10,11... | collective-permute-start | bytes 688136 | tf_op jit(solution)/shard_map/ppermute | solution.py:23
  42.3 2.0 %collective-permute-start.12 = (bf16[64,1152]{1,0:T(8,128)(2,1)S(1)}, bf16[64,1152]{1,0:T(8,128)(2,1)S(1)}, u32[]{:S(2)}, u32[]{:S(2)}) collective-permute-start(bf16[64,1152]{1,0:T(8,128)(2,1)S(1)} %collective-permute-done.5.refs_2_), channel_id=1, source_target_pairs={{0,1},{1,0},{2,3},{3,2},{4,5},{5,4},{6,7},{7,6},{8,9},{9,8},{10,11... | collective-permute-start | bytes 442376 | tf_op jit(solution)/shard_map/ppermute | solution.py:23
  42.3 6.7 %collective-permute-start.6 = (bf16[64,1152]{1,0:T(8,128)(2,1)S(1)}, bf16[64,1152]{1,0:T(8,128)(2,1)S(1)}, u32[]{:S(2)}, u32[]{:S(2)}) collective-permute-start(bf16[64,1152]{1,0:T(8,128)(2,1)S(1)} %collective-permute-done.5.refs_2_), channel_id=1, source_target_pairs={{0,16},{16,0},{1,17},{17,1},{2,18},{18,2},{3,19},{19,3},{4,20},{20... | collective-permute-start | bytes 442376 | tf_op jit(solution)/shard_map/ppermute | solution.py:132
  43.9 7.8 %collective-permute-start.2 = (bf16[64,1152]{1,0:T(8,128)(2,1)S(1)}, bf16[64,1152]{1,0:T(8,128)(2,1)S(1)}, u32[]{:S(2)}, u32[]{:S(2)}) collective-permute-start(bf16[64,1152]{1,0:T(8,128)(2,1)S(1)} %collective-permute-done.1.refs_2_), channel_id=1, source_target_pairs={{0,16},{16,0},{1,17},{17,1},{2,18},{18,2},{3,19},{19,3},{4,20},{20... | collective-permute-start | bytes 442376 | tf_op jit(solution)/shard_map/ppermute | solution.py:132
  44.4 9.7 %collective-permute-start.14 = (bf16[64,1152]{1,0:T(8,128)(2,1)S(1)}, bf16[64,1152]{1,0:T(8,128)(2,1)S(1)}, u32[]{:S(2)}, u32[]{:S(2)}) collective-permute-start(bf16[64,1152]{1,0:T(8,128)(2,1)S(1)} %collective-permute-done.13.refs_4_), channel_id=1, source_target_pairs={{0,1},{1,0},{2,3},{3,2},{4,5},{5,4},{6,7},{7,6},{8,9},{9,8},{10,11... | collective-permute-start | bytes 442376 | tf_op jit(solution)/shard_map/ppermute | solution.py:23
  49.1 5.9 %collective-permute-start.8 = (bf16[64,1152]{1,0:T(8,128)(2,1)S(1)}, bf16[64,1152]{1,0:T(8,128)(2,1)S(1)}, u32[]{:S(2)}, u32[]{:S(2)}) collective-permute-start(bf16[64,1152]{1,0:T(8,128)(2,1)S(1)} %collective-permute-done.1.refs_2_), channel_id=1, source_target_pairs={{0,1},{1,0},{2,3},{3,2},{4,5},{5,4},{6,7},{7,6},{8,9},{9,8},{10,11... | collective-permute-start | bytes 442376 | tf_op jit(solution)/shard_map/ppermute | solution.py:23
  51.8 3.2 %collective-permute-start.10 = (bf16[64,1152]{1,0:T(8,128)(2,1)S(1)}, bf16[64,1152]{1,0:T(8,128)(2,1)S(1)}, u32[]{:S(2)}, u32[]{:S(2)}) collective-permute-start(bf16[64,1152]{1,0:T(8,128)(2,1)S(1)} %collective-permute-done.9.refs_4_), channel_id=1, source_target_pairs={{0,1},{1,0},{2,3},{3,2},{4,5},{5,4},{6,7},{7,6},{8,9},{9,8},{10,11... | collective-permute-start | bytes 442376 | tf_op jit(solution)/shard_map/ppermute | solution.py:23
  51.8 3.2 %collective-permute-start.7 = (bf16[64,1152]{1,0:T(8,128)(2,1)S(1)}, bf16[64,1152]{1,0:T(8,128)(2,1)S(1)}, u32[]{:S(2)}, u32[]{:S(2)}) collective-permute-start(bf16[64,1152]{1,0:T(8,128)(2,1)S(1)} %collective-permute-done.6.refs_0_), channel_id=1, source_target_pairs={{0,1},{1,0},{2,3},{3,2},{4,5},{5,4},{6,7},{7,6},{8,9},{9,8},{10,11... | collective-permute-start | bytes 442376 | tf_op jit(solution)/shard_map/ppermute | solution.py:23
  52.3 3.4 %collective-permute-start.3 = (bf16[64,1152]{1,0:T(8,128)(2,1)S(1)}, bf16[64,1152]{1,0:T(8,128)(2,1)S(1)}, u32[]{:S(2)}, u32[]{:S(2)}) collective-permute-start(bf16[64,1152]{1,0:T(8,128)(2,1)S(1)} %collective-permute-done.2.refs_0_), channel_id=1, source_target_pairs={{0,1},{1,0},{2,3},{3,2},{4,5},{5,4},{6,7},{7,6},{8,9},{9,8},{10,11... | collective-permute-start | bytes 442376 | tf_op jit(solution)/shard_map/ppermute | solution.py:23
  56.2 6.1 %collective-permute-start.32 = (bf16[144,128]{1,0:T(8,128)(2,1)S(1)}, bf16[144,128]{1,0:T(8,128)(2,1)S(1)}, u32[]{:S(2)}, u32[]{:S(2)}) collective-permute-start(bf16[144,128]{1,0:T(8,128)(2,1)S(1)} %shard_map.95.refs_0_), channel_id=1, source_target_pairs={{0,12},{1,13},{2,14},{3,15},{4,8},{5,9},{6,10},{7,11},{8,4},{9,5},... | collective-permute-start | bytes 110600 | tf_op jit(solution)/shard_map/ppermute | solution.py:23
  58.6 4.9 %collective-permute-start.35 = (bf16[144,128]{1,0:T(8,128)(2,1)S(1)}, bf16[144,128]{1,0:T(8,128)(2,1)S(1)}, u32[]{:S(2)}, u32[]{:S(2)}) collective-permute-start(bf16[144,128]{1,0:T(8,128)(2,1)S(1)} %shard_map.95.refs_0_), channel_id=1, source_target_pairs={{0,8},{1,9},{2,10},{3,11},{4,12},{5,13},{6,14},{7,15},{8,0},{9,1},... | collective-permute-start | bytes 110600 | tf_op jit(solution)/shard_map/ppermute | solution.py:23
  59.9 4.2 %collective-permute-start.38 = (bf16[144,128]{1,0:T(8,128)(2,1)S(1)}, bf16[144,128]{1,0:T(8,128)(2,1)S(1)}, u32[]{:S(2)}, u32[]{:S(2)}) collective-permute-start(bf16[144,128]{1,0:T(8,128)(2,1)S(1)} %shard_map.95.refs_0_), channel_id=1, source_target_pairs={{0,4},{1,5},{2,6},{3,7},{4,0},{5,1},{6,2},{7,3},{8,12},{9,13},{10,... | collective-permute-start | bytes 110600 | tf_op jit(solution)/shard_map/ppermute | solution.py:23
  60.7 4.9 %collective-permute-start.41 = (bf16[144,128]{1,0:T(8,128)(2,1)S(1)}, bf16[144,128]{1,0:T(8,128)(2,1)S(1)}, u32[]{:S(2)}, u32[]{:S(2)}) collective-permute-start(bf16[144,128]{1,0:T(8,128)(2,1)S(1)} %shard_map.95.refs_0_), channel_id=1, source_target_pairs={{0,1},{1,0},{2,3},{3,2},{4,5},{5,4},{6,7},{7,6},{8,9},{9,8},{10,11... | collective-permute-start | bytes 110600 | tf_op jit(solution)/shard_map/ppermute | solution.py:23
  60.7 5.5 %collective-permute-start.30 = (bf16[144,128]{1,0:T(8,128)(2,1)S(1)}, bf16[144,128]{1,0:T(8,128)(2,1)S(1)}, u32[]{:S(2)}, u32[]{:S(2)}) collective-permute-start(bf16[144,128]{1,0:T(8,128)(2,1)S(1)} %shard_map.95.refs_0_), channel_id=1, source_target_pairs={{0,2},{1,3},{2,0},{3,1},{4,6},{5,7},{6,4},{7,5},{8,10},{9,11},{10,... | collective-permute-start | bytes 110600 | tf_op jit(solution)/shard_map/ppermute | solution.py:23
  62.3 5.3 %collective-permute-start.42 = (bf16[144,128]{1,0:T(8,128)(2,1)S(1)}, bf16[144,128]{1,0:T(8,128)(2,1)S(1)}, u32[]{:S(2)}, u32[]{:S(2)}) collective-permute-start(bf16[144,128]{1,0:T(8,128)(2,1)S(1)} %collective-permute-done.32.refs_1_), channel_id=1, source_target_pairs={{0,1},{1,0},{2,3},{3,2},{4,5},{5,4},{6,7},{7,6},{8,9},{9,8},{10,11... | collective-permute-start | bytes 110600 | tf_op jit(solution)/shard_map/ppermute | solution.py:23
  63.5 4.1 %collective-permute-start.43 = (bf16[144,128]{1,0:T(8,128)(2,1)S(1)}, bf16[144,128]{1,0:T(8,128)(2,1)S(1)}, u32[]{:S(2)}, u32[]{:S(2)}) collective-permute-start(bf16[144,128]{1,0:T(8,128)(2,1)S(1)} %collective-permute-done.35.refs_2_), channel_id=1, source_target_pairs={{0,1},{1,0},{2,3},{3,2},{4,5},{5,4},{6,7},{7,6},{8,9},{9,8},{10,11... | collective-permute-start | bytes 110600 | tf_op jit(solution)/shard_map/ppermute | solution.py:23
  64.1 4.1 %collective-permute-start.33 = (bf16[144,128]{1,0:T(8,128)(2,1)S(1)}, bf16[144,128]{1,0:T(8,128)(2,1)S(1)}, u32[]{:S(2)}, u32[]{:S(2)}) collective-permute-start(bf16[144,128]{1,0:T(8,128)(2,1)S(1)} %collective-permute-done.32.refs_1_), channel_id=1, source_target_pairs={{0,2},{1,3},{2,0},{3,1},{4,6},{5,7},{6,4},{7,5},{8,10},{9,11},{10,... | collective-permute-start | bytes 110600 | tf_op jit(solution)/shard_map/ppermute | solution.py:23
  65.6 4.0 %collective-permute-start.36 = (bf16[144,128]{1,0:T(8,128)(2,1)S(1)}, bf16[144,128]{1,0:T(8,128)(2,1)S(1)}, u32[]{:S(2)}, u32[]{:S(2)}) collective-permute-start(bf16[144,128]{1,0:T(8,128)(2,1)S(1)} %collective-permute-done.35.refs_2_), channel_id=1, source_target_pairs={{0,2},{1,3},{2,0},{3,1},{4,6},{5,7},{6,4},{7,5},{8,10},{9,11},{10,... | collective-permute-start | bytes 110600 | tf_op jit(solution)/shard_map/ppermute | solution.py:23
  66.1 4.0 %collective-permute-start.39 = (bf16[144,128]{1,0:T(8,128)(2,1)S(1)}, bf16[144,128]{1,0:T(8,128)(2,1)S(1)}, u32[]{:S(2)}, u32[]{:S(2)}) collective-permute-start(bf16[144,128]{1,0:T(8,128)(2,1)S(1)} %collective-permute-done.38.refs_3_), channel_id=1, source_target_pairs={{0,2},{1,3},{2,0},{3,1},{4,6},{5,7},{6,4},{7,5},{8,10},{9,11},{10,... | collective-permute-start | bytes 110600 | tf_op jit(solution)/shard_map/ppermute | solution.py:23
  67.6 4.2 %collective-permute-start.44 = (bf16[144,128]{1,0:T(8,128)(2,1)S(1)}, bf16[144,128]{1,0:T(8,128)(2,1)S(1)}, u32[]{:S(2)}, u32[]{:S(2)}) collective-permute-start(bf16[144,128]{1,0:T(8,128)(2,1)S(1)} %collective-permute-done.38.refs_3_), channel_id=1, source_target_pairs={{0,1},{1,0},{2,3},{3,2},{4,5},{5,4},{6,7},{7,6},{8,9},{9,8},{10,11... | collective-permute-start | bytes 110600 | tf_op jit(solution)/shard_map/ppermute | solution.py:23
  67.6 5.1 %collective-permute-start.31 = (bf16[144,128]{1,0:T(8,128)(2,1)S(1)}, bf16[144,128]{1,0:T(8,128)(2,1)S(1)}, u32[]{:S(2)}, u32[]{:S(2)}) collective-permute-start(bf16[144,128]{1,0:T(8,128)(2,1)S(1)} %collective-permute-done.30.refs_0_), channel_id=1, source_target_pairs={{0,1},{1,0},{2,3},{3,2},{4,5},{5,4},{6,7},{7,6},{8,9},{9,8},{10,11... | collective-permute-start | bytes 110600 | tf_op jit(solution)/shard_map/ppermute | solution.py:23
  68.2 4.5 %collective-permute-start.34 = (bf16[144,128]{1,0:T(8,128)(2,1)S(1)}, bf16[144,128]{1,0:T(8,128)(2,1)S(1)}, u32[]{:S(2)}, u32[]{:S(2)}) collective-permute-start(bf16[144,128]{1,0:T(8,128)(2,1)S(1)} %collective-permute-done.33.refs_1_), channel_id=1, source_target_pairs={{0,1},{1,0},{2,3},{3,2},{4,5},{5,4},{6,7},{7,6},{8,9},{9,8},{10,11... | collective-permute-start | bytes 110600 | tf_op jit(solution)/shard_map/ppermute | solution.py:23
  69.5 3.2 %collective-permute-start.37 = (bf16[144,128]{1,0:T(8,128)(2,1)S(1)}, bf16[144,128]{1,0:T(8,128)(2,1)S(1)}, u32[]{:S(2)}, u32[]{:S(2)}) collective-permute-start(bf16[144,128]{1,0:T(8,128)(2,1)S(1)} %collective-permute-done.36.refs_2_), channel_id=1, source_target_pairs={{0,1},{1,0},{2,3},{3,2},{4,5},{5,4},{6,7},{7,6},{8,9},{9,8},{10,11... | collective-permute-start | bytes 110600 | tf_op jit(solution)/shard_map/ppermute | solution.py:23
  70.1 2.7 %collective-permute-start.40 = (bf16[144,128]{1,0:T(8,128)(2,1)S(1)}, bf16[144,128]{1,0:T(8,128)(2,1)S(1)}, u32[]{:S(2)}, u32[]{:S(2)}) collective-permute-start(bf16[144,128]{1,0:T(8,128)(2,1)S(1)} %collective-permute-done.39.refs_3_), channel_id=1, source_target_pairs={{0,1},{1,0},{2,3},{3,2},{4,5},{5,4},{6,7},{7,6},{8,9},{9,8},{10,11... | collective-permute-start | bytes 110600 | tf_op jit(solution)/shard_map/ppermute | solution.py:23
  (8 other events, 107.7 us)

commit v2 on v1

--- a/solution.py
+++ b/solution.py
@@ -25,93 +25,63 @@
 
 NT = (((1,), (1,)), ((), ()))
 VMEM = pl.BlockSpec(memory_space=pltpu.VMEM)
-HBM = pl.BlockSpec(memory_space=pltpu.HBM)
 MIB = 1 << 20
 
 
-def columns(ref, first, width):
-    return ref.at[:, pl.ds(pl.multiple_of(first * width, 128), width)]
-
-
-def run_copies(pairs, sems):
-    copies = [pltpu.make_async_copy(src, dst, sems.at[i]) for i, (src, dst) in enumerate(pairs)]
-    for copy in copies:
-        copy.start()
-    for copy in copies:
-        copy.wait()
-
-
-def split_kernel(inner, outer, mine, sems):
-    h_in, h_out = inner.shape[1] // 2, outer.shape[1] // 2
-    dom = lax.axis_index("dom") % 2
-    run_copies(
-        [(columns(inner, dom, h_in), mine.at[:, :h_in]), (columns(outer, dom, h_out), mine.at[:, h_in:])], sems
-    )
-
-
-def split(in_factor, out_factor):
-    rank = in_factor.shape[0]
-    width = (in_factor.shape[1] + out_factor.shape[1]) // 2
+def numbers_kernel(ids, out):
+    out[...] = jnp.broadcast_to(ids[...].astype(jnp.float32), out.shape).astype(jnp.bfloat16)
+
+
+def numbers_of(ids):
     return pl.pallas_call(
-        split_kernel,
-        out_shape=jax.ShapeDtypeStruct((rank, width), in_factor.dtype),
-        in_specs=[HBM, HBM],
+        numbers_kernel,
+        out_shape=jax.ShapeDtypeStruct((16, ids.shape[1]), jnp.bfloat16),
+        in_specs=[VMEM],
         out_specs=VMEM,
-        scratch_shapes=[pltpu.SemaphoreType.DMA((2,))],
         cost_estimate=pl.CostEstimate(flops=2 * 10**10, bytes_accessed=0, transcendentals=0),
         compiler_params=pltpu.CompilerParams(vmem_limit_bytes=2 * MIB),
-        name="split",
-    )(in_factor, out_factor)
-
-
-INNER, OUTER, CARRIED, CROSSED = range(4)
-
-
-def project_kernel(keys, h_in, has_part, final, act, grad, *refs):
+        name="numbers",
+    )(ids)
+
+
+INNER, OUTER = 0, 1
+
+
+def project_kernel(keys, has_part, final, act, grad, *refs):
     count = len(keys)
     pieces = refs[:count]
     out = refs[-1]
     rank = pieces[0].shape[0]
     me = lax.axis_index("shard")
-    dom = lax.axis_index("dom") % 2
+    even = lax.axis_index("dom") % 2 == 0
     part = refs[count][...] if has_part else None
     sums = [part[:, :rank], part[:, rank:]] if has_part else [0.0, 0.0]
-
-    def add(j, piece, place, lo, size):
-        rows = (act, grad)[j][:, pl.ds(pl.multiple_of(place * size, 128), size)]
-        sums[j] = sums[j] + lax.dot_general(
-            rows, piece[:, lo : lo + size], NT, preferred_element_type=jnp.float32
+    for piece, (first, second, kind) in zip(pieces, keys):
+        src = me ^ (first if first == second else jnp.where(even, first, second))
+        width = piece.shape[1]
+        rows = (act, grad)[kind][:, pl.ds(pl.multiple_of(src * width, 128), width)]
+        sums[kind] = sums[kind] + lax.dot_general(
+            rows, piece[...], NT, preferred_element_type=jnp.float32
         )
-
-    for piece, (offset, kind) in zip(pieces, keys):
-        src = me ^ offset
-        width = piece.shape[1]
-        if kind in (INNER, OUTER):
-            add(kind, piece, src, 0, width)
-        else:
-            place = 2 * src + (dom if kind == CARRIED else 1 - dom)
-            add(INNER, piece, place, 0, h_in)
-            add(OUTER, piece, place, h_in, width - h_in)
     total = jnp.concatenate(sums, axis=1)
     if final:
-        ids = refs[count + 1]
         out[: 2 * rank] = total.T.astype(jnp.bfloat16)
-        out[2 * rank :] = jnp.broadcast_to(ids[...].astype(jnp.float32), (16, ids.shape[1])).astype(jnp.bfloat16)
+        out[2 * rank :] = refs[count + 1][...]
     else:
         out[...] = total
 
 
-def project(act, grad, pieces, keys, h_in, part, ids):
+def project(act, grad, pieces, keys, part, numbers):
     tokens = act.shape[0]
     rank = pieces[0].shape[0]
-    extra = (() if part is None else (part,)) + (() if ids is None else (ids,))
-    if ids is None:
+    extra = (() if part is None else (part,)) + (() if numbers is None else (numbers,))
+    if numbers is None:
         shape = jax.ShapeDtypeStruct((tokens, 2 * rank), jnp.float32)
     else:
         shape = jax.ShapeDtypeStruct((2 * rank + 16, tokens), jnp.bfloat16)
     size = sum(piece.size for piece in pieces)
     return pl.pallas_call(
-        functools.partial(project_kernel, tuple(keys), h_in, part is not None, ids is not None),
+        functools.partial(project_kernel, tuple(keys), part is not None, numbers is not None),
         out_shape=shape,
         in_specs=[VMEM] * (2 + len(pieces) + len(extra)),
         out_specs=VMEM,
@@ -122,51 +92,48 @@
     )(act, grad, *pieces, *extra)
 
 
-def project_halves(n, act, grad, ids, in_factor, out_factor):
+def project_paired(n, act, grad, ids, in_factor, out_factor):
     far, near, cores = grid_of(n)
     fars = [k * near * cores for k in range(1, far)]
     nears = [k * cores for k in range(1, near)]
-    h_in = in_factor.shape[1] // 2
-
-    def crossed(value):
-        return lax.ppermute(value, "dom", [(0, 1), (1, 0)])
-
-    mine = split(in_factor, out_factor)
-    held = {(0, INNER): in_factor, (0, OUTER): out_factor}
-
-    def bring(key, source, offset):
-        held[key] = moved(held[source] if source in held else mine, n, offset)
-
-    near_keys = []
-    for m in nears:
-        bring((m, CARRIED), (0, CARRIED), m)
-        held[m, CROSSED] = crossed(held[m, CARRIED])
-        near_keys += [(m, CARRIED), (m, CROSSED)]
-    waves = []
-    for i, f in enumerate(fars):
-        wave = []
-        for kind in (INNER, OUTER) if i == 0 else (CARRIED,):
-            bring((f, kind), (0, kind), f)
-            wave.append((f, kind))
-            for m in nears:
-                bring((f ^ m, kind), (f, kind), m)
-                wave.append((f ^ m, kind))
-        if i:
-            for o, _ in list(wave):
-                held[o, CROSSED] = crossed(held[o, CARRIED])
-            wave += [(o, CROSSED) for o, _ in wave]
-        waves.append(wave)
-    for o, kind in list(held):
-        held[o ^ 1, kind] = moved(held[o, kind], n, 1)
-    rest = [key for wave in waves[1:] for key in wave]
-    late = [key for key in rest[len(rest) // 2 - len(nears) :] if key != waves[-1][0]]
-    groups = [[(0, INNER), (0, OUTER)], near_keys + waves[0], [key for key in rest if key not in late]]
-    groups += [late[:-1], late[-1:]]
+    kinds = (OUTER, INNER)
+    held = {(0, 0, INNER): in_factor, (0, 0, OUTER): out_factor}
+
+    def bring(source, even, odd):
+        to = (source[0] ^ even, source[1] ^ odd)
+        pairs = [(i, i ^ even) for i in range(n)] + [(n + i, n + (i ^ odd)) for i in range(n)]
+        for kind in kinds:
+            held[(*to, kind)] = lax.ppermute(held[(*source, kind)], ("dom", "shard"), pairs)
+        return to
+
+    def cross(source):
+        to = source[::-1]
+        for kind in kinds:
+            held[(*to, kind)] = lax.ppermute(held[(*source, kind)], "dom", [(0, 1), (1, 0)])
+        return to
+
+    own = (0, 0)
+    first = [bring(own, m, m) for m in nears]
+    nearest = bring(own, fars[0], fars[0])
+    first.append(nearest)
+    turned = [bring(nearest, m, m) for m in nears]
+    middle, last = [], []
+    for i in range(1, far - 1, 2):
+        there = bring(own, fars[i], fars[i + 1])
+        beside = [bring(there, m, m) for m in nears]
+        middle += [there, *beside, cross(there)]
+        last += [cross(to) for to in beside]
+    for key in list(held):
+        held[key[0] ^ 1, key[1] ^ 1, key[2]] = lax.ppermute(
+            held[key], "shard", [(i, i ^ 1) for i in range(n)]
+        )
+    numbers = numbers_of(ids)
     part = None
-    for i, keys in enumerate(groups):
-        keys = [(o ^ c, kind) for o, kind in keys for c in (0, 1)]
-        last = ids if i == len(groups) - 1 else None
-        part = project(act, grad, [held[key] for key in keys], keys, h_in, part, last)
+    groups = ([own], first, middle, turned, last)
+    for i, group in enumerate(groups):
+        keys = [(a ^ c, b ^ c, kind) for a, b in group for c in (0, 1) for kind in kinds]
+        rows = numbers if i == len(groups) - 1 else None
+        part = project(act, grad, [held[key] for key in keys], keys, part, rows)
     return part
 
 
@@ -308,12 +275,12 @@
     far, near, cores = grid_of(n)
     fars = [k * near * cores for k in range(1, far)]
     nears = [k * cores for k in range(1, near)]
-    aligned = doms == 2 and in_factor.shape[1] % 256 == 0 and out_factor.shape[1] % 256 == 0
-    project_all = project_halves if aligned else project_plain
+    aligned = doms == 2 and far % 2 == 0 and in_factor.shape[1] % 128 == 0 and out_factor.shape[1] % 128 == 0
+    project_all = project_paired if aligned else project_plain
     mine = project_all(n, activations, out_grads, example_ids, in_factor, out_factor)
     query = precondition(query_grads, basis_in, basis_out, eigen)
     row = {0: mine}
-    for i, f in reversed(list(enumerate(fars))):
+    for i, f in sorted(enumerate(fars), key=lambda item: (item[0] == far // 2 - 1, -item[0])):
         row[f] = moved(mine, n, f)
     rest = {o ^ m: moved(block, n, m) for m in nears for o, block in row.items()}
     steps = [row, {o ^ 1: moved(block, n, 1) for o, block in row.items()}]

time: 74 us -> 62.6 us (0.85)
  waiting for transfers between devices: 30.9 us -> 23.6 us
  starting transfers between devices: 33.5 us -> 30.8 us
  local copies, waits for them, and re-layouts: 1.82 us -> 0.7 us
    ppermute x40 -> x15, waiting for transfers between devices: 23.5 us -> 4.13 us  [moved(): return lax.ppermute(value, 'shard', [(i, i ^ offset) for i in range(n)])]
    ppermute x40 -> x15, starting transfers between devices: 26.9 us -> 9.44 us  [moved(): return lax.ppermute(value, 'shard', [(i, i ^ offset) for i in range(n)])]
    ppermute x5 -> x30, starting transfers between devices: 6.64 us -> 21.3 us  [the longest x10 13.9 us: bring(): held[*to, kind] = lax.ppermute(held[*source, kind], ('dom', 'shard'), pairs)]
    ppermute x5 -> x30, waiting for transfers between devices: 7.39 us -> 19.5 us  [the longest x4 8.92 us: cross(): held[*to, kind] = lax.ppermute(held[*source, kind], 'dom', [(0, 1), (1, 0)])]
    unnamed x22 -> x18, local copies, waits for them, and re-layouts: 1.82 us -> 0.7 us
  transfers between devices with their start and end apart: 45 -> 45, of which waited for: 13 -> 19; matrix products, arithmetic and copies ran while one was open for 0% -> 0% of each run, Pallas kernels for 8% -> 9%
where the time goes in v2:
time: 62.6 us; the launch traced here: 62.4 us
  starting transfers between devices  30.8 us (49%)
  waiting for transfers between devices  23.6 us (38%)
  Pallas kernels  7.12 us (11%)
  local copies, waits for them, and re-layouts  0.7 us (1%)
    ppermute x10, starting transfers between devices, bring(): held[*to, kind] = lax.ppermute(held[*source, kind], ('dom', 'shard'), pairs)  13.9 us
    ppermute x15, starting transfers between devices, moved(): return lax.ppermute(value, 'shard', [(i, i ^ offset) for i in range(n)])  9.44 us
    ppermute x4, waiting for transfers between devices, cross(): held[*to, kind] = lax.ppermute(held[*source, kind], 'dom', [(0, 1), (1, 0)])  8.92 us
    ppermute x10, waiting for transfers between devices, bring(): held[*to, kind] = lax.ppermute(held[*source, kind], ('dom', 'shard'), pairs)  7.8 us
    ppermute x4, starting transfers between devices, cross(): held[*to, kind] = lax.ppermute(held[*source, kind], 'dom', [(0, 1), (1, 0)])  5.29 us
    ppermute x15, waiting for transfers between devices, moved(): return lax.ppermute(value, 'shard', [(i, i ^ offset) for i in range(n)])  4.13 us
    pallas_call x5, Pallas kernels, project(): pl.pallas_call(functools.partial(project_kernel, tuple(keys), part is not...  3.5 us
    ppermute x16, waiting for transfers between devices, project_paired(): lax.ppermute(held[key], 'shard', [(i, i ^ 1) for i in range(n)])  2.75 us
  transfers between devices with their start and end apart: 45, of which 19 were waited for; matrix products, arithmetic and copies ran while one was open for 0% of the time, Pallas kernels for 9%

profile of v2, /device:TPU:0, one launch (start us, length us, event | category | flops | bytes accessed | tf_op | source)
XLA Modules:
  0.0 62.4 jit_solution(12376099821551474860)
XLA Ops:
  0.0 3.1 %collective-permute-start.10 = (bf16[64,512]{1,0:T(8,128)(2,1)}, bf16[64,512]{1,0:T(8,128)(2,1)S(1)}, u32[]{:S(2)}, u32[]{:S(2)}) collective-permute-start(bf16[64,512]{1,0:T(8,128)(2,1)} %refs_1_.1), channel_id=1, source_target_pairs={{0,4},{1,5},{2,6},{3,7},{4,0},{5,1},{6,2},{7,3},{8,12},{9,13},{10,... | collective-permute-start | bytes 196616 | tf_op jit(solution)/shard_map/ppermute | solution.py:106
  3.1 1.5 %collective-permute-start.23 = (bf16[64,512]{1,0:T(8,128)(2,1)}, bf16[64,512]{1,0:T(8,128)(2,1)S(1)}, u32[]{:S(2)}, u32[]{:S(2)}) collective-permute-start(bf16[64,512]{1,0:T(8,128)(2,1)} %refs_1_.1), channel_id=1, source_target_pairs={{0,2},{1,3},{2,0},{3,1},{4,6},{5,7},{6,4},{7,5},{8,10},{9,11},{10,... | collective-permute-start | bytes 196616 | tf_op jit(solution)/shard_map/ppermute | solution.py:106
  4.7 2.6 %collective-permute-start.3 = (bf16[64,512]{1,0:T(8,128)(2,1)}, bf16[64,512]{1,0:T(8,128)(2,1)S(1)}, u32[]{:S(2)}, u32[]{:S(2)}) collective-permute-start(bf16[64,512]{1,0:T(8,128)(2,1)} %refs_1_.1), channel_id=1, source_target_pairs={{0,8},{1,9},{2,10},{3,11},{4,12},{5,13},{6,14},{7,15},{8,0},{9,1},... | collective-permute-start | bytes 196616 | tf_op jit(solution)/shard_map/ppermute | solution.py:106
  7.7 0.9 %collective-permute-start = (bf16[64,1792]{1,0:T(8,128)(2,1)}, bf16[64,1792]{1,0:T(8,128)(2,1)S(1)}, u32[]{:S(2)}, u32[]{:S(2)}) collective-permute-start(bf16[64,1792]{1,0:T(8,128)(2,1)} %refs_0_.1), channel_id=1, source_target_pairs={{0,8},{1,9},{2,10},{3,11},{4,12},{5,13},{6,14},{7,15},{8,0},{9,1},... | collective-permute-start | bytes 688136 | tf_op jit(solution)/shard_map/ppermute | solution.py:106
  8.6 1.9 %collective-permute-start.22 = (bf16[64,1792]{1,0:T(8,128)(2,1)}, bf16[64,1792]{1,0:T(8,128)(2,1)S(1)}, u32[]{:S(2)}, u32[]{:S(2)}) collective-permute-start(bf16[64,1792]{1,0:T(8,128)(2,1)} %refs_0_.1), channel_id=1, source_target_pairs={{0,2},{1,3},{2,0},{3,1},{4,6},{5,7},{6,4},{7,5},{8,10},{9,11},{10,... | collective-permute-start | bytes 688136 | tf_op jit(solution)/shard_map/ppermute | solution.py:106
  10.5 1.2 %collective-permute-done.3.refs_1_ = bf16[64,512]{1,0:T(8,128)(2,1)S(1)} collective-permute-done((bf16[64,512]{1,0:T(8,128)(2,1)}, bf16[64,512]{1,0:T(8,128)(2,1)S(1)}, u32[]{:S(2)}, u32[]{:S(2)}) %collective-permute-start.3) | collective-permute-done | bytes 65568 | tf_op jit(solution)/shard_map/ppermute | solution.py:106
  11.8 0.7 %collective-permute-start.4 = (bf16[64,512]{1,0:T(8,128)(2,1)S(1)}, bf16[64,512]{1,0:T(8,128)(2,1)S(1)}, u32[]{:S(2)}, u32[]{:S(2)}) collective-permute-start(bf16[64,512]{1,0:T(8,128)(2,1)S(1)} %collective-permute-done.3.refs_1_), channel_id=1, source_target_pairs={{0,2},{1,3},{2,0},{3,1},{4,6},{5,7},{6,4},{7,5},{8,10},{9,11},{10,... | collective-permute-start | bytes 196616 | tf_op jit(solution)/shard_map/ppermute | solution.py:106
  12.4 0.5 collective-permute-done.25.refs_3_
  13.0 1.5 %collective-permute-start.19 = (bf16[64,512]{1,0:T(8,128)(2,1)S(1)}, bf16[64,512]{1,0:T(8,128)(2,1)S(1)}, u32[]{:S(2)}, u32[]{:S(2)}) collective-permute-start(bf16[64,512]{1,0:T(8,128)(2,1)S(1)} %collective-permute-done.3.refs_1_), channel_id=1, source_target_pairs={{0,16},{16,0},{1,17},{17,1},{2,18},{18,2},{3,19},{19,3},{4,20},{20... | collective-permute-start | bytes 196616 | tf_op jit(solution)/shard_map/ppermute | solution.py:112
  14.4 2.4 %collective-permute-done.4.refs_5_ = bf16[64,512]{1,0:T(8,128)(2,1)S(1)} collective-permute-done((bf16[64,512]{1,0:T(8,128)(2,1)S(1)}, bf16[64,512]{1,0:T(8,128)(2,1)S(1)}, u32[]{:S(2)}, u32[]{:S(2)}) %collective-permute-start.4) | collective-permute-done | bytes 65568 | tf_op jit(solution)/shard_map/ppermute | solution.py:106
  17.2 1.0 %collective-permute-start.11 = (bf16[64,512]{1,0:T(8,128)(2,1)S(1)}, bf16[64,512]{1,0:T(8,128)(2,1)S(1)}, u32[]{:S(2)}, u32[]{:S(2)}) collective-permute-start(bf16[64,512]{1,0:T(8,128)(2,1)S(1)} %collective-permute-done.10.refs_5_), channel_id=1, source_target_pairs={{0,2},{1,3},{2,0},{3,1},{4,6},{5,7},{6,4},{7,5},{8,10},{9,11},{10,... | collective-permute-start | bytes 196616 | tf_op jit(solution)/shard_map/ppermute | solution.py:106
  18.4 1.7 %collective-permute-done.8.refs_4_ = bf16[64,1792]{1,0:T(8,128)(2,1)S(1)} collective-permute-done((bf16[64,1792]{1,0:T(8,128)(2,1)}, bf16[64,1792]{1,0:T(8,128)(2,1)S(1)}, u32[]{:S(2)}, u32[]{:S(2)}) %collective-permute-start.8) | collective-permute-done | bytes 229408 | tf_op jit(solution)/shard_map/ppermute | solution.py:106
  20.1 1.3 %collective-permute-done.refs_0_ = bf16[64,1792]{1,0:T(8,128)(2,1)S(1)} collective-permute-done((bf16[64,1792]{1,0:T(8,128)(2,1)}, bf16[64,1792]{1,0:T(8,128)(2,1)S(1)}, u32[]{:S(2)}, u32[]{:S(2)}) %collective-permute-start) | collective-permute-done | bytes 229408 | tf_op jit(solution)/shard_map/ppermute | solution.py:106
  21.4 0.5 collective-permute-start.1
  22.0 0.5 collective-permute-start.17
  22.5 1.1 %collective-permute-done.17.refs_7_ = bf16[64,512]{1,0:T(8,128)(2,1)S(1)} collective-permute-done((bf16[64,512]{1,0:T(8,128)(2,1)S(1)}, bf16[64,512]{1,0:T(8,128)(2,1)S(1)}, u32[]{:S(2)}, u32[]{:S(2)}) %collective-permute-start.17) | collective-permute-done | bytes 65568 | tf_op jit(solution)/shard_map/ppermute | solution.py:127
  23.8 1.1 %collective-permute-done.21.refs_11_ = bf16[64,512]{1,0:T(8,128)(2,1)S(1)} collective-permute-done((bf16[64,512]{1,0:T(8,128)(2,1)S(1)}, bf16[64,512]{1,0:T(8,128)(2,1)S(1)}, u32[]{:S(2)}, u32[]{:S(2)}) %collective-permute-start.21) | collective-permute-done | bytes 65568 | tf_op jit(solution)/shard_map/ppermute | solution.py:127
  24.8 1.5 %collective-permute-start.5 = (bf16[64,512]{1,0:T(8,128)(2,1)S(1)}, bf16[64,512]{1,0:T(8,128)(2,1)S(1)}, u32[]{:S(2)}, u32[]{:S(2)}) collective-permute-start(bf16[64,512]{1,0:T(8,128)(2,1)S(1)} %collective-permute-done.4.refs_5_), channel_id=1, source_target_pairs={{0,16},{16,0},{1,17},{17,1},{2,18},{18,2},{3,19},{19,3},{4,20},{20... | collective-permute-start | bytes 196616 | tf_op jit(solution)/shard_map/ppermute | solution.py:112
  26.3 2.8 %collective-permute-done.5.refs_1_ = bf16[64,512]{1,0:T(8,128)(2,1)S(1)} collective-permute-done((bf16[64,512]{1,0:T(8,128)(2,1)S(1)}, bf16[64,512]{1,0:T(8,128)(2,1)S(1)}, u32[]{:S(2)}, u32[]{:S(2)}) %collective-permute-start.5) | collective-permute-done | bytes 65568 | tf_op jit(solution)/shard_map/ppermute | solution.py:112
  29.1 1.5 %collective-permute-start.18 = (bf16[64,1792]{1,0:T(8,128)(2,1)S(1)}, bf16[64,1792]{1,0:T(8,128)(2,1)S(1)}, u32[]{:S(2)}, u32[]{:S(2)}) collective-permute-start(bf16[64,1792]{1,0:T(8,128)(2,1)S(1)} %collective-permute-done.refs_0_), channel_id=1, source_target_pairs={{0,16},{16,0},{1,17},{17,1},{2,18},{18,2},{3,19},{19,3},{4,20},{20... | collective-permute-start | bytes 688136 | tf_op jit(solution)/shard_map/ppermute | solution.py:112
  30.6 1.2 %collective-permute-start.9 = (bf16[64,1792]{1,0:T(8,128)(2,1)S(1)}, bf16[64,1792]{1,0:T(8,128)(2,1)S(1)}, u32[]{:S(2)}, u32[]{:S(2)}) collective-permute-start(bf16[64,1792]{1,0:T(8,128)(2,1)S(1)} %collective-permute-done.8.refs_4_), channel_id=1, source_target_pairs={{0,2},{1,3},{2,0},{3,1},{4,6},{5,7},{6,4},{7,5},{8,10},{9,11},{10,... | collective-permute-start | bytes 688136 | tf_op jit(solution)/shard_map/ppermute | solution.py:106
  32.0 0.9 %collective-permute-start.2 = (bf16[64,1792]{1,0:T(8,128)(2,1)S(1)}, bf16[64,1792]{1,0:T(8,128)(2,1)S(1)}, u32[]{:S(2)}, u32[]{:S(2)}) collective-permute-start(bf16[64,1792]{1,0:T(8,128)(2,1)S(1)} %collective-permute-done.1.refs_4_), channel_id=1, source_target_pairs={{0,16},{16,0},{1,17},{17,1},{2,18},{18,2},{3,19},{19,3},{4,20},{20... | collective-permute-start | bytes 688136 | tf_op jit(solution)/shard_map/ppermute | solution.py:112
  32.8 4.1 %collective-permute-done.18.refs_8_ = bf16[64,1792]{1,0:T(8,128)(2,1)S(1)} collective-permute-done((bf16[64,1792]{1,0:T(8,128)(2,1)S(1)}, bf16[64,1792]{1,0:T(8,128)(2,1)S(1)}, u32[]{:S(2)}, u32[]{:S(2)}) %collective-permute-start.18) | collective-permute-done | bytes 229408 | tf_op jit(solution)/shard_map/ppermute | solution.py:112
  36.9 0.5 collective-permute-start.7
  37.4 1.2 %collective-permute-done.9.refs_0_ = bf16[64,1792]{1,0:T(8,128)(2,1)S(1)} collective-permute-done((bf16[64,1792]{1,0:T(8,128)(2,1)S(1)}, bf16[64,1792]{1,0:T(8,128)(2,1)S(1)}, u32[]{:S(2)}, u32[]{:S(2)}) %collective-permute-start.9) | collective-permute-done | bytes 229408 | tf_op jit(solution)/shard_map/ppermute | solution.py:106
  38.6 0.5 collective-permute-start.12
  39.1 1.7 %collective-permute-done.2.refs_0_ = bf16[64,1792]{1,0:T(8,128)(2,1)S(1)} collective-permute-done((bf16[64,1792]{1,0:T(8,128)(2,1)S(1)}, bf16[64,1792]{1,0:T(8,128)(2,1)S(1)}, u32[]{:S(2)}, u32[]{:S(2)}) %collective-permute-start.2) | collective-permute-done | bytes 229408 | tf_op jit(solution)/shard_map/ppermute | solution.py:112
  40.8 0.7 %copy-done.8 = s32[1,128]{1,0:T(1,128)S(1)} copy-done((s32[1,128]{1,0:T(1,128)S(1)}, s32[1,128]{1,0:T(1,128)}, u32[]{:S(2)}) %copy-start.8) | copy-done | bytes 536
  41.5 0.5 shard_map.91.refs_8_
  42.0 0.8 %shard_map.92.refs_12_ = f32[128,128]{1,0:T(8,128)S(1)} custom-call(bf16[128,8192]{1,0:T(8,128)(2,1)S(1)} %copy-done.1, bf16[128,28672]{1,0:T(8,128)(2,1)S(1)} %copy-done, bf16[64,1792]{1,0:T(8,128)(2,1)S(1)} %collective-permute-done.22.refs_0_, bf16[64,512]{1,0:T(8,128)(2,1)S(1)} %collective-permute-done.23.refs_1_, ...), custom_call_target="tpu_custom_call" | custom-call | flops 150994944 | bytes 2359296 | tf_op jit(solution)/shard_map/pallas_call | solution.py:83
  42.9 1.2 %shard_map.93.refs_4_ = f32[128,128]{1,0:T(8,128)S(1)} custom-call(bf16[128,8192]{1,0:T(8,128)(2,1)S(1)} %copy-done.1, bf16[128,28672]{1,0:T(8,128)(2,1)S(1)} %copy-done, bf16[64,1792]{1,0:T(8,128)(2,1)S(1)} %collective-permute-done.refs_0_, bf16[64,512]{1,0:T(8,128)(2,1)S(1)} %collective-permute-done.3.refs_1_, ...), custom_call_target="tpu_custom_call" | custom-call | flops 226492416 | bytes 3538944 | tf_op jit(solution)/shard_map/pallas_call | solution.py:83
  44.1 0.5 shard_map.94.refs_4_
  44.6 0.5 shard_map.95.refs_0_
  45.2 2.7 %collective-permute-start.32 = (bf16[144,128]{1,0:T(8,128)(2,1)S(1)}, bf16[144,128]{1,0:T(8,128)(2,1)S(1)}, u32[]{:S(2)}, u32[]{:S(2)}) collective-permute-start(bf16[144,128]{1,0:T(8,128)(2,1)S(1)} %shard_map.95.refs_0_), channel_id=1, source_target_pairs={{0,12},{1,13},{2,14},{3,15},{4,8},{5,9},{6,10},{7,11},{8,4},{9,5},... | collective-permute-start | bytes 110600 | tf_op jit(solution)/shard_map/ppermute | solution.py:23
  47.9 1.8 %collective-permute-start.38 = (bf16[144,128]{1,0:T(8,128)(2,1)S(1)}, bf16[144,128]{1,0:T(8,128)(2,1)S(1)}, u32[]{:S(2)}, u32[]{:S(2)}) collective-permute-start(bf16[144,128]{1,0:T(8,128)(2,1)S(1)} %shard_map.95.refs_0_), channel_id=1, source_target_pairs={{0,8},{1,9},{2,10},{3,11},{4,12},{5,13},{6,14},{7,15},{8,0},{9,1},... | collective-permute-start | bytes 110600 | tf_op jit(solution)/shard_map/ppermute | solution.py:23
  49.6 1.2 %collective-permute-start.30 = (bf16[144,128]{1,0:T(8,128)(2,1)S(1)}, bf16[144,128]{1,0:T(8,128)(2,1)S(1)}, u32[]{:S(2)}, u32[]{:S(2)}) collective-permute-start(bf16[144,128]{1,0:T(8,128)(2,1)S(1)} %shard_map.95.refs_0_), channel_id=1, source_target_pairs={{0,2},{1,3},{2,0},{3,1},{4,6},{5,7},{6,4},{7,5},{8,10},{9,11},{10,... | collective-permute-start | bytes 110600 | tf_op jit(solution)/shard_map/ppermute | solution.py:23
  50.8 0.6 collective-permute-done.32.refs_1_
  51.4 0.8 %collective-permute-done.35.refs_2_ = bf16[144,128]{1,0:T(8,128)(2,1)S(1)} collective-permute-done((bf16[144,128]{1,0:T(8,128)(2,1)S(1)}, bf16[144,128]{1,0:T(8,128)(2,1)S(1)}, u32[]{:S(2)}, u32[]{:S(2)}) %collective-permute-start.35) | collective-permute-done | bytes 36896 | tf_op jit(solution)/shard_map/ppermute | solution.py:23
  52.2 0.5 collective-permute-done.38.refs_3_
  52.7 1.2 %collective-permute-start.33 = (bf16[144,128]{1,0:T(8,128)(2,1)S(1)}, bf16[144,128]{1,0:T(8,128)(2,1)S(1)}, u32[]{:S(2)}, u32[]{:S(2)}) collective-permute-start(bf16[144,128]{1,0:T(8,128)(2,1)S(1)} %collective-permute-done.32.refs_1_), channel_id=1, source_target_pairs={{0,2},{1,3},{2,0},{3,1},{4,6},{5,7},{6,4},{7,5},{8,10},{9,11},{10,... | collective-permute-start | bytes 110600 | tf_op jit(solution)/shard_map/ppermute | solution.py:23
  53.9 0.8 %collective-permute-start.36 = (bf16[144,128]{1,0:T(8,128)(2,1)S(1)}, bf16[144,128]{1,0:T(8,128)(2,1)S(1)}, u32[]{:S(2)}, u32[]{:S(2)}) collective-permute-start(bf16[144,128]{1,0:T(8,128)(2,1)S(1)} %collective-permute-done.35.refs_2_), channel_id=1, source_target_pairs={{0,2},{1,3},{2,0},{3,1},{4,6},{5,7},{6,4},{7,5},{8,10},{9,11},{10,... | collective-permute-start | bytes 110600 | tf_op jit(solution)/shard_map/ppermute | solution.py:23
  54.7 1.2 %collective-permute-start.39 = (bf16[144,128]{1,0:T(8,128)(2,1)S(1)}, bf16[144,128]{1,0:T(8,128)(2,1)S(1)}, u32[]{:S(2)}, u32[]{:S(2)}) collective-permute-start(bf16[144,128]{1,0:T(8,128)(2,1)S(1)} %collective-permute-done.38.refs_3_), channel_id=1, source_target_pairs={{0,2},{1,3},{2,0},{3,1},{4,6},{5,7},{6,4},{7,5},{8,10},{9,11},{10,... | collective-permute-start | bytes 110600 | tf_op jit(solution)/shard_map/ppermute | solution.py:23
  56.0 0.5 collective-permute-start.31
  56.5 0.6 collective-permute-done.33.refs_1_
  57.1 0.8 %collective-permute-done.36.refs_2_ = bf16[144,128]{1,0:T(8,128)(2,1)S(1)} collective-permute-done((bf16[144,128]{1,0:T(8,128)(2,1)S(1)}, bf16[144,128]{1,0:T(8,128)(2,1)S(1)}, u32[]{:S(2)}, u32[]{:S(2)}) %collective-permute-start.36) | collective-permute-done | bytes 36896 | tf_op jit(solution)/shard_map/ppermute | solution.py:23
  57.9 0.8 %collective-permute-done.39.refs_3_ = bf16[144,128]{1,0:T(8,128)(2,1)S(1)} collective-permute-done((bf16[144,128]{1,0:T(8,128)(2,1)S(1)}, bf16[144,128]{1,0:T(8,128)(2,1)S(1)}, u32[]{:S(2)}, u32[]{:S(2)}) %collective-permute-start.39) | collective-permute-done | bytes 36896 | tf_op jit(solution)/shard_map/ppermute | solution.py:23
  58.7 1.3 %precondition.1.query = bf16[512,64]{1,0:T(8,128)(2,1)S(1)} custom-call(f32[8,4096]{1,0:T(8,128)S(1)} %copy-done.4, f32[64,64]{1,0:T(8,128)S(1)} %copy-done.5, f32[64,64]{1,0:T(8,128)S(1)} %copy-done.6, f32[64,64]{1,0:T(8,128)S(1)} %copy-done.7), custom_call_target="tpu_custom_call" | custom-call | flops 10000000000 | bytes 131072 | tf_op jit(solution)/shard_map/precondition/pallas_call | solution.py:191
  61.4 1.0 %shard_map.99 = f32[8,128]{1,0:T(8,128)} custom-call(bf16[512,64]{1,0:T(8,128)(2,1)S(1)} %precondition.1.query, bf16[144,128]{1,0:T(8,128)(2,1)S(1)} %collective-permute-done.31.refs_0_, bf16[144,128]{1,0:T(8,128)(2,1)S(1)} %collective-permute-done.34.refs_1_, bf16[144,128]{1,0:T(8,128)(2,1)S(1)} %collective-permute-done.37.refs_2_, ...), custom_call_target="tpu_custom_call" | custom-call | flops 33554432 | bytes 147456 | tf_op jit(solution)/shard_map/pallas_call | solution.py:244
  (71 shorter events, 3.0 us)
Async XLA Ops:
  0.0 41.5 %copy-start.2 = (bf16[64,1792]{1,0:T(8,128)(2,1)S(1)}, bf16[64,1792]{1,0:T(8,128)(2,1)}, u32[]{:S(2)}) copy-start(bf16[64,1792]{1,0:T(8,128)(2,1)} %refs_0_.1) | copy-start | bytes 688132
  0.0 41.5 %copy-start = (bf16[128,28672]{1,0:T(8,128)(2,1)S(1)}, bf16[128,28672]{1,0:T(8,128)(2,1)}, u32[]{:S(2)}) copy-start(bf16[128,28672]{1,0:T(8,128)(2,1)} %grad.9) | copy-start | bytes 22020100
  0.0 41.5 %copy-start.1 = (bf16[128,8192]{1,0:T(8,128)(2,1)S(1)}, bf16[128,8192]{1,0:T(8,128)(2,1)}, u32[]{:S(2)}) copy-start(bf16[128,8192]{1,0:T(8,128)(2,1)} %act.9) | copy-start | bytes 6291460
  0.0 7.7 %collective-permute-start.10 = (bf16[64,512]{1,0:T(8,128)(2,1)}, bf16[64,512]{1,0:T(8,128)(2,1)S(1)}, u32[]{:S(2)}, u32[]{:S(2)}) collective-permute-start(bf16[64,512]{1,0:T(8,128)(2,1)} %refs_1_.1), channel_id=1, source_target_pairs={{0,4},{1,5},{2,6},{3,7},{4,0},{5,1},{6,2},{7,3},{8,12},{9,13},{10,... | collective-permute-start | bytes 196616 | tf_op jit(solution)/shard_map/ppermute | solution.py:106
  3.1 5.5 %collective-permute-start.23 = (bf16[64,512]{1,0:T(8,128)(2,1)}, bf16[64,512]{1,0:T(8,128)(2,1)S(1)}, u32[]{:S(2)}, u32[]{:S(2)}) collective-permute-start(bf16[64,512]{1,0:T(8,128)(2,1)} %refs_1_.1), channel_id=1, source_target_pairs={{0,2},{1,3},{2,0},{3,1},{4,6},{5,7},{6,4},{7,5},{8,10},{9,11},{10,... | collective-permute-start | bytes 196616 | tf_op jit(solution)/shard_map/ppermute | solution.py:106
  4.7 5.9 %collective-permute-start.29 = (bf16[64,512]{1,0:T(8,128)(2,1)}, bf16[64,512]{1,0:T(8,128)(2,1)S(1)}, u32[]{:S(2)}, u32[]{:S(2)}) collective-permute-start(bf16[64,512]{1,0:T(8,128)(2,1)} %refs_1_.1), channel_id=1, source_target_pairs={{0,1},{1,0},{2,3},{3,2},{4,5},{5,4},{6,7},{7,6},{8,9},{9,8},{10,11... | collective-permute-start | bytes 196616 | tf_op jit(solution)/shard_map/ppermute | solution.py:127
  4.7 7.0 %collective-permute-start.3 = (bf16[64,512]{1,0:T(8,128)(2,1)}, bf16[64,512]{1,0:T(8,128)(2,1)S(1)}, u32[]{:S(2)}, u32[]{:S(2)}) collective-permute-start(bf16[64,512]{1,0:T(8,128)(2,1)} %refs_1_.1), channel_id=1, source_target_pairs={{0,8},{1,9},{2,10},{3,11},{4,12},{5,13},{6,14},{7,15},{8,0},{9,1},... | collective-permute-start | bytes 196616 | tf_op jit(solution)/shard_map/ppermute | solution.py:106
  7.2 12.8 %collective-permute-start.8 = (bf16[64,1792]{1,0:T(8,128)(2,1)}, bf16[64,1792]{1,0:T(8,128)(2,1)S(1)}, u32[]{:S(2)}, u32[]{:S(2)}) collective-permute-start(bf16[64,1792]{1,0:T(8,128)(2,1)} %refs_0_.1), channel_id=1, source_target_pairs={{0,4},{1,5},{2,6},{3,7},{4,0},{5,1},{6,2},{7,3},{8,12},{9,13},{10,... | collective-permute-start | bytes 688136 | tf_op jit(solution)/shard_map/ppermute | solution.py:106
  7.7 13.7 %collective-permute-start = (bf16[64,1792]{1,0:T(8,128)(2,1)}, bf16[64,1792]{1,0:T(8,128)(2,1)S(1)}, u32[]{:S(2)}, u32[]{:S(2)}) collective-permute-start(bf16[64,1792]{1,0:T(8,128)(2,1)} %refs_0_.1), channel_id=1, source_target_pairs={{0,8},{1,9},{2,10},{3,11},{4,12},{5,13},{6,14},{7,15},{8,0},{9,1},... | collective-permute-start | bytes 688136 | tf_op jit(solution)/shard_map/ppermute | solution.py:106
  8.6 13.4 %collective-permute-start.22 = (bf16[64,1792]{1,0:T(8,128)(2,1)}, bf16[64,1792]{1,0:T(8,128)(2,1)S(1)}, u32[]{:S(2)}, u32[]{:S(2)}) collective-permute-start(bf16[64,1792]{1,0:T(8,128)(2,1)} %refs_0_.1), channel_id=1, source_target_pairs={{0,2},{1,3},{2,0},{3,1},{4,6},{5,7},{6,4},{7,5},{8,10},{9,11},{10,... | collective-permute-start | bytes 688136 | tf_op jit(solution)/shard_map/ppermute | solution.py:106
  10.5 1.3 %collective-permute-start.27 = (bf16[64,512]{1,0:T(8,128)(2,1)S(1)}, bf16[64,512]{1,0:T(8,128)(2,1)S(1)}, u32[]{:S(2)}, u32[]{:S(2)}) collective-permute-start(bf16[64,512]{1,0:T(8,128)(2,1)S(1)} %collective-permute-done.10.refs_5_), channel_id=1, source_target_pairs={{0,1},{1,0},{2,3},{3,2},{4,5},{5,4},{6,7},{7,6},{8,9},{9,8},{10,11... | collective-permute-start | bytes 196616 | tf_op jit(solution)/shard_map/ppermute | solution.py:127
  11.7 1.3 %collective-permute-start.25 = (bf16[64,512]{1,0:T(8,128)(2,1)S(1)}, bf16[64,512]{1,0:T(8,128)(2,1)S(1)}, u32[]{:S(2)}, u32[]{:S(2)}) collective-permute-start(bf16[64,512]{1,0:T(8,128)(2,1)S(1)} %collective-permute-done.23.refs_1_), channel_id=1, source_target_pairs={{0,1},{1,0},{2,3},{3,2},{4,5},{5,4},{6,7},{7,6},{8,9},{9,8},{10,11... | collective-permute-start | bytes 196616 | tf_op jit(solution)/shard_map/ppermute | solution.py:127
  11.8 5.1 %collective-permute-start.4 = (bf16[64,512]{1,0:T(8,128)(2,1)S(1)}, bf16[64,512]{1,0:T(8,128)(2,1)S(1)}, u32[]{:S(2)}, u32[]{:S(2)}) collective-permute-start(bf16[64,512]{1,0:T(8,128)(2,1)S(1)} %collective-permute-done.3.refs_1_), channel_id=1, source_target_pairs={{0,2},{1,3},{2,0},{3,1},{4,6},{5,7},{6,4},{7,5},{8,10},{9,11},{10,... | collective-permute-start | bytes 196616 | tf_op jit(solution)/shard_map/ppermute | solution.py:106
  13.0 4.3 %collective-permute-start.19 = (bf16[64,512]{1,0:T(8,128)(2,1)S(1)}, bf16[64,512]{1,0:T(8,128)(2,1)S(1)}, u32[]{:S(2)}, u32[]{:S(2)}) collective-permute-start(bf16[64,512]{1,0:T(8,128)(2,1)S(1)} %collective-permute-done.3.refs_1_), channel_id=1, source_target_pairs={{0,16},{16,0},{1,17},{17,1},{2,18},{18,2},{3,19},{19,3},{4,20},{20... | collective-permute-start | bytes 196616 | tf_op jit(solution)/shard_map/ppermute | solution.py:112
  16.8 1.3 %collective-permute-start.15 = (bf16[64,512]{1,0:T(8,128)(2,1)S(1)}, bf16[64,512]{1,0:T(8,128)(2,1)S(1)}, u32[]{:S(2)}, u32[]{:S(2)}) collective-permute-start(bf16[64,512]{1,0:T(8,128)(2,1)S(1)} %collective-permute-done.3.refs_1_), channel_id=1, source_target_pairs={{0,1},{1,0},{2,3},{3,2},{4,5},{5,4},{6,7},{7,6},{8,9},{9,8},{10,11... | collective-permute-start | bytes 196616 | tf_op jit(solution)/shard_map/ppermute | solution.py:127
  17.2 4.8 %collective-permute-start.11 = (bf16[64,512]{1,0:T(8,128)(2,1)S(1)}, bf16[64,512]{1,0:T(8,128)(2,1)S(1)}, u32[]{:S(2)}, u32[]{:S(2)}) collective-permute-start(bf16[64,512]{1,0:T(8,128)(2,1)S(1)} %collective-permute-done.10.refs_5_), channel_id=1, source_target_pairs={{0,2},{1,3},{2,0},{3,1},{4,6},{5,7},{6,4},{7,5},{8,10},{9,11},{10,... | collective-permute-start | bytes 196616 | tf_op jit(solution)/shard_map/ppermute | solution.py:106
  18.2 12.4 %collective-permute-start.28 = (bf16[64,1792]{1,0:T(8,128)(2,1)}, bf16[64,1792]{1,0:T(8,128)(2,1)S(1)}, u32[]{:S(2)}, u32[]{:S(2)}) collective-permute-start(bf16[64,1792]{1,0:T(8,128)(2,1)} %refs_0_.1), channel_id=1, source_target_pairs={{0,1},{1,0},{2,3},{3,2},{4,5},{5,4},{6,7},{7,6},{8,9},{9,8},{10,11... | collective-permute-start | bytes 688136 | tf_op jit(solution)/shard_map/ppermute | solution.py:127
  20.1 10.5 %collective-permute-start.26 = (bf16[64,1792]{1,0:T(8,128)(2,1)S(1)}, bf16[64,1792]{1,0:T(8,128)(2,1)S(1)}, u32[]{:S(2)}, u32[]{:S(2)}) collective-permute-start(bf16[64,1792]{1,0:T(8,128)(2,1)S(1)} %collective-permute-done.8.refs_4_), channel_id=1, source_target_pairs={{0,1},{1,0},{2,3},{3,2},{4,5},{5,4},{6,7},{7,6},{8,9},{9,8},{10,11... | collective-permute-start | bytes 688136 | tf_op jit(solution)/shard_map/ppermute | solution.py:127
  21.4 10.4 %collective-permute-start.1 = (bf16[64,1792]{1,0:T(8,128)(2,1)S(1)}, bf16[64,1792]{1,0:T(8,128)(2,1)S(1)}, u32[]{:S(2)}, u32[]{:S(2)}) collective-permute-start(bf16[64,1792]{1,0:T(8,128)(2,1)S(1)} %collective-permute-done.refs_0_), channel_id=1, source_target_pairs={{0,2},{1,3},{2,0},{3,1},{4,6},{5,7},{6,4},{7,5},{8,10},{9,11},{10,... | collective-permute-start | bytes 688136 | tf_op jit(solution)/shard_map/ppermute | solution.py:106
  22.0 10.0 %collective-permute-start.24 = (bf16[64,1792]{1,0:T(8,128)(2,1)S(1)}, bf16[64,1792]{1,0:T(8,128)(2,1)S(1)}, u32[]{:S(2)}, u32[]{:S(2)}) collective-permute-start(bf16[64,1792]{1,0:T(8,128)(2,1)S(1)} %collective-permute-done.22.refs_0_), channel_id=1, source_target_pairs={{0,1},{1,0},{2,3},{3,2},{4,5},{5,4},{6,7},{7,6},{8,9},{9,8},{10,11... | collective-permute-start | bytes 688136 | tf_op jit(solution)/shard_map/ppermute | solution.py:127
  22.0 1.6 %collective-permute-start.17 = (bf16[64,512]{1,0:T(8,128)(2,1)S(1)}, bf16[64,512]{1,0:T(8,128)(2,1)S(1)}, u32[]{:S(2)}, u32[]{:S(2)}) collective-permute-start(bf16[64,512]{1,0:T(8,128)(2,1)S(1)} %collective-permute-done.4.refs_5_), channel_id=1, source_target_pairs={{0,1},{1,0},{2,3},{3,2},{4,5},{5,4},{6,7},{7,6},{8,9},{9,8},{10,11... | collective-permute-start | bytes 196616 | tf_op jit(solution)/shard_map/ppermute | solution.py:127
  23.6 1.3 %collective-permute-start.21 = (bf16[64,512]{1,0:T(8,128)(2,1)S(1)}, bf16[64,512]{1,0:T(8,128)(2,1)S(1)}, u32[]{:S(2)}, u32[]{:S(2)}) collective-permute-start(bf16[64,512]{1,0:T(8,128)(2,1)S(1)} %collective-permute-done.19.refs_9_), channel_id=1, source_target_pairs={{0,1},{1,0},{2,3},{3,2},{4,5},{5,4},{6,7},{7,6},{8,9},{9,8},{10,11... | collective-permute-start | bytes 196616 | tf_op jit(solution)/shard_map/ppermute | solution.py:127
  24.8 4.3 %collective-permute-start.5 = (bf16[64,512]{1,0:T(8,128)(2,1)S(1)}, bf16[64,512]{1,0:T(8,128)(2,1)S(1)}, u32[]{:S(2)}, u32[]{:S(2)}) collective-permute-start(bf16[64,512]{1,0:T(8,128)(2,1)S(1)} %collective-permute-done.4.refs_5_), channel_id=1, source_target_pairs={{0,16},{16,0},{1,17},{17,1},{2,18},{18,2},{3,19},{19,3},{4,20},{20... | collective-permute-start | bytes 196616 | tf_op jit(solution)/shard_map/ppermute | solution.py:112
  29.1 7.8 %collective-permute-start.18 = (bf16[64,1792]{1,0:T(8,128)(2,1)S(1)}, bf16[64,1792]{1,0:T(8,128)(2,1)S(1)}, u32[]{:S(2)}, u32[]{:S(2)}) collective-permute-start(bf16[64,1792]{1,0:T(8,128)(2,1)S(1)} %collective-permute-done.refs_0_), channel_id=1, source_target_pairs={{0,16},{16,0},{1,17},{17,1},{2,18},{18,2},{3,19},{19,3},{4,20},{20... | collective-permute-start | bytes 688136 | tf_op jit(solution)/shard_map/ppermute | solution.py:112
  30.6 6.3 %collective-permute-start.14 = (bf16[64,1792]{1,0:T(8,128)(2,1)S(1)}, bf16[64,1792]{1,0:T(8,128)(2,1)S(1)}, u32[]{:S(2)}, u32[]{:S(2)}) collective-permute-start(bf16[64,1792]{1,0:T(8,128)(2,1)S(1)} %collective-permute-done.refs_0_), channel_id=1, source_target_pairs={{0,1},{1,0},{2,3},{3,2},{4,5},{5,4},{6,7},{7,6},{8,9},{9,8},{10,11... | collective-permute-start | bytes 688136 | tf_op jit(solution)/shard_map/ppermute | solution.py:127
  30.6 8.0 %collective-permute-start.9 = (bf16[64,1792]{1,0:T(8,128)(2,1)S(1)}, bf16[64,1792]{1,0:T(8,128)(2,1)S(1)}, u32[]{:S(2)}, u32[]{:S(2)}) collective-permute-start(bf16[64,1792]{1,0:T(8,128)(2,1)S(1)} %collective-permute-done.8.refs_4_), channel_id=1, source_target_pairs={{0,2},{1,3},{2,0},{3,1},{4,6},{5,7},{6,4},{7,5},{8,10},{9,11},{10,... | collective-permute-start | bytes 688136 | tf_op jit(solution)/shard_map/ppermute | solution.py:106
  31.8 6.8 %collective-permute-start.16 = (bf16[64,1792]{1,0:T(8,128)(2,1)S(1)}, bf16[64,1792]{1,0:T(8,128)(2,1)S(1)}, u32[]{:S(2)}, u32[]{:S(2)}) collective-permute-start(bf16[64,1792]{1,0:T(8,128)(2,1)S(1)} %collective-permute-done.1.refs_4_), channel_id=1, source_target_pairs={{0,1},{1,0},{2,3},{3,2},{4,5},{5,4},{6,7},{7,6},{8,9},{9,8},{10,11... | collective-permute-start | bytes 688136 | tf_op jit(solution)/shard_map/ppermute | solution.py:127
  32.0 8.8 %collective-permute-start.2 = (bf16[64,1792]{1,0:T(8,128)(2,1)S(1)}, bf16[64,1792]{1,0:T(8,128)(2,1)S(1)}, u32[]{:S(2)}, u32[]{:S(2)}) collective-permute-start(bf16[64,1792]{1,0:T(8,128)(2,1)S(1)} %collective-permute-done.1.refs_4_), channel_id=1, source_target_pairs={{0,16},{16,0},{1,17},{17,1},{2,18},{18,2},{3,19},{19,3},{4,20},{20... | collective-permute-start | bytes 688136 | tf_op jit(solution)/shard_map/ppermute | solution.py:112
  36.9 7.2 %collective-permute-start.13 = (bf16[64,512]{1,0:T(8,128)(2,1)S(1)}, bf16[64,512]{1,0:T(8,128)(2,1)S(1)}, u32[]{:S(2)}, u32[]{:S(2)}) collective-permute-start(bf16[64,512]{1,0:T(8,128)(2,1)S(1)} %collective-permute-done.11.refs_1_), channel_id=1, source_target_pairs={{0,1},{1,0},{2,3},{3,2},{4,5},{5,4},{6,7},{7,6},{8,9},{9,8},{10,11... | collective-permute-start | bytes 196616 | tf_op jit(solution)/shard_map/ppermute | solution.py:127
  36.9 7.7 %collective-permute-start.7 = (bf16[64,512]{1,0:T(8,128)(2,1)S(1)}, bf16[64,512]{1,0:T(8,128)(2,1)S(1)}, u32[]{:S(2)}, u32[]{:S(2)}) collective-permute-start(bf16[64,512]{1,0:T(8,128)(2,1)S(1)} %collective-permute-done.5.refs_1_), channel_id=1, source_target_pairs={{0,1},{1,0},{2,3},{3,2},{4,5},{5,4},{6,7},{7,6},{8,9},{9,8},{10,11... | collective-permute-start | bytes 196616 | tf_op jit(solution)/shard_map/ppermute | solution.py:127
  38.6 4.3 %collective-permute-start.20 = (bf16[64,1792]{1,0:T(8,128)(2,1)S(1)}, bf16[64,1792]{1,0:T(8,128)(2,1)S(1)}, u32[]{:S(2)}, u32[]{:S(2)}) collective-permute-start(bf16[64,1792]{1,0:T(8,128)(2,1)S(1)} %collective-permute-done.18.refs_8_), channel_id=1, source_target_pairs={{0,1},{1,0},{2,3},{3,2},{4,5},{5,4},{6,7},{7,6},{8,9},{9,8},{10,11... | collective-permute-start | bytes 688136 | tf_op jit(solution)/shard_map/ppermute | solution.py:127
  38.6 5.5 %collective-permute-start.12 = (bf16[64,1792]{1,0:T(8,128)(2,1)S(1)}, bf16[64,1792]{1,0:T(8,128)(2,1)S(1)}, u32[]{:S(2)}, u32[]{:S(2)}) collective-permute-start(bf16[64,1792]{1,0:T(8,128)(2,1)S(1)} %collective-permute-done.9.refs_0_), channel_id=1, source_target_pairs={{0,1},{1,0},{2,3},{3,2},{4,5},{5,4},{6,7},{7,6},{8,9},{9,8},{10,11... | collective-permute-start | bytes 688136 | tf_op jit(solution)/shard_map/ppermute | solution.py:127
  40.8 3.8 %collective-permute-start.6 = (bf16[64,1792]{1,0:T(8,128)(2,1)S(1)}, bf16[64,1792]{1,0:T(8,128)(2,1)S(1)}, u32[]{:S(2)}, u32[]{:S(2)}) collective-permute-start(bf16[64,1792]{1,0:T(8,128)(2,1)S(1)} %collective-permute-done.2.refs_0_), channel_id=1, source_target_pairs={{0,1},{1,0},{2,3},{3,2},{4,5},{5,4},{6,7},{7,6},{8,9},{9,8},{10,11... | collective-permute-start | bytes 688136 | tf_op jit(solution)/shard_map/ppermute | solution.py:127
  45.2 6.2 %collective-permute-start.32 = (bf16[144,128]{1,0:T(8,128)(2,1)S(1)}, bf16[144,128]{1,0:T(8,128)(2,1)S(1)}, u32[]{:S(2)}, u32[]{:S(2)}) collective-permute-start(bf16[144,128]{1,0:T(8,128)(2,1)S(1)} %shard_map.95.refs_0_), channel_id=1, source_target_pairs={{0,12},{1,13},{2,14},{3,15},{4,8},{5,9},{6,10},{7,11},{8,4},{9,5},... | collective-permute-start | bytes 110600 | tf_op jit(solution)/shard_map/ppermute | solution.py:23
  47.8 4.4 %collective-permute-start.35 = (bf16[144,128]{1,0:T(8,128)(2,1)S(1)}, bf16[144,128]{1,0:T(8,128)(2,1)S(1)}, u32[]{:S(2)}, u32[]{:S(2)}) collective-permute-start(bf16[144,128]{1,0:T(8,128)(2,1)S(1)} %shard_map.95.refs_0_), channel_id=1, source_target_pairs={{0,4},{1,5},{2,6},{3,7},{4,0},{5,1},{6,2},{7,3},{8,12},{9,13},{10,... | collective-permute-start | bytes 110600 | tf_op jit(solution)/shard_map/ppermute | solution.py:23
  47.9 4.9 %collective-permute-start.38 = (bf16[144,128]{1,0:T(8,128)(2,1)S(1)}, bf16[144,128]{1,0:T(8,128)(2,1)S(1)}, u32[]{:S(2)}, u32[]{:S(2)}) collective-permute-start(bf16[144,128]{1,0:T(8,128)(2,1)S(1)} %shard_map.95.refs_0_), channel_id=1, source_target_pairs={{0,8},{1,9},{2,10},{3,11},{4,12},{5,13},{6,14},{7,15},{8,0},{9,1},... | collective-permute-start | bytes 110600 | tf_op jit(solution)/shard_map/ppermute | solution.py:23
  49.6 4.3 %collective-permute-start.41 = (bf16[144,128]{1,0:T(8,128)(2,1)S(1)}, bf16[144,128]{1,0:T(8,128)(2,1)S(1)}, u32[]{:S(2)}, u32[]{:S(2)}) collective-permute-start(bf16[144,128]{1,0:T(8,128)(2,1)S(1)} %shard_map.95.refs_0_), channel_id=1, source_target_pairs={{0,1},{1,0},{2,3},{3,2},{4,5},{5,4},{6,7},{7,6},{8,9},{9,8},{10,11... | collective-permute-start | bytes 110600 | tf_op jit(solution)/shard_map/ppermute | solution.py:23
  49.6 5.1 %collective-permute-start.30 = (bf16[144,128]{1,0:T(8,128)(2,1)S(1)}, bf16[144,128]{1,0:T(8,128)(2,1)S(1)}, u32[]{:S(2)}, u32[]{:S(2)}) collective-permute-start(bf16[144,128]{1,0:T(8,128)(2,1)S(1)} %shard_map.95.refs_0_), channel_id=1, source_target_pairs={{0,2},{1,3},{2,0},{3,1},{4,6},{5,7},{6,4},{7,5},{8,10},{9,11},{10,... | collective-permute-start | bytes 110600 | tf_op jit(solution)/shard_map/ppermute | solution.py:23
  51.4 4.6 %collective-permute-start.42 = (bf16[144,128]{1,0:T(8,128)(2,1)S(1)}, bf16[144,128]{1,0:T(8,128)(2,1)S(1)}, u32[]{:S(2)}, u32[]{:S(2)}) collective-permute-start(bf16[144,128]{1,0:T(8,128)(2,1)S(1)} %collective-permute-done.32.refs_1_), channel_id=1, source_target_pairs={{0,1},{1,0},{2,3},{3,2},{4,5},{5,4},{6,7},{7,6},{8,9},{9,8},{10,11... | collective-permute-start | bytes 110600 | tf_op jit(solution)/shard_map/ppermute | solution.py:23
  52.2 3.8 %collective-permute-start.43 = (bf16[144,128]{1,0:T(8,128)(2,1)S(1)}, bf16[144,128]{1,0:T(8,128)(2,1)S(1)}, u32[]{:S(2)}, u32[]{:S(2)}) collective-permute-start(bf16[144,128]{1,0:T(8,128)(2,1)S(1)} %collective-permute-done.35.refs_2_), channel_id=1, source_target_pairs={{0,1},{1,0},{2,3},{3,2},{4,5},{5,4},{6,7},{7,6},{8,9},{9,8},{10,11... | collective-permute-start | bytes 110600 | tf_op jit(solution)/shard_map/ppermute | solution.py:23
  52.7 4.4 %collective-permute-start.33 = (bf16[144,128]{1,0:T(8,128)(2,1)S(1)}, bf16[144,128]{1,0:T(8,128)(2,1)S(1)}, u32[]{:S(2)}, u32[]{:S(2)}) collective-permute-start(bf16[144,128]{1,0:T(8,128)(2,1)S(1)} %collective-permute-done.32.refs_1_), channel_id=1, source_target_pairs={{0,2},{1,3},{2,0},{3,1},{4,6},{5,7},{6,4},{7,5},{8,10},{9,11},{10,... | collective-permute-start | bytes 110600 | tf_op jit(solution)/shard_map/ppermute | solution.py:23
  53.9 4.0 %collective-permute-start.36 = (bf16[144,128]{1,0:T(8,128)(2,1)S(1)}, bf16[144,128]{1,0:T(8,128)(2,1)S(1)}, u32[]{:S(2)}, u32[]{:S(2)}) collective-permute-start(bf16[144,128]{1,0:T(8,128)(2,1)S(1)} %collective-permute-done.35.refs_2_), channel_id=1, source_target_pairs={{0,2},{1,3},{2,0},{3,1},{4,6},{5,7},{6,4},{7,5},{8,10},{9,11},{10,... | collective-permute-start | bytes 110600 | tf_op jit(solution)/shard_map/ppermute | solution.py:23
  54.7 4.0 %collective-permute-start.39 = (bf16[144,128]{1,0:T(8,128)(2,1)S(1)}, bf16[144,128]{1,0:T(8,128)(2,1)S(1)}, u32[]{:S(2)}, u32[]{:S(2)}) collective-permute-start(bf16[144,128]{1,0:T(8,128)(2,1)S(1)} %collective-permute-done.38.refs_3_), channel_id=1, source_target_pairs={{0,2},{1,3},{2,0},{3,1},{4,6},{5,7},{6,4},{7,5},{8,10},{9,11},{10,... | collective-permute-start | bytes 110600 | tf_op jit(solution)/shard_map/ppermute | solution.py:23
  56.0 4.5 %collective-permute-start.44 = (bf16[144,128]{1,0:T(8,128)(2,1)S(1)}, bf16[144,128]{1,0:T(8,128)(2,1)S(1)}, u32[]{:S(2)}, u32[]{:S(2)}) collective-permute-start(bf16[144,128]{1,0:T(8,128)(2,1)S(1)} %collective-permute-done.38.refs_3_), channel_id=1, source_target_pairs={{0,1},{1,0},{2,3},{3,2},{4,5},{5,4},{6,7},{7,6},{8,9},{9,8},{10,11... | collective-permute-start | bytes 110600 | tf_op jit(solution)/shard_map/ppermute | solution.py:23
  56.0 5.3 %collective-permute-start.31 = (bf16[144,128]{1,0:T(8,128)(2,1)S(1)}, bf16[144,128]{1,0:T(8,128)(2,1)S(1)}, u32[]{:S(2)}, u32[]{:S(2)}) collective-permute-start(bf16[144,128]{1,0:T(8,128)(2,1)S(1)} %collective-permute-done.30.refs_0_), channel_id=1, source_target_pairs={{0,1},{1,0},{2,3},{3,2},{4,5},{5,4},{6,7},{7,6},{8,9},{9,8},{10,11... | collective-permute-start | bytes 110600 | tf_op jit(solution)/shard_map/ppermute | solution.py:23
  57.1 4.3 %collective-permute-start.34 = (bf16[144,128]{1,0:T(8,128)(2,1)S(1)}, bf16[144,128]{1,0:T(8,128)(2,1)S(1)}, u32[]{:S(2)}, u32[]{:S(2)}) collective-permute-start(bf16[144,128]{1,0:T(8,128)(2,1)S(1)} %collective-permute-done.33.refs_1_), channel_id=1, source_target_pairs={{0,1},{1,0},{2,3},{3,2},{4,5},{5,4},{6,7},{7,6},{8,9},{9,8},{10,11... | collective-permute-start | bytes 110600 | tf_op jit(solution)/shard_map/ppermute | solution.py:23
  57.9 3.5 %collective-permute-start.37 = (bf16[144,128]{1,0:T(8,128)(2,1)S(1)}, bf16[144,128]{1,0:T(8,128)(2,1)S(1)}, u32[]{:S(2)}, u32[]{:S(2)}) collective-permute-start(bf16[144,128]{1,0:T(8,128)(2,1)S(1)} %collective-permute-done.36.refs_2_), channel_id=1, source_target_pairs={{0,1},{1,0},{2,3},{3,2},{4,5},{5,4},{6,7},{7,6},{8,9},{9,8},{10,11... | collective-permute-start | bytes 110600 | tf_op jit(solution)/shard_map/ppermute | solution.py:23
  58.7 2.7 %collective-permute-start.40 = (bf16[144,128]{1,0:T(8,128)(2,1)S(1)}, bf16[144,128]{1,0:T(8,128)(2,1)S(1)}, u32[]{:S(2)}, u32[]{:S(2)}) collective-permute-start(bf16[144,128]{1,0:T(8,128)(2,1)S(1)} %collective-permute-done.39.refs_3_), channel_id=1, source_target_pairs={{0,1},{1,0},{2,3},{3,2},{4,5},{5,4},{6,7},{7,6},{8,9},{9,8},{10,11... | collective-permute-start | bytes 110600 | tf_op jit(solution)/shard_map/ppermute | solution.py:23
  (6 other events, 98.7 us)

commit v3 on v2

--- a/solution.py
+++ b/solution.py
@@ -35,7 +35,7 @@
 def numbers_of(ids):
     return pl.pallas_call(
         numbers_kernel,
-        out_shape=jax.ShapeDtypeStruct((16, ids.shape[1]), jnp.bfloat16),
+        out_shape=jax.ShapeDtypeStruct((8, ids.shape[1]), jnp.bfloat16),
         in_specs=[VMEM],
         out_specs=VMEM,
         cost_estimate=pl.CostEstimate(flops=2 * 10**10, bytes_accessed=0, transcendentals=0),
@@ -78,7 +78,7 @@
     if numbers is None:
         shape = jax.ShapeDtypeStruct((tokens, 2 * rank), jnp.float32)
     else:
-        shape = jax.ShapeDtypeStruct((2 * rank + 16, tokens), jnp.bfloat16)
+        shape = jax.ShapeDtypeStruct((2 * rank + 8, tokens), jnp.bfloat16)
     size = sum(piece.size for piece in pieces)
     return pl.pallas_call(
         functools.partial(project_kernel, tuple(keys), part is not None, numbers is not None),
@@ -153,7 +153,7 @@
         for i, (rows, part, width) in enumerate(((act, piece[:, :w_in], w_in), (grad, piece[:, w_in:], w_out))):
             cols = lax.dynamic_slice_in_dim(rows, src * width, width, axis=1)
             sums[i] = sums[i] + lax.dot_general(part, cols, NT, preferred_element_type=jnp.float32)
-    numbers = jnp.broadcast_to(ids, (16, ids.shape[1]))
+    numbers = jnp.broadcast_to(ids, (8, ids.shape[1]))
     return jnp.concatenate([s.astype(jnp.bfloat16) for s in (*sums, numbers)], axis=0)
 
 

time: 62.6 us -> 62.5 us (level)
  no operation moved by 1% of the time
where the time goes in v3:
time: 62.5 us; the launch traced here: 62.4 us
  starting transfers between devices  30.8 us (49%)
  waiting for transfers between devices  23.6 us (38%)
  Pallas kernels  7.12 us (11%)
  local copies, waits for them, and re-layouts  0.7 us (1%)
    ppermute x10, starting transfers between devices, bring(): held[*to, kind] = lax.ppermute(held[*source, kind], ('dom', 'shard'), pairs)  13.9 us
    ppermute x15, starting transfers between devices, moved(): return lax.ppermute(value, 'shard', [(i, i ^ offset) for i in range(n)])  9.44 us
    ppermute x4, waiting for transfers between devices, cross(): held[*to, kind] = lax.ppermute(held[*source, kind], 'dom', [(0, 1), (1, 0)])  8.92 us
    ppermute x10, waiting for transfers between devices, bring(): held[*to, kind] = lax.ppermute(held[*source, kind], ('dom', 'shard'), pairs)  7.8 us
    ppermute x4, starting transfers between devices, cross(): held[*to, kind] = lax.ppermute(held[*source, kind], 'dom', [(0, 1), (1, 0)])  5.29 us
    ppermute x15, waiting for transfers between devices, moved(): return lax.ppermute(value, 'shard', [(i, i ^ offset) for i in range(n)])  4.09 us
    pallas_call x5, Pallas kernels, project(): pl.pallas_call(functools.partial(project_kernel, tuple(keys), part is not...  3.5 us
    ppermute x16, waiting for transfers between devices, project_paired(): lax.ppermute(held[key], 'shard', [(i, i ^ 1) for i in range(n)])  2.75 us
  transfers between devices with their start and end apart: 45, of which 19 were waited for; matrix products, arithmetic and copies ran while one was open for 0% of the time, Pallas kernels for 9%

profile of v3, /device:TPU:0, one launch (start us, length us, event | category | flops | bytes accessed | tf_op | source)
XLA Modules:
  0.0 62.4 jit_solution(3351580055725300842)
XLA Ops:
  0.0 3.1 %collective-permute-start.10 = (bf16[64,512]{1,0:T(8,128)(2,1)}, bf16[64,512]{1,0:T(8,128)(2,1)S(1)}, u32[]{:S(2)}, u32[]{:S(2)}) collective-permute-start(bf16[64,512]{1,0:T(8,128)(2,1)} %refs_1_.1), channel_id=1, source_target_pairs={{0,4},{1,5},{2,6},{3,7},{4,0},{5,1},{6,2},{7,3},{8,12},{9,13},{10,... | collective-permute-start | bytes 196616 | tf_op jit(solution)/shard_map/ppermute | solution.py:106
  3.1 1.5 %collective-permute-start.23 = (bf16[64,512]{1,0:T(8,128)(2,1)}, bf16[64,512]{1,0:T(8,128)(2,1)S(1)}, u32[]{:S(2)}, u32[]{:S(2)}) collective-permute-start(bf16[64,512]{1,0:T(8,128)(2,1)} %refs_1_.1), channel_id=1, source_target_pairs={{0,2},{1,3},{2,0},{3,1},{4,6},{5,7},{6,4},{7,5},{8,10},{9,11},{10,... | collective-permute-start | bytes 196616 | tf_op jit(solution)/shard_map/ppermute | solution.py:106
  4.7 2.6 %collective-permute-start.3 = (bf16[64,512]{1,0:T(8,128)(2,1)}, bf16[64,512]{1,0:T(8,128)(2,1)S(1)}, u32[]{:S(2)}, u32[]{:S(2)}) collective-permute-start(bf16[64,512]{1,0:T(8,128)(2,1)} %refs_1_.1), channel_id=1, source_target_pairs={{0,8},{1,9},{2,10},{3,11},{4,12},{5,13},{6,14},{7,15},{8,0},{9,1},... | collective-permute-start | bytes 196616 | tf_op jit(solution)/shard_map/ppermute | solution.py:106
  7.7 0.9 %collective-permute-start = (bf16[64,1792]{1,0:T(8,128)(2,1)}, bf16[64,1792]{1,0:T(8,128)(2,1)S(1)}, u32[]{:S(2)}, u32[]{:S(2)}) collective-permute-start(bf16[64,1792]{1,0:T(8,128)(2,1)} %refs_0_.1), channel_id=1, source_target_pairs={{0,8},{1,9},{2,10},{3,11},{4,12},{5,13},{6,14},{7,15},{8,0},{9,1},... | collective-permute-start | bytes 688136 | tf_op jit(solution)/shard_map/ppermute | solution.py:106
  8.6 1.9 %collective-permute-start.22 = (bf16[64,1792]{1,0:T(8,128)(2,1)}, bf16[64,1792]{1,0:T(8,128)(2,1)S(1)}, u32[]{:S(2)}, u32[]{:S(2)}) collective-permute-start(bf16[64,1792]{1,0:T(8,128)(2,1)} %refs_0_.1), channel_id=1, source_target_pairs={{0,2},{1,3},{2,0},{3,1},{4,6},{5,7},{6,4},{7,5},{8,10},{9,11},{10,... | collective-permute-start | bytes 688136 | tf_op jit(solution)/shard_map/ppermute | solution.py:106
  10.5 1.2 %collective-permute-done.3.refs_1_ = bf16[64,512]{1,0:T(8,128)(2,1)S(1)} collective-permute-done((bf16[64,512]{1,0:T(8,128)(2,1)}, bf16[64,512]{1,0:T(8,128)(2,1)S(1)}, u32[]{:S(2)}, u32[]{:S(2)}) %collective-permute-start.3) | collective-permute-done | bytes 65568 | tf_op jit(solution)/shard_map/ppermute | solution.py:106
  11.8 0.7 %collective-permute-start.4 = (bf16[64,512]{1,0:T(8,128)(2,1)S(1)}, bf16[64,512]{1,0:T(8,128)(2,1)S(1)}, u32[]{:S(2)}, u32[]{:S(2)}) collective-permute-start(bf16[64,512]{1,0:T(8,128)(2,1)S(1)} %collective-permute-done.3.refs_1_), channel_id=1, source_target_pairs={{0,2},{1,3},{2,0},{3,1},{4,6},{5,7},{6,4},{7,5},{8,10},{9,11},{10,... | collective-permute-start | bytes 196616 | tf_op jit(solution)/shard_map/ppermute | solution.py:106
  12.4 0.5 collective-permute-done.25.refs_3_
  13.0 1.5 %collective-permute-start.19 = (bf16[64,512]{1,0:T(8,128)(2,1)S(1)}, bf16[64,512]{1,0:T(8,128)(2,1)S(1)}, u32[]{:S(2)}, u32[]{:S(2)}) collective-permute-start(bf16[64,512]{1,0:T(8,128)(2,1)S(1)} %collective-permute-done.3.refs_1_), channel_id=1, source_target_pairs={{0,16},{16,0},{1,17},{17,1},{2,18},{18,2},{3,19},{19,3},{4,20},{20... | collective-permute-start | bytes 196616 | tf_op jit(solution)/shard_map/ppermute | solution.py:112
  14.4 2.4 %collective-permute-done.4.refs_5_ = bf16[64,512]{1,0:T(8,128)(2,1)S(1)} collective-permute-done((bf16[64,512]{1,0:T(8,128)(2,1)S(1)}, bf16[64,512]{1,0:T(8,128)(2,1)S(1)}, u32[]{:S(2)}, u32[]{:S(2)}) %collective-permute-start.4) | collective-permute-done | bytes 65568 | tf_op jit(solution)/shard_map/ppermute | solution.py:106
  17.2 1.0 %collective-permute-start.11 = (bf16[64,512]{1,0:T(8,128)(2,1)S(1)}, bf16[64,512]{1,0:T(8,128)(2,1)S(1)}, u32[]{:S(2)}, u32[]{:S(2)}) collective-permute-start(bf16[64,512]{1,0:T(8,128)(2,1)S(1)} %collective-permute-done.10.refs_5_), channel_id=1, source_target_pairs={{0,2},{1,3},{2,0},{3,1},{4,6},{5,7},{6,4},{7,5},{8,10},{9,11},{10,... | collective-permute-start | bytes 196616 | tf_op jit(solution)/shard_map/ppermute | solution.py:106
  18.4 1.7 %collective-permute-done.8.refs_4_ = bf16[64,1792]{1,0:T(8,128)(2,1)S(1)} collective-permute-done((bf16[64,1792]{1,0:T(8,128)(2,1)}, bf16[64,1792]{1,0:T(8,128)(2,1)S(1)}, u32[]{:S(2)}, u32[]{:S(2)}) %collective-permute-start.8) | collective-permute-done | bytes 229408 | tf_op jit(solution)/shard_map/ppermute | solution.py:106
  20.1 1.3 %collective-permute-done.refs_0_ = bf16[64,1792]{1,0:T(8,128)(2,1)S(1)} collective-permute-done((bf16[64,1792]{1,0:T(8,128)(2,1)}, bf16[64,1792]{1,0:T(8,128)(2,1)S(1)}, u32[]{:S(2)}, u32[]{:S(2)}) %collective-permute-start) | collective-permute-done | bytes 229408 | tf_op jit(solution)/shard_map/ppermute | solution.py:106
  21.4 0.5 collective-permute-start.1
  22.0 0.5 collective-permute-start.17
  22.5 1.1 %collective-permute-done.17.refs_7_ = bf16[64,512]{1,0:T(8,128)(2,1)S(1)} collective-permute-done((bf16[64,512]{1,0:T(8,128)(2,1)S(1)}, bf16[64,512]{1,0:T(8,128)(2,1)S(1)}, u32[]{:S(2)}, u32[]{:S(2)}) %collective-permute-start.17) | collective-permute-done | bytes 65568 | tf_op jit(solution)/shard_map/ppermute | solution.py:127
  23.8 1.1 %collective-permute-done.21.refs_11_ = bf16[64,512]{1,0:T(8,128)(2,1)S(1)} collective-permute-done((bf16[64,512]{1,0:T(8,128)(2,1)S(1)}, bf16[64,512]{1,0:T(8,128)(2,1)S(1)}, u32[]{:S(2)}, u32[]{:S(2)}) %collective-permute-start.21) | collective-permute-done | bytes 65568 | tf_op jit(solution)/shard_map/ppermute | solution.py:127
  24.8 1.5 %collective-permute-start.5 = (bf16[64,512]{1,0:T(8,128)(2,1)S(1)}, bf16[64,512]{1,0:T(8,128)(2,1)S(1)}, u32[]{:S(2)}, u32[]{:S(2)}) collective-permute-start(bf16[64,512]{1,0:T(8,128)(2,1)S(1)} %collective-permute-done.4.refs_5_), channel_id=1, source_target_pairs={{0,16},{16,0},{1,17},{17,1},{2,18},{18,2},{3,19},{19,3},{4,20},{20... | collective-permute-start | bytes 196616 | tf_op jit(solution)/shard_map/ppermute | solution.py:112
  26.3 2.8 %collective-permute-done.5.refs_1_ = bf16[64,512]{1,0:T(8,128)(2,1)S(1)} collective-permute-done((bf16[64,512]{1,0:T(8,128)(2,1)S(1)}, bf16[64,512]{1,0:T(8,128)(2,1)S(1)}, u32[]{:S(2)}, u32[]{:S(2)}) %collective-permute-start.5) | collective-permute-done | bytes 65568 | tf_op jit(solution)/shard_map/ppermute | solution.py:112
  29.1 1.5 %collective-permute-start.18 = (bf16[64,1792]{1,0:T(8,128)(2,1)S(1)}, bf16[64,1792]{1,0:T(8,128)(2,1)S(1)}, u32[]{:S(2)}, u32[]{:S(2)}) collective-permute-start(bf16[64,1792]{1,0:T(8,128)(2,1)S(1)} %collective-permute-done.refs_0_), channel_id=1, source_target_pairs={{0,16},{16,0},{1,17},{17,1},{2,18},{18,2},{3,19},{19,3},{4,20},{20... | collective-permute-start | bytes 688136 | tf_op jit(solution)/shard_map/ppermute | solution.py:112
  30.6 1.2 %collective-permute-start.9 = (bf16[64,1792]{1,0:T(8,128)(2,1)S(1)}, bf16[64,1792]{1,0:T(8,128)(2,1)S(1)}, u32[]{:S(2)}, u32[]{:S(2)}) collective-permute-start(bf16[64,1792]{1,0:T(8,128)(2,1)S(1)} %collective-permute-done.8.refs_4_), channel_id=1, source_target_pairs={{0,2},{1,3},{2,0},{3,1},{4,6},{5,7},{6,4},{7,5},{8,10},{9,11},{10,... | collective-permute-start | bytes 688136 | tf_op jit(solution)/shard_map/ppermute | solution.py:106
  32.0 0.9 %collective-permute-start.2 = (bf16[64,1792]{1,0:T(8,128)(2,1)S(1)}, bf16[64,1792]{1,0:T(8,128)(2,1)S(1)}, u32[]{:S(2)}, u32[]{:S(2)}) collective-permute-start(bf16[64,1792]{1,0:T(8,128)(2,1)S(1)} %collective-permute-done.1.refs_4_), channel_id=1, source_target_pairs={{0,16},{16,0},{1,17},{17,1},{2,18},{18,2},{3,19},{19,3},{4,20},{20... | collective-permute-start | bytes 688136 | tf_op jit(solution)/shard_map/ppermute | solution.py:112
  32.8 4.1 %collective-permute-done.18.refs_8_ = bf16[64,1792]{1,0:T(8,128)(2,1)S(1)} collective-permute-done((bf16[64,1792]{1,0:T(8,128)(2,1)S(1)}, bf16[64,1792]{1,0:T(8,128)(2,1)S(1)}, u32[]{:S(2)}, u32[]{:S(2)}) %collective-permute-start.18) | collective-permute-done | bytes 229408 | tf_op jit(solution)/shard_map/ppermute | solution.py:112
  36.9 0.5 collective-permute-start.7
  37.4 1.2 %collective-permute-done.9.refs_0_ = bf16[64,1792]{1,0:T(8,128)(2,1)S(1)} collective-permute-done((bf16[64,1792]{1,0:T(8,128)(2,1)S(1)}, bf16[64,1792]{1,0:T(8,128)(2,1)S(1)}, u32[]{:S(2)}, u32[]{:S(2)}) %collective-permute-start.9) | collective-permute-done | bytes 229408 | tf_op jit(solution)/shard_map/ppermute | solution.py:106
  38.6 0.5 collective-permute-start.12
  39.1 1.7 %collective-permute-done.2.refs_0_ = bf16[64,1792]{1,0:T(8,128)(2,1)S(1)} collective-permute-done((bf16[64,1792]{1,0:T(8,128)(2,1)S(1)}, bf16[64,1792]{1,0:T(8,128)(2,1)S(1)}, u32[]{:S(2)}, u32[]{:S(2)}) %collective-permute-start.2) | collective-permute-done | bytes 229408 | tf_op jit(solution)/shard_map/ppermute | solution.py:112
  40.8 0.7 %copy-done.8 = s32[1,128]{1,0:T(1,128)S(1)} copy-done((s32[1,128]{1,0:T(1,128)S(1)}, s32[1,128]{1,0:T(1,128)}, u32[]{:S(2)}) %copy-start.8) | copy-done | bytes 536
  41.5 0.5 shard_map.91.refs_8_
  42.0 0.8 %shard_map.92.refs_12_ = f32[128,128]{1,0:T(8,128)S(1)} custom-call(bf16[128,8192]{1,0:T(8,128)(2,1)S(1)} %copy-done.1, bf16[128,28672]{1,0:T(8,128)(2,1)S(1)} %copy-done, bf16[64,1792]{1,0:T(8,128)(2,1)S(1)} %collective-permute-done.22.refs_0_, bf16[64,512]{1,0:T(8,128)(2,1)S(1)} %collective-permute-done.23.refs_1_, ...), custom_call_target="tpu_custom_call" | custom-call | flops 150994944 | bytes 2359296 | tf_op jit(solution)/shard_map/pallas_call | solution.py:83
  42.9 1.2 %shard_map.93.refs_4_ = f32[128,128]{1,0:T(8,128)S(1)} custom-call(bf16[128,8192]{1,0:T(8,128)(2,1)S(1)} %copy-done.1, bf16[128,28672]{1,0:T(8,128)(2,1)S(1)} %copy-done, bf16[64,1792]{1,0:T(8,128)(2,1)S(1)} %collective-permute-done.refs_0_, bf16[64,512]{1,0:T(8,128)(2,1)S(1)} %collective-permute-done.3.refs_1_, ...), custom_call_target="tpu_custom_call" | custom-call | flops 226492416 | bytes 3538944 | tf_op jit(solution)/shard_map/pallas_call | solution.py:83
  44.1 0.5 shard_map.94.refs_4_
  44.6 0.5 shard_map.95.refs_0_
  45.2 2.7 %collective-permute-start.32 = (bf16[136,128]{1,0:T(8,128)(2,1)S(1)}, bf16[136,128]{1,0:T(8,128)(2,1)S(1)}, u32[]{:S(2)}, u32[]{:S(2)}) collective-permute-start(bf16[136,128]{1,0:T(8,128)(2,1)S(1)} %shard_map.95.refs_0_), channel_id=1, source_target_pairs={{0,12},{1,13},{2,14},{3,15},{4,8},{5,9},{6,10},{7,11},{8,4},{9,5},... | collective-permute-start | bytes 104456 | tf_op jit(solution)/shard_map/ppermute | solution.py:23
  47.9 1.8 %collective-permute-start.38 = (bf16[136,128]{1,0:T(8,128)(2,1)S(1)}, bf16[136,128]{1,0:T(8,128)(2,1)S(1)}, u32[]{:S(2)}, u32[]{:S(2)}) collective-permute-start(bf16[136,128]{1,0:T(8,128)(2,1)S(1)} %shard_map.95.refs_0_), channel_id=1, source_target_pairs={{0,8},{1,9},{2,10},{3,11},{4,12},{5,13},{6,14},{7,15},{8,0},{9,1},... | collective-permute-start | bytes 104456 | tf_op jit(solution)/shard_map/ppermute | solution.py:23
  49.6 1.2 %collective-permute-start.30 = (bf16[136,128]{1,0:T(8,128)(2,1)S(1)}, bf16[136,128]{1,0:T(8,128)(2,1)S(1)}, u32[]{:S(2)}, u32[]{:S(2)}) collective-permute-start(bf16[136,128]{1,0:T(8,128)(2,1)S(1)} %shard_map.95.refs_0_), channel_id=1, source_target_pairs={{0,2},{1,3},{2,0},{3,1},{4,6},{5,7},{6,4},{7,5},{8,10},{9,11},{10,... | collective-permute-start | bytes 104456 | tf_op jit(solution)/shard_map/ppermute | solution.py:23
  50.8 0.5 collective-permute-done.32.refs_1_
  51.3 0.8 %collective-permute-done.35.refs_2_ = bf16[136,128]{1,0:T(8,128)(2,1)S(1)} collective-permute-done((bf16[136,128]{1,0:T(8,128)(2,1)S(1)}, bf16[136,128]{1,0:T(8,128)(2,1)S(1)}, u32[]{:S(2)}, u32[]{:S(2)}) %collective-permute-start.35) | collective-permute-done | bytes 34848 | tf_op jit(solution)/shard_map/ppermute | solution.py:23
  52.2 0.5 collective-permute-done.38.refs_3_
  52.7 1.2 %collective-permute-start.33 = (bf16[136,128]{1,0:T(8,128)(2,1)S(1)}, bf16[136,128]{1,0:T(8,128)(2,1)S(1)}, u32[]{:S(2)}, u32[]{:S(2)}) collective-permute-start(bf16[136,128]{1,0:T(8,128)(2,1)S(1)} %collective-permute-done.32.refs_1_), channel_id=1, source_target_pairs={{0,2},{1,3},{2,0},{3,1},{4,6},{5,7},{6,4},{7,5},{8,10},{9,11},{10,... | collective-permute-start | bytes 104456 | tf_op jit(solution)/shard_map/ppermute | solution.py:23
  53.9 0.8 %collective-permute-start.36 = (bf16[136,128]{1,0:T(8,128)(2,1)S(1)}, bf16[136,128]{1,0:T(8,128)(2,1)S(1)}, u32[]{:S(2)}, u32[]{:S(2)}) collective-permute-start(bf16[136,128]{1,0:T(8,128)(2,1)S(1)} %collective-permute-done.35.refs_2_), channel_id=1, source_target_pairs={{0,2},{1,3},{2,0},{3,1},{4,6},{5,7},{6,4},{7,5},{8,10},{9,11},{10,... | collective-permute-start | bytes 104456 | tf_op jit(solution)/shard_map/ppermute | solution.py:23
  54.7 1.2 %collective-permute-start.39 = (bf16[136,128]{1,0:T(8,128)(2,1)S(1)}, bf16[136,128]{1,0:T(8,128)(2,1)S(1)}, u32[]{:S(2)}, u32[]{:S(2)}) collective-permute-start(bf16[136,128]{1,0:T(8,128)(2,1)S(1)} %collective-permute-done.38.refs_3_), channel_id=1, source_target_pairs={{0,2},{1,3},{2,0},{3,1},{4,6},{5,7},{6,4},{7,5},{8,10},{9,11},{10,... | collective-permute-start | bytes 104456 | tf_op jit(solution)/shard_map/ppermute | solution.py:23
  56.0 0.5 collective-permute-start.31
  56.5 0.5 collective-permute-done.33.refs_1_
  57.0 0.9 %collective-permute-done.36.refs_2_ = bf16[136,128]{1,0:T(8,128)(2,1)S(1)} collective-permute-done((bf16[136,128]{1,0:T(8,128)(2,1)S(1)}, bf16[136,128]{1,0:T(8,128)(2,1)S(1)}, u32[]{:S(2)}, u32[]{:S(2)}) %collective-permute-start.36) | collective-permute-done | bytes 34848 | tf_op jit(solution)/shard_map/ppermute | solution.py:23
  57.9 0.8 %collective-permute-done.39.refs_3_ = bf16[136,128]{1,0:T(8,128)(2,1)S(1)} collective-permute-done((bf16[136,128]{1,0:T(8,128)(2,1)S(1)}, bf16[136,128]{1,0:T(8,128)(2,1)S(1)}, u32[]{:S(2)}, u32[]{:S(2)}) %collective-permute-start.39) | collective-permute-done | bytes 34848 | tf_op jit(solution)/shard_map/ppermute | solution.py:23
  58.7 1.3 %precondition.1.query = bf16[512,64]{1,0:T(8,128)(2,1)S(1)} custom-call(f32[8,4096]{1,0:T(8,128)S(1)} %copy-done.4, f32[64,64]{1,0:T(8,128)S(1)} %copy-done.5, f32[64,64]{1,0:T(8,128)S(1)} %copy-done.6, f32[64,64]{1,0:T(8,128)S(1)} %copy-done.7), custom_call_target="tpu_custom_call" | custom-call | flops 10000000000 | bytes 131072 | tf_op jit(solution)/shard_map/precondition/pallas_call | solution.py:191
  61.3 1.0 %shard_map.99 = f32[8,128]{1,0:T(8,128)} custom-call(bf16[512,64]{1,0:T(8,128)(2,1)S(1)} %precondition.1.query, bf16[136,128]{1,0:T(8,128)(2,1)S(1)} %collective-permute-done.31.refs_0_, bf16[136,128]{1,0:T(8,128)(2,1)S(1)} %collective-permute-done.34.refs_1_, bf16[136,128]{1,0:T(8,128)(2,1)S(1)} %collective-permute-done.37.refs_2_, ...), custom_call_target="tpu_custom_call" | custom-call | flops 33554432 | bytes 139264 | tf_op jit(solution)/shard_map/pallas_call | solution.py:244
  (71 shorter events, 3.0 us)
Async XLA Ops:
  0.0 41.5 %copy-start.2 = (bf16[64,1792]{1,0:T(8,128)(2,1)S(1)}, bf16[64,1792]{1,0:T(8,128)(2,1)}, u32[]{:S(2)}) copy-start(bf16[64,1792]{1,0:T(8,128)(2,1)} %refs_0_.1) | copy-start | bytes 688132
  0.0 41.5 %copy-start = (bf16[128,28672]{1,0:T(8,128)(2,1)S(1)}, bf16[128,28672]{1,0:T(8,128)(2,1)}, u32[]{:S(2)}) copy-start(bf16[128,28672]{1,0:T(8,128)(2,1)} %grad.9) | copy-start | bytes 22020100
  0.0 41.5 %copy-start.1 = (bf16[128,8192]{1,0:T(8,128)(2,1)S(1)}, bf16[128,8192]{1,0:T(8,128)(2,1)}, u32[]{:S(2)}) copy-start(bf16[128,8192]{1,0:T(8,128)(2,1)} %act.9) | copy-start | bytes 6291460
  0.0 7.7 %collective-permute-start.10 = (bf16[64,512]{1,0:T(8,128)(2,1)}, bf16[64,512]{1,0:T(8,128)(2,1)S(1)}, u32[]{:S(2)}, u32[]{:S(2)}) collective-permute-start(bf16[64,512]{1,0:T(8,128)(2,1)} %refs_1_.1), channel_id=1, source_target_pairs={{0,4},{1,5},{2,6},{3,7},{4,0},{5,1},{6,2},{7,3},{8,12},{9,13},{10,... | collective-permute-start | bytes 196616 | tf_op jit(solution)/shard_map/ppermute | solution.py:106
  3.1 5.5 %collective-permute-start.23 = (bf16[64,512]{1,0:T(8,128)(2,1)}, bf16[64,512]{1,0:T(8,128)(2,1)S(1)}, u32[]{:S(2)}, u32[]{:S(2)}) collective-permute-start(bf16[64,512]{1,0:T(8,128)(2,1)} %refs_1_.1), channel_id=1, source_target_pairs={{0,2},{1,3},{2,0},{3,1},{4,6},{5,7},{6,4},{7,5},{8,10},{9,11},{10,... | collective-permute-start | bytes 196616 | tf_op jit(solution)/shard_map/ppermute | solution.py:106
  4.7 5.9 %collective-permute-start.29 = (bf16[64,512]{1,0:T(8,128)(2,1)}, bf16[64,512]{1,0:T(8,128)(2,1)S(1)}, u32[]{:S(2)}, u32[]{:S(2)}) collective-permute-start(bf16[64,512]{1,0:T(8,128)(2,1)} %refs_1_.1), channel_id=1, source_target_pairs={{0,1},{1,0},{2,3},{3,2},{4,5},{5,4},{6,7},{7,6},{8,9},{9,8},{10,11... | collective-permute-start | bytes 196616 | tf_op jit(solution)/shard_map/ppermute | solution.py:127
  4.7 7.0 %collective-permute-start.3 = (bf16[64,512]{1,0:T(8,128)(2,1)}, bf16[64,512]{1,0:T(8,128)(2,1)S(1)}, u32[]{:S(2)}, u32[]{:S(2)}) collective-permute-start(bf16[64,512]{1,0:T(8,128)(2,1)} %refs_1_.1), channel_id=1, source_target_pairs={{0,8},{1,9},{2,10},{3,11},{4,12},{5,13},{6,14},{7,15},{8,0},{9,1},... | collective-permute-start | bytes 196616 | tf_op jit(solution)/shard_map/ppermute | solution.py:106
  7.2 12.8 %collective-permute-start.8 = (bf16[64,1792]{1,0:T(8,128)(2,1)}, bf16[64,1792]{1,0:T(8,128)(2,1)S(1)}, u32[]{:S(2)}, u32[]{:S(2)}) collective-permute-start(bf16[64,1792]{1,0:T(8,128)(2,1)} %refs_0_.1), channel_id=1, source_target_pairs={{0,4},{1,5},{2,6},{3,7},{4,0},{5,1},{6,2},{7,3},{8,12},{9,13},{10,... | collective-permute-start | bytes 688136 | tf_op jit(solution)/shard_map/ppermute | solution.py:106
  7.7 13.7 %collective-permute-start = (bf16[64,1792]{1,0:T(8,128)(2,1)}, bf16[64,1792]{1,0:T(8,128)(2,1)S(1)}, u32[]{:S(2)}, u32[]{:S(2)}) collective-permute-start(bf16[64,1792]{1,0:T(8,128)(2,1)} %refs_0_.1), channel_id=1, source_target_pairs={{0,8},{1,9},{2,10},{3,11},{4,12},{5,13},{6,14},{7,15},{8,0},{9,1},... | collective-permute-start | bytes 688136 | tf_op jit(solution)/shard_map/ppermute | solution.py:106
  8.6 13.4 %collective-permute-start.22 = (bf16[64,1792]{1,0:T(8,128)(2,1)}, bf16[64,1792]{1,0:T(8,128)(2,1)S(1)}, u32[]{:S(2)}, u32[]{:S(2)}) collective-permute-start(bf16[64,1792]{1,0:T(8,128)(2,1)} %refs_0_.1), channel_id=1, source_target_pairs={{0,2},{1,3},{2,0},{3,1},{4,6},{5,7},{6,4},{7,5},{8,10},{9,11},{10,... | collective-permute-start | bytes 688136 | tf_op jit(solution)/shard_map/ppermute | solution.py:106
  10.5 1.3 %collective-permute-start.27 = (bf16[64,512]{1,0:T(8,128)(2,1)S(1)}, bf16[64,512]{1,0:T(8,128)(2,1)S(1)}, u32[]{:S(2)}, u32[]{:S(2)}) collective-permute-start(bf16[64,512]{1,0:T(8,128)(2,1)S(1)} %collective-permute-done.10.refs_5_), channel_id=1, source_target_pairs={{0,1},{1,0},{2,3},{3,2},{4,5},{5,4},{6,7},{7,6},{8,9},{9,8},{10,11... | collective-permute-start | bytes 196616 | tf_op jit(solution)/shard_map/ppermute | solution.py:127
  11.7 1.3 %collective-permute-start.25 = (bf16[64,512]{1,0:T(8,128)(2,1)S(1)}, bf16[64,512]{1,0:T(8,128)(2,1)S(1)}, u32[]{:S(2)}, u32[]{:S(2)}) collective-permute-start(bf16[64,512]{1,0:T(8,128)(2,1)S(1)} %collective-permute-done.23.refs_1_), channel_id=1, source_target_pairs={{0,1},{1,0},{2,3},{3,2},{4,5},{5,4},{6,7},{7,6},{8,9},{9,8},{10,11... | collective-permute-start | bytes 196616 | tf_op jit(solution)/shard_map/ppermute | solution.py:127
  11.8 5.1 %collective-permute-start.4 = (bf16[64,512]{1,0:T(8,128)(2,1)S(1)}, bf16[64,512]{1,0:T(8,128)(2,1)S(1)}, u32[]{:S(2)}, u32[]{:S(2)}) collective-permute-start(bf16[64,512]{1,0:T(8,128)(2,1)S(1)} %collective-permute-done.3.refs_1_), channel_id=1, source_target_pairs={{0,2},{1,3},{2,0},{3,1},{4,6},{5,7},{6,4},{7,5},{8,10},{9,11},{10,... | collective-permute-start | bytes 196616 | tf_op jit(solution)/shard_map/ppermute | solution.py:106
  13.0 4.3 %collective-permute-start.19 = (bf16[64,512]{1,0:T(8,128)(2,1)S(1)}, bf16[64,512]{1,0:T(8,128)(2,1)S(1)}, u32[]{:S(2)}, u32[]{:S(2)}) collective-permute-start(bf16[64,512]{1,0:T(8,128)(2,1)S(1)} %collective-permute-done.3.refs_1_), channel_id=1, source_target_pairs={{0,16},{16,0},{1,17},{17,1},{2,18},{18,2},{3,19},{19,3},{4,20},{20... | collective-permute-start | bytes 196616 | tf_op jit(solution)/shard_map/ppermute | solution.py:112
  16.8 1.3 %collective-permute-start.15 = (bf16[64,512]{1,0:T(8,128)(2,1)S(1)}, bf16[64,512]{1,0:T(8,128)(2,1)S(1)}, u32[]{:S(2)}, u32[]{:S(2)}) collective-permute-start(bf16[64,512]{1,0:T(8,128)(2,1)S(1)} %collective-permute-done.3.refs_1_), channel_id=1, source_target_pairs={{0,1},{1,0},{2,3},{3,2},{4,5},{5,4},{6,7},{7,6},{8,9},{9,8},{10,11... | collective-permute-start | bytes 196616 | tf_op jit(solution)/shard_map/ppermute | solution.py:127
  17.2 4.8 %collective-permute-start.11 = (bf16[64,512]{1,0:T(8,128)(2,1)S(1)}, bf16[64,512]{1,0:T(8,128)(2,1)S(1)}, u32[]{:S(2)}, u32[]{:S(2)}) collective-permute-start(bf16[64,512]{1,0:T(8,128)(2,1)S(1)} %collective-permute-done.10.refs_5_), channel_id=1, source_target_pairs={{0,2},{1,3},{2,0},{3,1},{4,6},{5,7},{6,4},{7,5},{8,10},{9,11},{10,... | collective-permute-start | bytes 196616 | tf_op jit(solution)/shard_map/ppermute | solution.py:106
  18.2 12.4 %collective-permute-start.28 = (bf16[64,1792]{1,0:T(8,128)(2,1)}, bf16[64,1792]{1,0:T(8,128)(2,1)S(1)}, u32[]{:S(2)}, u32[]{:S(2)}) collective-permute-start(bf16[64,1792]{1,0:T(8,128)(2,1)} %refs_0_.1), channel_id=1, source_target_pairs={{0,1},{1,0},{2,3},{3,2},{4,5},{5,4},{6,7},{7,6},{8,9},{9,8},{10,11... | collective-permute-start | bytes 688136 | tf_op jit(solution)/shard_map/ppermute | solution.py:127
  20.1 10.5 %collective-permute-start.26 = (bf16[64,1792]{1,0:T(8,128)(2,1)S(1)}, bf16[64,1792]{1,0:T(8,128)(2,1)S(1)}, u32[]{:S(2)}, u32[]{:S(2)}) collective-permute-start(bf16[64,1792]{1,0:T(8,128)(2,1)S(1)} %collective-permute-done.8.refs_4_), channel_id=1, source_target_pairs={{0,1},{1,0},{2,3},{3,2},{4,5},{5,4},{6,7},{7,6},{8,9},{9,8},{10,11... | collective-permute-start | bytes 688136 | tf_op jit(solution)/shard_map/ppermute | solution.py:127
  21.4 10.4 %collective-permute-start.1 = (bf16[64,1792]{1,0:T(8,128)(2,1)S(1)}, bf16[64,1792]{1,0:T(8,128)(2,1)S(1)}, u32[]{:S(2)}, u32[]{:S(2)}) collective-permute-start(bf16[64,1792]{1,0:T(8,128)(2,1)S(1)} %collective-permute-done.refs_0_), channel_id=1, source_target_pairs={{0,2},{1,3},{2,0},{3,1},{4,6},{5,7},{6,4},{7,5},{8,10},{9,11},{10,... | collective-permute-start | bytes 688136 | tf_op jit(solution)/shard_map/ppermute | solution.py:106
  22.0 10.0 %collective-permute-start.24 = (bf16[64,1792]{1,0:T(8,128)(2,1)S(1)}, bf16[64,1792]{1,0:T(8,128)(2,1)S(1)}, u32[]{:S(2)}, u32[]{:S(2)}) collective-permute-start(bf16[64,1792]{1,0:T(8,128)(2,1)S(1)} %collective-permute-done.22.refs_0_), channel_id=1, source_target_pairs={{0,1},{1,0},{2,3},{3,2},{4,5},{5,4},{6,7},{7,6},{8,9},{9,8},{10,11... | collective-permute-start | bytes 688136 | tf_op jit(solution)/shard_map/ppermute | solution.py:127
  22.0 1.6 %collective-permute-start.17 = (bf16[64,512]{1,0:T(8,128)(2,1)S(1)}, bf16[64,512]{1,0:T(8,128)(2,1)S(1)}, u32[]{:S(2)}, u32[]{:S(2)}) collective-permute-start(bf16[64,512]{1,0:T(8,128)(2,1)S(1)} %collective-permute-done.4.refs_5_), channel_id=1, source_target_pairs={{0,1},{1,0},{2,3},{3,2},{4,5},{5,4},{6,7},{7,6},{8,9},{9,8},{10,11... | collective-permute-start | bytes 196616 | tf_op jit(solution)/shard_map/ppermute | solution.py:127
  23.6 1.3 %collective-permute-start.21 = (bf16[64,512]{1,0:T(8,128)(2,1)S(1)}, bf16[64,512]{1,0:T(8,128)(2,1)S(1)}, u32[]{:S(2)}, u32[]{:S(2)}) collective-permute-start(bf16[64,512]{1,0:T(8,128)(2,1)S(1)} %collective-permute-done.19.refs_9_), channel_id=1, source_target_pairs={{0,1},{1,0},{2,3},{3,2},{4,5},{5,4},{6,7},{7,6},{8,9},{9,8},{10,11... | collective-permute-start | bytes 196616 | tf_op jit(solution)/shard_map/ppermute | solution.py:127
  24.8 4.3 %collective-permute-start.5 = (bf16[64,512]{1,0:T(8,128)(2,1)S(1)}, bf16[64,512]{1,0:T(8,128)(2,1)S(1)}, u32[]{:S(2)}, u32[]{:S(2)}) collective-permute-start(bf16[64,512]{1,0:T(8,128)(2,1)S(1)} %collective-permute-done.4.refs_5_), channel_id=1, source_target_pairs={{0,16},{16,0},{1,17},{17,1},{2,18},{18,2},{3,19},{19,3},{4,20},{20... | collective-permute-start | bytes 196616 | tf_op jit(solution)/shard_map/ppermute | solution.py:112
  29.1 7.8 %collective-permute-start.18 = (bf16[64,1792]{1,0:T(8,128)(2,1)S(1)}, bf16[64,1792]{1,0:T(8,128)(2,1)S(1)}, u32[]{:S(2)}, u32[]{:S(2)}) collective-permute-start(bf16[64,1792]{1,0:T(8,128)(2,1)S(1)} %collective-permute-done.refs_0_), channel_id=1, source_target_pairs={{0,16},{16,0},{1,17},{17,1},{2,18},{18,2},{3,19},{19,3},{4,20},{20... | collective-permute-start | bytes 688136 | tf_op jit(solution)/shard_map/ppermute | solution.py:112
  30.6 6.3 %collective-permute-start.14 = (bf16[64,1792]{1,0:T(8,128)(2,1)S(1)}, bf16[64,1792]{1,0:T(8,128)(2,1)S(1)}, u32[]{:S(2)}, u32[]{:S(2)}) collective-permute-start(bf16[64,1792]{1,0:T(8,128)(2,1)S(1)} %collective-permute-done.refs_0_), channel_id=1, source_target_pairs={{0,1},{1,0},{2,3},{3,2},{4,5},{5,4},{6,7},{7,6},{8,9},{9,8},{10,11... | collective-permute-start | bytes 688136 | tf_op jit(solution)/shard_map/ppermute | solution.py:127
  30.6 8.0 %collective-permute-start.9 = (bf16[64,1792]{1,0:T(8,128)(2,1)S(1)}, bf16[64,1792]{1,0:T(8,128)(2,1)S(1)}, u32[]{:S(2)}, u32[]{:S(2)}) collective-permute-start(bf16[64,1792]{1,0:T(8,128)(2,1)S(1)} %collective-permute-done.8.refs_4_), channel_id=1, source_target_pairs={{0,2},{1,3},{2,0},{3,1},{4,6},{5,7},{6,4},{7,5},{8,10},{9,11},{10,... | collective-permute-start | bytes 688136 | tf_op jit(solution)/shard_map/ppermute | solution.py:106
  31.8 6.8 %collective-permute-start.16 = (bf16[64,1792]{1,0:T(8,128)(2,1)S(1)}, bf16[64,1792]{1,0:T(8,128)(2,1)S(1)}, u32[]{:S(2)}, u32[]{:S(2)}) collective-permute-start(bf16[64,1792]{1,0:T(8,128)(2,1)S(1)} %collective-permute-done.1.refs_4_), channel_id=1, source_target_pairs={{0,1},{1,0},{2,3},{3,2},{4,5},{5,4},{6,7},{7,6},{8,9},{9,8},{10,11... | collective-permute-start | bytes 688136 | tf_op jit(solution)/shard_map/ppermute | solution.py:127
  32.0 8.8 %collective-permute-start.2 = (bf16[64,1792]{1,0:T(8,128)(2,1)S(1)}, bf16[64,1792]{1,0:T(8,128)(2,1)S(1)}, u32[]{:S(2)}, u32[]{:S(2)}) collective-permute-start(bf16[64,1792]{1,0:T(8,128)(2,1)S(1)} %collective-permute-done.1.refs_4_), channel_id=1, source_target_pairs={{0,16},{16,0},{1,17},{17,1},{2,18},{18,2},{3,19},{19,3},{4,20},{20... | collective-permute-start | bytes 688136 | tf_op jit(solution)/shard_map/ppermute | solution.py:112
  36.9 7.2 %collective-permute-start.13 = (bf16[64,512]{1,0:T(8,128)(2,1)S(1)}, bf16[64,512]{1,0:T(8,128)(2,1)S(1)}, u32[]{:S(2)}, u32[]{:S(2)}) collective-permute-start(bf16[64,512]{1,0:T(8,128)(2,1)S(1)} %collective-permute-done.11.refs_1_), channel_id=1, source_target_pairs={{0,1},{1,0},{2,3},{3,2},{4,5},{5,4},{6,7},{7,6},{8,9},{9,8},{10,11... | collective-permute-start | bytes 196616 | tf_op jit(solution)/shard_map/ppermute | solution.py:127
  36.9 7.7 %collective-permute-start.7 = (bf16[64,512]{1,0:T(8,128)(2,1)S(1)}, bf16[64,512]{1,0:T(8,128)(2,1)S(1)}, u32[]{:S(2)}, u32[]{:S(2)}) collective-permute-start(bf16[64,512]{1,0:T(8,128)(2,1)S(1)} %collective-permute-done.5.refs_1_), channel_id=1, source_target_pairs={{0,1},{1,0},{2,3},{3,2},{4,5},{5,4},{6,7},{7,6},{8,9},{9,8},{10,11... | collective-permute-start | bytes 196616 | tf_op jit(solution)/shard_map/ppermute | solution.py:127
  38.6 4.3 %collective-permute-start.20 = (bf16[64,1792]{1,0:T(8,128)(2,1)S(1)}, bf16[64,1792]{1,0:T(8,128)(2,1)S(1)}, u32[]{:S(2)}, u32[]{:S(2)}) collective-permute-start(bf16[64,1792]{1,0:T(8,128)(2,1)S(1)} %collective-permute-done.18.refs_8_), channel_id=1, source_target_pairs={{0,1},{1,0},{2,3},{3,2},{4,5},{5,4},{6,7},{7,6},{8,9},{9,8},{10,11... | collective-permute-start | bytes 688136 | tf_op jit(solution)/shard_map/ppermute | solution.py:127
  38.6 5.5 %collective-permute-start.12 = (bf16[64,1792]{1,0:T(8,128)(2,1)S(1)}, bf16[64,1792]{1,0:T(8,128)(2,1)S(1)}, u32[]{:S(2)}, u32[]{:S(2)}) collective-permute-start(bf16[64,1792]{1,0:T(8,128)(2,1)S(1)} %collective-permute-done.9.refs_0_), channel_id=1, source_target_pairs={{0,1},{1,0},{2,3},{3,2},{4,5},{5,4},{6,7},{7,6},{8,9},{9,8},{10,11... | collective-permute-start | bytes 688136 | tf_op jit(solution)/shard_map/ppermute | solution.py:127
  40.8 3.8 %collective-permute-start.6 = (bf16[64,1792]{1,0:T(8,128)(2,1)S(1)}, bf16[64,1792]{1,0:T(8,128)(2,1)S(1)}, u32[]{:S(2)}, u32[]{:S(2)}) collective-permute-start(bf16[64,1792]{1,0:T(8,128)(2,1)S(1)} %collective-permute-done.2.refs_0_), channel_id=1, source_target_pairs={{0,1},{1,0},{2,3},{3,2},{4,5},{5,4},{6,7},{7,6},{8,9},{9,8},{10,11... | collective-permute-start | bytes 688136 | tf_op jit(solution)/shard_map/ppermute | solution.py:127
  45.2 6.2 %collective-permute-start.32 = (bf16[136,128]{1,0:T(8,128)(2,1)S(1)}, bf16[136,128]{1,0:T(8,128)(2,1)S(1)}, u32[]{:S(2)}, u32[]{:S(2)}) collective-permute-start(bf16[136,128]{1,0:T(8,128)(2,1)S(1)} %shard_map.95.refs_0_), channel_id=1, source_target_pairs={{0,12},{1,13},{2,14},{3,15},{4,8},{5,9},{6,10},{7,11},{8,4},{9,5},... | collective-permute-start | bytes 104456 | tf_op jit(solution)/shard_map/ppermute | solution.py:23
  47.8 4.3 %collective-permute-start.35 = (bf16[136,128]{1,0:T(8,128)(2,1)S(1)}, bf16[136,128]{1,0:T(8,128)(2,1)S(1)}, u32[]{:S(2)}, u32[]{:S(2)}) collective-permute-start(bf16[136,128]{1,0:T(8,128)(2,1)S(1)} %shard_map.95.refs_0_), channel_id=1, source_target_pairs={{0,4},{1,5},{2,6},{3,7},{4,0},{5,1},{6,2},{7,3},{8,12},{9,13},{10,... | collective-permute-start | bytes 104456 | tf_op jit(solution)/shard_map/ppermute | solution.py:23
  47.9 4.8 %collective-permute-start.38 = (bf16[136,128]{1,0:T(8,128)(2,1)S(1)}, bf16[136,128]{1,0:T(8,128)(2,1)S(1)}, u32[]{:S(2)}, u32[]{:S(2)}) collective-permute-start(bf16[136,128]{1,0:T(8,128)(2,1)S(1)} %shard_map.95.refs_0_), channel_id=1, source_target_pairs={{0,8},{1,9},{2,10},{3,11},{4,12},{5,13},{6,14},{7,15},{8,0},{9,1},... | collective-permute-start | bytes 104456 | tf_op jit(solution)/shard_map/ppermute | solution.py:23
  49.6 4.3 %collective-permute-start.41 = (bf16[136,128]{1,0:T(8,128)(2,1)S(1)}, bf16[136,128]{1,0:T(8,128)(2,1)S(1)}, u32[]{:S(2)}, u32[]{:S(2)}) collective-permute-start(bf16[136,128]{1,0:T(8,128)(2,1)S(1)} %shard_map.95.refs_0_), channel_id=1, source_target_pairs={{0,1},{1,0},{2,3},{3,2},{4,5},{5,4},{6,7},{7,6},{8,9},{9,8},{10,11... | collective-permute-start | bytes 104456 | tf_op jit(solution)/shard_map/ppermute | solution.py:23
  49.6 5.1 %collective-permute-start.30 = (bf16[136,128]{1,0:T(8,128)(2,1)S(1)}, bf16[136,128]{1,0:T(8,128)(2,1)S(1)}, u32[]{:S(2)}, u32[]{:S(2)}) collective-permute-start(bf16[136,128]{1,0:T(8,128)(2,1)S(1)} %shard_map.95.refs_0_), channel_id=1, source_target_pairs={{0,2},{1,3},{2,0},{3,1},{4,6},{5,7},{6,4},{7,5},{8,10},{9,11},{10,... | collective-permute-start | bytes 104456 | tf_op jit(solution)/shard_map/ppermute | solution.py:23
  51.3 4.6 %collective-permute-start.42 = (bf16[136,128]{1,0:T(8,128)(2,1)S(1)}, bf16[136,128]{1,0:T(8,128)(2,1)S(1)}, u32[]{:S(2)}, u32[]{:S(2)}) collective-permute-start(bf16[136,128]{1,0:T(8,128)(2,1)S(1)} %collective-permute-done.32.refs_1_), channel_id=1, source_target_pairs={{0,1},{1,0},{2,3},{3,2},{4,5},{5,4},{6,7},{7,6},{8,9},{9,8},{10,11... | collective-permute-start | bytes 104456 | tf_op jit(solution)/shard_map/ppermute | solution.py:23
  52.2 3.8 %collective-permute-start.43 = (bf16[136,128]{1,0:T(8,128)(2,1)S(1)}, bf16[136,128]{1,0:T(8,128)(2,1)S(1)}, u32[]{:S(2)}, u32[]{:S(2)}) collective-permute-start(bf16[136,128]{1,0:T(8,128)(2,1)S(1)} %collective-permute-done.35.refs_2_), channel_id=1, source_target_pairs={{0,1},{1,0},{2,3},{3,2},{4,5},{5,4},{6,7},{7,6},{8,9},{9,8},{10,11... | collective-permute-start | bytes 104456 | tf_op jit(solution)/shard_map/ppermute | solution.py:23
  52.7 4.3 %collective-permute-start.33 = (bf16[136,128]{1,0:T(8,128)(2,1)S(1)}, bf16[136,128]{1,0:T(8,128)(2,1)S(1)}, u32[]{:S(2)}, u32[]{:S(2)}) collective-permute-start(bf16[136,128]{1,0:T(8,128)(2,1)S(1)} %collective-permute-done.32.refs_1_), channel_id=1, source_target_pairs={{0,2},{1,3},{2,0},{3,1},{4,6},{5,7},{6,4},{7,5},{8,10},{9,11},{10,... | collective-permute-start | bytes 104456 | tf_op jit(solution)/shard_map/ppermute | solution.py:23
  53.9 3.9 %collective-permute-start.36 = (bf16[136,128]{1,0:T(8,128)(2,1)S(1)}, bf16[136,128]{1,0:T(8,128)(2,1)S(1)}, u32[]{:S(2)}, u32[]{:S(2)}) collective-permute-start(bf16[136,128]{1,0:T(8,128)(2,1)S(1)} %collective-permute-done.35.refs_2_), channel_id=1, source_target_pairs={{0,2},{1,3},{2,0},{3,1},{4,6},{5,7},{6,4},{7,5},{8,10},{9,11},{10,... | collective-permute-start | bytes 104456 | tf_op jit(solution)/shard_map/ppermute | solution.py:23
  54.7 3.9 %collective-permute-start.39 = (bf16[136,128]{1,0:T(8,128)(2,1)S(1)}, bf16[136,128]{1,0:T(8,128)(2,1)S(1)}, u32[]{:S(2)}, u32[]{:S(2)}) collective-permute-start(bf16[136,128]{1,0:T(8,128)(2,1)S(1)} %collective-permute-done.38.refs_3_), channel_id=1, source_target_pairs={{0,2},{1,3},{2,0},{3,1},{4,6},{5,7},{6,4},{7,5},{8,10},{9,11},{10,... | collective-permute-start | bytes 104456 | tf_op jit(solution)/shard_map/ppermute | solution.py:23
  56.0 4.4 %collective-permute-start.44 = (bf16[136,128]{1,0:T(8,128)(2,1)S(1)}, bf16[136,128]{1,0:T(8,128)(2,1)S(1)}, u32[]{:S(2)}, u32[]{:S(2)}) collective-permute-start(bf16[136,128]{1,0:T(8,128)(2,1)S(1)} %collective-permute-done.38.refs_3_), channel_id=1, source_target_pairs={{0,1},{1,0},{2,3},{3,2},{4,5},{5,4},{6,7},{7,6},{8,9},{9,8},{10,11... | collective-permute-start | bytes 104456 | tf_op jit(solution)/shard_map/ppermute | solution.py:23
  56.0 5.3 %collective-permute-start.31 = (bf16[136,128]{1,0:T(8,128)(2,1)S(1)}, bf16[136,128]{1,0:T(8,128)(2,1)S(1)}, u32[]{:S(2)}, u32[]{:S(2)}) collective-permute-start(bf16[136,128]{1,0:T(8,128)(2,1)S(1)} %collective-permute-done.30.refs_0_), channel_id=1, source_target_pairs={{0,1},{1,0},{2,3},{3,2},{4,5},{5,4},{6,7},{7,6},{8,9},{9,8},{10,11... | collective-permute-start | bytes 104456 | tf_op jit(solution)/shard_map/ppermute | solution.py:23
  57.0 4.3 %collective-permute-start.34 = (bf16[136,128]{1,0:T(8,128)(2,1)S(1)}, bf16[136,128]{1,0:T(8,128)(2,1)S(1)}, u32[]{:S(2)}, u32[]{:S(2)}) collective-permute-start(bf16[136,128]{1,0:T(8,128)(2,1)S(1)} %collective-permute-done.33.refs_1_), channel_id=1, source_target_pairs={{0,1},{1,0},{2,3},{3,2},{4,5},{5,4},{6,7},{7,6},{8,9},{9,8},{10,11... | collective-permute-start | bytes 104456 | tf_op jit(solution)/shard_map/ppermute | solution.py:23
  57.9 3.5 %collective-permute-start.37 = (bf16[136,128]{1,0:T(8,128)(2,1)S(1)}, bf16[136,128]{1,0:T(8,128)(2,1)S(1)}, u32[]{:S(2)}, u32[]{:S(2)}) collective-permute-start(bf16[136,128]{1,0:T(8,128)(2,1)S(1)} %collective-permute-done.36.refs_2_), channel_id=1, source_target_pairs={{0,1},{1,0},{2,3},{3,2},{4,5},{5,4},{6,7},{7,6},{8,9},{9,8},{10,11... | collective-permute-start | bytes 104456 | tf_op jit(solution)/shard_map/ppermute | solution.py:23
  58.7 2.7 %collective-permute-start.40 = (bf16[136,128]{1,0:T(8,128)(2,1)S(1)}, bf16[136,128]{1,0:T(8,128)(2,1)S(1)}, u32[]{:S(2)}, u32[]{:S(2)}) collective-permute-start(bf16[136,128]{1,0:T(8,128)(2,1)S(1)} %collective-permute-done.39.refs_3_), channel_id=1, source_target_pairs={{0,1},{1,0},{2,3},{3,2},{4,5},{5,4},{6,7},{7,6},{8,9},{9,8},{10,11... | collective-permute-start | bytes 104456 | tf_op jit(solution)/shard_map/ppermute | solution.py:23
  (6 other events, 98.5 us)

commit v4 on v3

--- a/solution.py
+++ b/solution.py
@@ -239,7 +239,7 @@
 def score(query, blocks, offsets, examples, part, final):
     rank2, tokens = blocks[0].shape
     queries = query.shape[0] // query.shape[1]
-    group = math.gcd(4, len(offsets))
+    group = next(size for size in range(8, 0, -1) if len(offsets) % size == 0)
     parts = () if part is None else (part,)
     return pl.pallas_call(
         functools.partial(score_kernel, tuple(offsets), final, bool(parts)),
@@ -287,7 +287,8 @@
     cores = {}
     for o, block in rest.items():
         cores[o ^ 1] = moved(block, n, 1)
-    steps += [rest, cores]
+    *most, final = cores.items()
+    steps += [{**rest, **dict(most)}, dict([final])]
     total = None
     for i, step in enumerate(steps):
         total = score(query, list(step.values()), list(step), EX_DEV * n, total, i == len(steps) - 1)

time: 62.5 us -> 62.6 us (level)
  no operation moved by 1% of the time
where the time goes in v4:
time: 62.6 us; the launch traced here: 62.4 us
  starting transfers between devices  30.8 us (49%)
  waiting for transfers between devices  23.6 us (38%)
  Pallas kernels  7.19 us (11%)
  local copies, waits for them, and re-layouts  0.7 us (1%)
    ppermute x10, starting transfers between devices, bring(): held[*to, kind] = lax.ppermute(held[*source, kind], ('dom', 'shard'), pairs)  13.9 us
    ppermute x15, starting transfers between devices, moved(): return lax.ppermute(value, 'shard', [(i, i ^ offset) for i in range(n)])  9.44 us
    ppermute x4, waiting for transfers between devices, cross(): held[*to, kind] = lax.ppermute(held[*source, kind], 'dom', [(0, 1), (1, 0)])  8.92 us
    ppermute x10, waiting for transfers between devices, bring(): held[*to, kind] = lax.ppermute(held[*source, kind], ('dom', 'shard'), pairs)  7.8 us
    ppermute x4, starting transfers between devices, cross(): held[*to, kind] = lax.ppermute(held[*source, kind], 'dom', [(0, 1), (1, 0)])  5.29 us
    ppermute x15, waiting for transfers between devices, moved(): return lax.ppermute(value, 'shard', [(i, i ^ offset) for i in range(n)])  4.09 us
    pallas_call x5, Pallas kernels, project(): pl.pallas_call(functools.partial(project_kernel, tuple(keys), part is not...  3.5 us
    ppermute x16, waiting for transfers between devices, project_paired(): lax.ppermute(held[key], 'shard', [(i, i ^ 1) for i in range(n)])  2.75 us
  transfers between devices with their start and end apart: 45, of which 19 were waited for; matrix products, arithmetic and copies ran while one was open for 0% of the time, Pallas kernels for 9%

profile of v4, /device:TPU:0, one launch (start us, length us, event | category | flops | bytes accessed | tf_op | source)
XLA Modules:
  0.0 62.4 jit_solution(16467704443754337877)
XLA Ops:
  0.0 3.1 %collective-permute-start.10 = (bf16[64,512]{1,0:T(8,128)(2,1)}, bf16[64,512]{1,0:T(8,128)(2,1)S(1)}, u32[]{:S(2)}, u32[]{:S(2)}) collective-permute-start(bf16[64,512]{1,0:T(8,128)(2,1)} %refs_1_.1), channel_id=1, source_target_pairs={{0,4},{1,5},{2,6},{3,7},{4,0},{5,1},{6,2},{7,3},{8,12},{9,13},{10,... | collective-permute-start | bytes 196616 | tf_op jit(solution)/shard_map/ppermute | solution.py:106
  3.1 1.5 %collective-permute-start.23 = (bf16[64,512]{1,0:T(8,128)(2,1)}, bf16[64,512]{1,0:T(8,128)(2,1)S(1)}, u32[]{:S(2)}, u32[]{:S(2)}) collective-permute-start(bf16[64,512]{1,0:T(8,128)(2,1)} %refs_1_.1), channel_id=1, source_target_pairs={{0,2},{1,3},{2,0},{3,1},{4,6},{5,7},{6,4},{7,5},{8,10},{9,11},{10,... | collective-permute-start | bytes 196616 | tf_op jit(solution)/shard_map/ppermute | solution.py:106
  4.7 2.6 %collective-permute-start.3 = (bf16[64,512]{1,0:T(8,128)(2,1)}, bf16[64,512]{1,0:T(8,128)(2,1)S(1)}, u32[]{:S(2)}, u32[]{:S(2)}) collective-permute-start(bf16[64,512]{1,0:T(8,128)(2,1)} %refs_1_.1), channel_id=1, source_target_pairs={{0,8},{1,9},{2,10},{3,11},{4,12},{5,13},{6,14},{7,15},{8,0},{9,1},... | collective-permute-start | bytes 196616 | tf_op jit(solution)/shard_map/ppermute | solution.py:106
  7.7 0.9 %collective-permute-start = (bf16[64,1792]{1,0:T(8,128)(2,1)}, bf16[64,1792]{1,0:T(8,128)(2,1)S(1)}, u32[]{:S(2)}, u32[]{:S(2)}) collective-permute-start(bf16[64,1792]{1,0:T(8,128)(2,1)} %refs_0_.1), channel_id=1, source_target_pairs={{0,8},{1,9},{2,10},{3,11},{4,12},{5,13},{6,14},{7,15},{8,0},{9,1},... | collective-permute-start | bytes 688136 | tf_op jit(solution)/shard_map/ppermute | solution.py:106
  8.6 1.9 %collective-permute-start.22 = (bf16[64,1792]{1,0:T(8,128)(2,1)}, bf16[64,1792]{1,0:T(8,128)(2,1)S(1)}, u32[]{:S(2)}, u32[]{:S(2)}) collective-permute-start(bf16[64,1792]{1,0:T(8,128)(2,1)} %refs_0_.1), channel_id=1, source_target_pairs={{0,2},{1,3},{2,0},{3,1},{4,6},{5,7},{6,4},{7,5},{8,10},{9,11},{10,... | collective-permute-start | bytes 688136 | tf_op jit(solution)/shard_map/ppermute | solution.py:106
  10.5 1.2 %collective-permute-done.3.refs_1_ = bf16[64,512]{1,0:T(8,128)(2,1)S(1)} collective-permute-done((bf16[64,512]{1,0:T(8,128)(2,1)}, bf16[64,512]{1,0:T(8,128)(2,1)S(1)}, u32[]{:S(2)}, u32[]{:S(2)}) %collective-permute-start.3) | collective-permute-done | bytes 65568 | tf_op jit(solution)/shard_map/ppermute | solution.py:106
  11.8 0.7 %collective-permute-start.4 = (bf16[64,512]{1,0:T(8,128)(2,1)S(1)}, bf16[64,512]{1,0:T(8,128)(2,1)S(1)}, u32[]{:S(2)}, u32[]{:S(2)}) collective-permute-start(bf16[64,512]{1,0:T(8,128)(2,1)S(1)} %collective-permute-done.3.refs_1_), channel_id=1, source_target_pairs={{0,2},{1,3},{2,0},{3,1},{4,6},{5,7},{6,4},{7,5},{8,10},{9,11},{10,... | collective-permute-start | bytes 196616 | tf_op jit(solution)/shard_map/ppermute | solution.py:106
  12.4 0.5 collective-permute-done.25.refs_3_
  13.0 1.5 %collective-permute-start.19 = (bf16[64,512]{1,0:T(8,128)(2,1)S(1)}, bf16[64,512]{1,0:T(8,128)(2,1)S(1)}, u32[]{:S(2)}, u32[]{:S(2)}) collective-permute-start(bf16[64,512]{1,0:T(8,128)(2,1)S(1)} %collective-permute-done.3.refs_1_), channel_id=1, source_target_pairs={{0,16},{16,0},{1,17},{17,1},{2,18},{18,2},{3,19},{19,3},{4,20},{20... | collective-permute-start | bytes 196616 | tf_op jit(solution)/shard_map/ppermute | solution.py:112
  14.4 2.4 %collective-permute-done.4.refs_5_ = bf16[64,512]{1,0:T(8,128)(2,1)S(1)} collective-permute-done((bf16[64,512]{1,0:T(8,128)(2,1)S(1)}, bf16[64,512]{1,0:T(8,128)(2,1)S(1)}, u32[]{:S(2)}, u32[]{:S(2)}) %collective-permute-start.4) | collective-permute-done | bytes 65568 | tf_op jit(solution)/shard_map/ppermute | solution.py:106
  17.2 1.0 %collective-permute-start.11 = (bf16[64,512]{1,0:T(8,128)(2,1)S(1)}, bf16[64,512]{1,0:T(8,128)(2,1)S(1)}, u32[]{:S(2)}, u32[]{:S(2)}) collective-permute-start(bf16[64,512]{1,0:T(8,128)(2,1)S(1)} %collective-permute-done.10.refs_5_), channel_id=1, source_target_pairs={{0,2},{1,3},{2,0},{3,1},{4,6},{5,7},{6,4},{7,5},{8,10},{9,11},{10,... | collective-permute-start | bytes 196616 | tf_op jit(solution)/shard_map/ppermute | solution.py:106
  18.4 1.7 %collective-permute-done.8.refs_4_ = bf16[64,1792]{1,0:T(8,128)(2,1)S(1)} collective-permute-done((bf16[64,1792]{1,0:T(8,128)(2,1)}, bf16[64,1792]{1,0:T(8,128)(2,1)S(1)}, u32[]{:S(2)}, u32[]{:S(2)}) %collective-permute-start.8) | collective-permute-done | bytes 229408 | tf_op jit(solution)/shard_map/ppermute | solution.py:106
  20.1 1.3 %collective-permute-done.refs_0_ = bf16[64,1792]{1,0:T(8,128)(2,1)S(1)} collective-permute-done((bf16[64,1792]{1,0:T(8,128)(2,1)}, bf16[64,1792]{1,0:T(8,128)(2,1)S(1)}, u32[]{:S(2)}, u32[]{:S(2)}) %collective-permute-start) | collective-permute-done | bytes 229408 | tf_op jit(solution)/shard_map/ppermute | solution.py:106
  21.4 0.5 collective-permute-start.1
  22.0 0.5 collective-permute-start.17
  22.5 1.1 %collective-permute-done.17.refs_7_ = bf16[64,512]{1,0:T(8,128)(2,1)S(1)} collective-permute-done((bf16[64,512]{1,0:T(8,128)(2,1)S(1)}, bf16[64,512]{1,0:T(8,128)(2,1)S(1)}, u32[]{:S(2)}, u32[]{:S(2)}) %collective-permute-start.17) | collective-permute-done | bytes 65568 | tf_op jit(solution)/shard_map/ppermute | solution.py:127
  23.8 1.1 %collective-permute-done.21.refs_11_ = bf16[64,512]{1,0:T(8,128)(2,1)S(1)} collective-permute-done((bf16[64,512]{1,0:T(8,128)(2,1)S(1)}, bf16[64,512]{1,0:T(8,128)(2,1)S(1)}, u32[]{:S(2)}, u32[]{:S(2)}) %collective-permute-start.21) | collective-permute-done | bytes 65568 | tf_op jit(solution)/shard_map/ppermute | solution.py:127
  24.8 1.5 %collective-permute-start.5 = (bf16[64,512]{1,0:T(8,128)(2,1)S(1)}, bf16[64,512]{1,0:T(8,128)(2,1)S(1)}, u32[]{:S(2)}, u32[]{:S(2)}) collective-permute-start(bf16[64,512]{1,0:T(8,128)(2,1)S(1)} %collective-permute-done.4.refs_5_), channel_id=1, source_target_pairs={{0,16},{16,0},{1,17},{17,1},{2,18},{18,2},{3,19},{19,3},{4,20},{20... | collective-permute-start | bytes 196616 | tf_op jit(solution)/shard_map/ppermute | solution.py:112
  26.3 2.8 %collective-permute-done.5.refs_1_ = bf16[64,512]{1,0:T(8,128)(2,1)S(1)} collective-permute-done((bf16[64,512]{1,0:T(8,128)(2,1)S(1)}, bf16[64,512]{1,0:T(8,128)(2,1)S(1)}, u32[]{:S(2)}, u32[]{:S(2)}) %collective-permute-start.5) | collective-permute-done | bytes 65568 | tf_op jit(solution)/shard_map/ppermute | solution.py:112
  29.1 1.5 %collective-permute-start.18 = (bf16[64,1792]{1,0:T(8,128)(2,1)S(1)}, bf16[64,1792]{1,0:T(8,128)(2,1)S(1)}, u32[]{:S(2)}, u32[]{:S(2)}) collective-permute-start(bf16[64,1792]{1,0:T(8,128)(2,1)S(1)} %collective-permute-done.refs_0_), channel_id=1, source_target_pairs={{0,16},{16,0},{1,17},{17,1},{2,18},{18,2},{3,19},{19,3},{4,20},{20... | collective-permute-start | bytes 688136 | tf_op jit(solution)/shard_map/ppermute | solution.py:112
  30.6 1.2 %collective-permute-start.9 = (bf16[64,1792]{1,0:T(8,128)(2,1)S(1)}, bf16[64,1792]{1,0:T(8,128)(2,1)S(1)}, u32[]{:S(2)}, u32[]{:S(2)}) collective-permute-start(bf16[64,1792]{1,0:T(8,128)(2,1)S(1)} %collective-permute-done.8.refs_4_), channel_id=1, source_target_pairs={{0,2},{1,3},{2,0},{3,1},{4,6},{5,7},{6,4},{7,5},{8,10},{9,11},{10,... | collective-permute-start | bytes 688136 | tf_op jit(solution)/shard_map/ppermute | solution.py:106
  32.0 0.9 %collective-permute-start.2 = (bf16[64,1792]{1,0:T(8,128)(2,1)S(1)}, bf16[64,1792]{1,0:T(8,128)(2,1)S(1)}, u32[]{:S(2)}, u32[]{:S(2)}) collective-permute-start(bf16[64,1792]{1,0:T(8,128)(2,1)S(1)} %collective-permute-done.1.refs_4_), channel_id=1, source_target_pairs={{0,16},{16,0},{1,17},{17,1},{2,18},{18,2},{3,19},{19,3},{4,20},{20... | collective-permute-start | bytes 688136 | tf_op jit(solution)/shard_map/ppermute | solution.py:112
  32.8 4.1 %collective-permute-done.18.refs_8_ = bf16[64,1792]{1,0:T(8,128)(2,1)S(1)} collective-permute-done((bf16[64,1792]{1,0:T(8,128)(2,1)S(1)}, bf16[64,1792]{1,0:T(8,128)(2,1)S(1)}, u32[]{:S(2)}, u32[]{:S(2)}) %collective-permute-start.18) | collective-permute-done | bytes 229408 | tf_op jit(solution)/shard_map/ppermute | solution.py:112
  36.9 0.5 collective-permute-start.7
  37.4 1.2 %collective-permute-done.9.refs_0_ = bf16[64,1792]{1,0:T(8,128)(2,1)S(1)} collective-permute-done((bf16[64,1792]{1,0:T(8,128)(2,1)S(1)}, bf16[64,1792]{1,0:T(8,128)(2,1)S(1)}, u32[]{:S(2)}, u32[]{:S(2)}) %collective-permute-start.9) | collective-permute-done | bytes 229408 | tf_op jit(solution)/shard_map/ppermute | solution.py:106
  38.6 0.5 collective-permute-start.12
  39.1 1.7 %collective-permute-done.2.refs_0_ = bf16[64,1792]{1,0:T(8,128)(2,1)S(1)} collective-permute-done((bf16[64,1792]{1,0:T(8,128)(2,1)S(1)}, bf16[64,1792]{1,0:T(8,128)(2,1)S(1)}, u32[]{:S(2)}, u32[]{:S(2)}) %collective-permute-start.2) | collective-permute-done | bytes 229408 | tf_op jit(solution)/shard_map/ppermute | solution.py:112
  40.8 0.7 %copy-done.8 = s32[1,128]{1,0:T(1,128)S(1)} copy-done((s32[1,128]{1,0:T(1,128)S(1)}, s32[1,128]{1,0:T(1,128)}, u32[]{:S(2)}) %copy-start.8) | copy-done | bytes 536
  41.5 0.5 shard_map.91.refs_8_
  42.0 0.8 %shard_map.92.refs_12_ = f32[128,128]{1,0:T(8,128)S(1)} custom-call(bf16[128,8192]{1,0:T(8,128)(2,1)S(1)} %copy-done.1, bf16[128,28672]{1,0:T(8,128)(2,1)S(1)} %copy-done, bf16[64,1792]{1,0:T(8,128)(2,1)S(1)} %collective-permute-done.22.refs_0_, bf16[64,512]{1,0:T(8,128)(2,1)S(1)} %collective-permute-done.23.refs_1_, ...), custom_call_target="tpu_custom_call" | custom-call | flops 150994944 | bytes 2359296 | tf_op jit(solution)/shard_map/pallas_call | solution.py:83
  42.9 1.2 %shard_map.93.refs_4_ = f32[128,128]{1,0:T(8,128)S(1)} custom-call(bf16[128,8192]{1,0:T(8,128)(2,1)S(1)} %copy-done.1, bf16[128,28672]{1,0:T(8,128)(2,1)S(1)} %copy-done, bf16[64,1792]{1,0:T(8,128)(2,1)S(1)} %collective-permute-done.refs_0_, bf16[64,512]{1,0:T(8,128)(2,1)S(1)} %collective-permute-done.3.refs_1_, ...), custom_call_target="tpu_custom_call" | custom-call | flops 226492416 | bytes 3538944 | tf_op jit(solution)/shard_map/pallas_call | solution.py:83
  44.6 0.5 shard_map.95.refs_0_
  45.2 2.7 %collective-permute-start.34 = (bf16[136,128]{1,0:T(8,128)(2,1)S(1)}, bf16[136,128]{1,0:T(8,128)(2,1)S(1)}, u32[]{:S(2)}, u32[]{:S(2)}) collective-permute-start(bf16[136,128]{1,0:T(8,128)(2,1)S(1)} %shard_map.95.refs_0_), channel_id=1, source_target_pairs={{0,12},{1,13},{2,14},{3,15},{4,8},{5,9},{6,10},{7,11},{8,4},{9,5},... | collective-permute-start | bytes 104456 | tf_op jit(solution)/shard_map/ppermute | solution.py:23
  47.9 1.8 %collective-permute-start.30 = (bf16[136,128]{1,0:T(8,128)(2,1)S(1)}, bf16[136,128]{1,0:T(8,128)(2,1)S(1)}, u32[]{:S(2)}, u32[]{:S(2)}) collective-permute-start(bf16[136,128]{1,0:T(8,128)(2,1)S(1)} %shard_map.95.refs_0_), channel_id=1, source_target_pairs={{0,8},{1,9},{2,10},{3,11},{4,12},{5,13},{6,14},{7,15},{8,0},{9,1},... | collective-permute-start | bytes 104456 | tf_op jit(solution)/shard_map/ppermute | solution.py:23
  49.6 1.2 %collective-permute-start.33 = (bf16[136,128]{1,0:T(8,128)(2,1)S(1)}, bf16[136,128]{1,0:T(8,128)(2,1)S(1)}, u32[]{:S(2)}, u32[]{:S(2)}) collective-permute-start(bf16[136,128]{1,0:T(8,128)(2,1)S(1)} %shard_map.95.refs_0_), channel_id=1, source_target_pairs={{0,2},{1,3},{2,0},{3,1},{4,6},{5,7},{6,4},{7,5},{8,10},{9,11},{10,... | collective-permute-start | bytes 104456 | tf_op jit(solution)/shard_map/ppermute | solution.py:23
  50.8 0.5 collective-permute-done.34.refs_1_
  51.3 0.8 %collective-permute-done.36.refs_2_ = bf16[136,128]{1,0:T(8,128)(2,1)S(1)} collective-permute-done((bf16[136,128]{1,0:T(8,128)(2,1)S(1)}, bf16[136,128]{1,0:T(8,128)(2,1)S(1)}, u32[]{:S(2)}, u32[]{:S(2)}) %collective-permute-start.36) | collective-permute-done | bytes 34848 | tf_op jit(solution)/shard_map/ppermute | solution.py:23
  52.2 0.5 collective-permute-done.30.refs_3_
  52.7 1.2 %collective-permute-start.35 = (bf16[136,128]{1,0:T(8,128)(2,1)S(1)}, bf16[136,128]{1,0:T(8,128)(2,1)S(1)}, u32[]{:S(2)}, u32[]{:S(2)}) collective-permute-start(bf16[136,128]{1,0:T(8,128)(2,1)S(1)} %collective-permute-done.34.refs_1_), channel_id=1, source_target_pairs={{0,2},{1,3},{2,0},{3,1},{4,6},{5,7},{6,4},{7,5},{8,10},{9,11},{10,... | collective-permute-start | bytes 104456 | tf_op jit(solution)/shard_map/ppermute | solution.py:23
  53.9 0.8 %collective-permute-start.37 = (bf16[136,128]{1,0:T(8,128)(2,1)S(1)}, bf16[136,128]{1,0:T(8,128)(2,1)S(1)}, u32[]{:S(2)}, u32[]{:S(2)}) collective-permute-start(bf16[136,128]{1,0:T(8,128)(2,1)S(1)} %collective-permute-done.36.refs_2_), channel_id=1, source_target_pairs={{0,2},{1,3},{2,0},{3,1},{4,6},{5,7},{6,4},{7,5},{8,10},{9,11},{10,... | collective-permute-start | bytes 104456 | tf_op jit(solution)/shard_map/ppermute | solution.py:23
  54.7 1.2 %collective-permute-start.31 = (bf16[136,128]{1,0:T(8,128)(2,1)S(1)}, bf16[136,128]{1,0:T(8,128)(2,1)S(1)}, u32[]{:S(2)}, u32[]{:S(2)}) collective-permute-start(bf16[136,128]{1,0:T(8,128)(2,1)S(1)} %collective-permute-done.30.refs_3_), channel_id=1, source_target_pairs={{0,2},{1,3},{2,0},{3,1},{4,6},{5,7},{6,4},{7,5},{8,10},{9,11},{10,... | collective-permute-start | bytes 104456 | tf_op jit(solution)/shard_map/ppermute | solution.py:23
  56.0 0.5 collective-permute-start.38
  56.5 0.5 collective-permute-done.35.refs_1_
  57.0 0.9 %collective-permute-done.37.refs_2_ = bf16[136,128]{1,0:T(8,128)(2,1)S(1)} collective-permute-done((bf16[136,128]{1,0:T(8,128)(2,1)S(1)}, bf16[136,128]{1,0:T(8,128)(2,1)S(1)}, u32[]{:S(2)}, u32[]{:S(2)}) %collective-permute-start.37) | collective-permute-done | bytes 34848 | tf_op jit(solution)/shard_map/ppermute | solution.py:23
  57.9 0.8 %collective-permute-done.31.refs_3_ = bf16[136,128]{1,0:T(8,128)(2,1)S(1)} collective-permute-done((bf16[136,128]{1,0:T(8,128)(2,1)S(1)}, bf16[136,128]{1,0:T(8,128)(2,1)S(1)}, u32[]{:S(2)}, u32[]{:S(2)}) %collective-permute-start.31) | collective-permute-done | bytes 34848 | tf_op jit(solution)/shard_map/ppermute | solution.py:23
  58.7 1.3 %precondition.1.query = bf16[512,64]{1,0:T(8,128)(2,1)S(1)} custom-call(f32[8,4096]{1,0:T(8,128)S(1)} %copy-done.4, f32[64,64]{1,0:T(8,128)S(1)} %copy-done.5, f32[64,64]{1,0:T(8,128)S(1)} %copy-done.6, f32[64,64]{1,0:T(8,128)S(1)} %copy-done.7), custom_call_target="tpu_custom_call" | custom-call | flops 10000000000 | bytes 131072 | tf_op jit(solution)/shard_map/precondition/pallas_call | solution.py:191
  60.9 0.6 shard_map.98.refs_1_
  61.5 1.0 %shard_map.99 = f32[8,128]{1,0:T(8,128)} custom-call(bf16[512,64]{1,0:T(8,128)(2,1)S(1)} %precondition.1.query, bf16[136,128]{1,0:T(8,128)(2,1)S(1)} %collective-permute-done.32.refs_0_, f32[8,128]{1,0:T(8,128)S(1)} %shard_map.98.refs_1_), custom_call_target="tpu_custom_call" | custom-call | flops 8388608 | bytes 34816 | tf_op jit(solution)/shard_map/pallas_call | solution.py:244
  (71 shorter events, 3.0 us)
Async XLA Ops:
  0.0 41.5 %copy-start.2 = (bf16[64,1792]{1,0:T(8,128)(2,1)S(1)}, bf16[64,1792]{1,0:T(8,128)(2,1)}, u32[]{:S(2)}) copy-start(bf16[64,1792]{1,0:T(8,128)(2,1)} %refs_0_.1) | copy-start | bytes 688132
  0.0 41.5 %copy-start = (bf16[128,28672]{1,0:T(8,128)(2,1)S(1)}, bf16[128,28672]{1,0:T(8,128)(2,1)}, u32[]{:S(2)}) copy-start(bf16[128,28672]{1,0:T(8,128)(2,1)} %grad.9) | copy-start | bytes 22020100
  0.0 41.5 %copy-start.1 = (bf16[128,8192]{1,0:T(8,128)(2,1)S(1)}, bf16[128,8192]{1,0:T(8,128)(2,1)}, u32[]{:S(2)}) copy-start(bf16[128,8192]{1,0:T(8,128)(2,1)} %act.9) | copy-start | bytes 6291460
  0.0 7.7 %collective-permute-start.10 = (bf16[64,512]{1,0:T(8,128)(2,1)}, bf16[64,512]{1,0:T(8,128)(2,1)S(1)}, u32[]{:S(2)}, u32[]{:S(2)}) collective-permute-start(bf16[64,512]{1,0:T(8,128)(2,1)} %refs_1_.1), channel_id=1, source_target_pairs={{0,4},{1,5},{2,6},{3,7},{4,0},{5,1},{6,2},{7,3},{8,12},{9,13},{10,... | collective-permute-start | bytes 196616 | tf_op jit(solution)/shard_map/ppermute | solution.py:106
  3.1 5.5 %collective-permute-start.23 = (bf16[64,512]{1,0:T(8,128)(2,1)}, bf16[64,512]{1,0:T(8,128)(2,1)S(1)}, u32[]{:S(2)}, u32[]{:S(2)}) collective-permute-start(bf16[64,512]{1,0:T(8,128)(2,1)} %refs_1_.1), channel_id=1, source_target_pairs={{0,2},{1,3},{2,0},{3,1},{4,6},{5,7},{6,4},{7,5},{8,10},{9,11},{10,... | collective-permute-start | bytes 196616 | tf_op jit(solution)/shard_map/ppermute | solution.py:106
  4.7 5.9 %collective-permute-start.29 = (bf16[64,512]{1,0:T(8,128)(2,1)}, bf16[64,512]{1,0:T(8,128)(2,1)S(1)}, u32[]{:S(2)}, u32[]{:S(2)}) collective-permute-start(bf16[64,512]{1,0:T(8,128)(2,1)} %refs_1_.1), channel_id=1, source_target_pairs={{0,1},{1,0},{2,3},{3,2},{4,5},{5,4},{6,7},{7,6},{8,9},{9,8},{10,11... | collective-permute-start | bytes 196616 | tf_op jit(solution)/shard_map/ppermute | solution.py:127
  4.7 7.0 %collective-permute-start.3 = (bf16[64,512]{1,0:T(8,128)(2,1)}, bf16[64,512]{1,0:T(8,128)(2,1)S(1)}, u32[]{:S(2)}, u32[]{:S(2)}) collective-permute-start(bf16[64,512]{1,0:T(8,128)(2,1)} %refs_1_.1), channel_id=1, source_target_pairs={{0,8},{1,9},{2,10},{3,11},{4,12},{5,13},{6,14},{7,15},{8,0},{9,1},... | collective-permute-start | bytes 196616 | tf_op jit(solution)/shard_map/ppermute | solution.py:106
  7.2 12.8 %collective-permute-start.8 = (bf16[64,1792]{1,0:T(8,128)(2,1)}, bf16[64,1792]{1,0:T(8,128)(2,1)S(1)}, u32[]{:S(2)}, u32[]{:S(2)}) collective-permute-start(bf16[64,1792]{1,0:T(8,128)(2,1)} %refs_0_.1), channel_id=1, source_target_pairs={{0,4},{1,5},{2,6},{3,7},{4,0},{5,1},{6,2},{7,3},{8,12},{9,13},{10,... | collective-permute-start | bytes 688136 | tf_op jit(solution)/shard_map/ppermute | solution.py:106
  7.7 13.7 %collective-permute-start = (bf16[64,1792]{1,0:T(8,128)(2,1)}, bf16[64,1792]{1,0:T(8,128)(2,1)S(1)}, u32[]{:S(2)}, u32[]{:S(2)}) collective-permute-start(bf16[64,1792]{1,0:T(8,128)(2,1)} %refs_0_.1), channel_id=1, source_target_pairs={{0,8},{1,9},{2,10},{3,11},{4,12},{5,13},{6,14},{7,15},{8,0},{9,1},... | collective-permute-start | bytes 688136 | tf_op jit(solution)/shard_map/ppermute | solution.py:106
  8.6 13.4 %collective-permute-start.22 = (bf16[64,1792]{1,0:T(8,128)(2,1)}, bf16[64,1792]{1,0:T(8,128)(2,1)S(1)}, u32[]{:S(2)}, u32[]{:S(2)}) collective-permute-start(bf16[64,1792]{1,0:T(8,128)(2,1)} %refs_0_.1), channel_id=1, source_target_pairs={{0,2},{1,3},{2,0},{3,1},{4,6},{5,7},{6,4},{7,5},{8,10},{9,11},{10,... | collective-permute-start | bytes 688136 | tf_op jit(solution)/shard_map/ppermute | solution.py:106
  10.5 1.3 %collective-permute-start.27 = (bf16[64,512]{1,0:T(8,128)(2,1)S(1)}, bf16[64,512]{1,0:T(8,128)(2,1)S(1)}, u32[]{:S(2)}, u32[]{:S(2)}) collective-permute-start(bf16[64,512]{1,0:T(8,128)(2,1)S(1)} %collective-permute-done.10.refs_5_), channel_id=1, source_target_pairs={{0,1},{1,0},{2,3},{3,2},{4,5},{5,4},{6,7},{7,6},{8,9},{9,8},{10,11... | collective-permute-start | bytes 196616 | tf_op jit(solution)/shard_map/ppermute | solution.py:127
  11.7 1.3 %collective-permute-start.25 = (bf16[64,512]{1,0:T(8,128)(2,1)S(1)}, bf16[64,512]{1,0:T(8,128)(2,1)S(1)}, u32[]{:S(2)}, u32[]{:S(2)}) collective-permute-start(bf16[64,512]{1,0:T(8,128)(2,1)S(1)} %collective-permute-done.23.refs_1_), channel_id=1, source_target_pairs={{0,1},{1,0},{2,3},{3,2},{4,5},{5,4},{6,7},{7,6},{8,9},{9,8},{10,11... | collective-permute-start | bytes 196616 | tf_op jit(solution)/shard_map/ppermute | solution.py:127
  11.8 5.1 %collective-permute-start.4 = (bf16[64,512]{1,0:T(8,128)(2,1)S(1)}, bf16[64,512]{1,0:T(8,128)(2,1)S(1)}, u32[]{:S(2)}, u32[]{:S(2)}) collective-permute-start(bf16[64,512]{1,0:T(8,128)(2,1)S(1)} %collective-permute-done.3.refs_1_), channel_id=1, source_target_pairs={{0,2},{1,3},{2,0},{3,1},{4,6},{5,7},{6,4},{7,5},{8,10},{9,11},{10,... | collective-permute-start | bytes 196616 | tf_op jit(solution)/shard_map/ppermute | solution.py:106
  13.0 4.3 %collective-permute-start.19 = (bf16[64,512]{1,0:T(8,128)(2,1)S(1)}, bf16[64,512]{1,0:T(8,128)(2,1)S(1)}, u32[]{:S(2)}, u32[]{:S(2)}) collective-permute-start(bf16[64,512]{1,0:T(8,128)(2,1)S(1)} %collective-permute-done.3.refs_1_), channel_id=1, source_target_pairs={{0,16},{16,0},{1,17},{17,1},{2,18},{18,2},{3,19},{19,3},{4,20},{20... | collective-permute-start | bytes 196616 | tf_op jit(solution)/shard_map/ppermute | solution.py:112
  16.8 1.3 %collective-permute-start.15 = (bf16[64,512]{1,0:T(8,128)(2,1)S(1)}, bf16[64,512]{1,0:T(8,128)(2,1)S(1)}, u32[]{:S(2)}, u32[]{:S(2)}) collective-permute-start(bf16[64,512]{1,0:T(8,128)(2,1)S(1)} %collective-permute-done.3.refs_1_), channel_id=1, source_target_pairs={{0,1},{1,0},{2,3},{3,2},{4,5},{5,4},{6,7},{7,6},{8,9},{9,8},{10,11... | collective-permute-start | bytes 196616 | tf_op jit(solution)/shard_map/ppermute | solution.py:127
  17.2 4.8 %collective-permute-start.11 = (bf16[64,512]{1,0:T(8,128)(2,1)S(1)}, bf16[64,512]{1,0:T(8,128)(2,1)S(1)}, u32[]{:S(2)}, u32[]{:S(2)}) collective-permute-start(bf16[64,512]{1,0:T(8,128)(2,1)S(1)} %collective-permute-done.10.refs_5_), channel_id=1, source_target_pairs={{0,2},{1,3},{2,0},{3,1},{4,6},{5,7},{6,4},{7,5},{8,10},{9,11},{10,... | collective-permute-start | bytes 196616 | tf_op jit(solution)/shard_map/ppermute | solution.py:106
  18.2 12.4 %collective-permute-start.28 = (bf16[64,1792]{1,0:T(8,128)(2,1)}, bf16[64,1792]{1,0:T(8,128)(2,1)S(1)}, u32[]{:S(2)}, u32[]{:S(2)}) collective-permute-start(bf16[64,1792]{1,0:T(8,128)(2,1)} %refs_0_.1), channel_id=1, source_target_pairs={{0,1},{1,0},{2,3},{3,2},{4,5},{5,4},{6,7},{7,6},{8,9},{9,8},{10,11... | collective-permute-start | bytes 688136 | tf_op jit(solution)/shard_map/ppermute | solution.py:127
  20.1 10.5 %collective-permute-start.26 = (bf16[64,1792]{1,0:T(8,128)(2,1)S(1)}, bf16[64,1792]{1,0:T(8,128)(2,1)S(1)}, u32[]{:S(2)}, u32[]{:S(2)}) collective-permute-start(bf16[64,1792]{1,0:T(8,128)(2,1)S(1)} %collective-permute-done.8.refs_4_), channel_id=1, source_target_pairs={{0,1},{1,0},{2,3},{3,2},{4,5},{5,4},{6,7},{7,6},{8,9},{9,8},{10,11... | collective-permute-start | bytes 688136 | tf_op jit(solution)/shard_map/ppermute | solution.py:127
  21.4 10.4 %collective-permute-start.1 = (bf16[64,1792]{1,0:T(8,128)(2,1)S(1)}, bf16[64,1792]{1,0:T(8,128)(2,1)S(1)}, u32[]{:S(2)}, u32[]{:S(2)}) collective-permute-start(bf16[64,1792]{1,0:T(8,128)(2,1)S(1)} %collective-permute-done.refs_0_), channel_id=1, source_target_pairs={{0,2},{1,3},{2,0},{3,1},{4,6},{5,7},{6,4},{7,5},{8,10},{9,11},{10,... | collective-permute-start | bytes 688136 | tf_op jit(solution)/shard_map/ppermute | solution.py:106
  22.0 10.0 %collective-permute-start.24 = (bf16[64,1792]{1,0:T(8,128)(2,1)S(1)}, bf16[64,1792]{1,0:T(8,128)(2,1)S(1)}, u32[]{:S(2)}, u32[]{:S(2)}) collective-permute-start(bf16[64,1792]{1,0:T(8,128)(2,1)S(1)} %collective-permute-done.22.refs_0_), channel_id=1, source_target_pairs={{0,1},{1,0},{2,3},{3,2},{4,5},{5,4},{6,7},{7,6},{8,9},{9,8},{10,11... | collective-permute-start | bytes 688136 | tf_op jit(solution)/shard_map/ppermute | solution.py:127
  22.0 1.6 %collective-permute-start.17 = (bf16[64,512]{1,0:T(8,128)(2,1)S(1)}, bf16[64,512]{1,0:T(8,128)(2,1)S(1)}, u32[]{:S(2)}, u32[]{:S(2)}) collective-permute-start(bf16[64,512]{1,0:T(8,128)(2,1)S(1)} %collective-permute-done.4.refs_5_), channel_id=1, source_target_pairs={{0,1},{1,0},{2,3},{3,2},{4,5},{5,4},{6,7},{7,6},{8,9},{9,8},{10,11... | collective-permute-start | bytes 196616 | tf_op jit(solution)/shard_map/ppermute | solution.py:127
  23.6 1.3 %collective-permute-start.21 = (bf16[64,512]{1,0:T(8,128)(2,1)S(1)}, bf16[64,512]{1,0:T(8,128)(2,1)S(1)}, u32[]{:S(2)}, u32[]{:S(2)}) collective-permute-start(bf16[64,512]{1,0:T(8,128)(2,1)S(1)} %collective-permute-done.19.refs_9_), channel_id=1, source_target_pairs={{0,1},{1,0},{2,3},{3,2},{4,5},{5,4},{6,7},{7,6},{8,9},{9,8},{10,11... | collective-permute-start | bytes 196616 | tf_op jit(solution)/shard_map/ppermute | solution.py:127
  24.8 4.3 %collective-permute-start.5 = (bf16[64,512]{1,0:T(8,128)(2,1)S(1)}, bf16[64,512]{1,0:T(8,128)(2,1)S(1)}, u32[]{:S(2)}, u32[]{:S(2)}) collective-permute-start(bf16[64,512]{1,0:T(8,128)(2,1)S(1)} %collective-permute-done.4.refs_5_), channel_id=1, source_target_pairs={{0,16},{16,0},{1,17},{17,1},{2,18},{18,2},{3,19},{19,3},{4,20},{20... | collective-permute-start | bytes 196616 | tf_op jit(solution)/shard_map/ppermute | solution.py:112
  29.1 7.8 %collective-permute-start.18 = (bf16[64,1792]{1,0:T(8,128)(2,1)S(1)}, bf16[64,1792]{1,0:T(8,128)(2,1)S(1)}, u32[]{:S(2)}, u32[]{:S(2)}) collective-permute-start(bf16[64,1792]{1,0:T(8,128)(2,1)S(1)} %collective-permute-done.refs_0_), channel_id=1, source_target_pairs={{0,16},{16,0},{1,17},{17,1},{2,18},{18,2},{3,19},{19,3},{4,20},{20... | collective-permute-start | bytes 688136 | tf_op jit(solution)/shard_map/ppermute | solution.py:112
  30.6 6.3 %collective-permute-start.14 = (bf16[64,1792]{1,0:T(8,128)(2,1)S(1)}, bf16[64,1792]{1,0:T(8,128)(2,1)S(1)}, u32[]{:S(2)}, u32[]{:S(2)}) collective-permute-start(bf16[64,1792]{1,0:T(8,128)(2,1)S(1)} %collective-permute-done.refs_0_), channel_id=1, source_target_pairs={{0,1},{1,0},{2,3},{3,2},{4,5},{5,4},{6,7},{7,6},{8,9},{9,8},{10,11... | collective-permute-start | bytes 688136 | tf_op jit(solution)/shard_map/ppermute | solution.py:127
  30.6 8.0 %collective-permute-start.9 = (bf16[64,1792]{1,0:T(8,128)(2,1)S(1)}, bf16[64,1792]{1,0:T(8,128)(2,1)S(1)}, u32[]{:S(2)}, u32[]{:S(2)}) collective-permute-start(bf16[64,1792]{1,0:T(8,128)(2,1)S(1)} %collective-permute-done.8.refs_4_), channel_id=1, source_target_pairs={{0,2},{1,3},{2,0},{3,1},{4,6},{5,7},{6,4},{7,5},{8,10},{9,11},{10,... | collective-permute-start | bytes 688136 | tf_op jit(solution)/shard_map/ppermute | solution.py:106
  31.8 6.8 %collective-permute-start.16 = (bf16[64,1792]{1,0:T(8,128)(2,1)S(1)}, bf16[64,1792]{1,0:T(8,128)(2,1)S(1)}, u32[]{:S(2)}, u32[]{:S(2)}) collective-permute-start(bf16[64,1792]{1,0:T(8,128)(2,1)S(1)} %collective-permute-done.1.refs_4_), channel_id=1, source_target_pairs={{0,1},{1,0},{2,3},{3,2},{4,5},{5,4},{6,7},{7,6},{8,9},{9,8},{10,11... | collective-permute-start | bytes 688136 | tf_op jit(solution)/shard_map/ppermute | solution.py:127
  32.0 8.8 %collective-permute-start.2 = (bf16[64,1792]{1,0:T(8,128)(2,1)S(1)}, bf16[64,1792]{1,0:T(8,128)(2,1)S(1)}, u32[]{:S(2)}, u32[]{:S(2)}) collective-permute-start(bf16[64,1792]{1,0:T(8,128)(2,1)S(1)} %collective-permute-done.1.refs_4_), channel_id=1, source_target_pairs={{0,16},{16,0},{1,17},{17,1},{2,18},{18,2},{3,19},{19,3},{4,20},{20... | collective-permute-start | bytes 688136 | tf_op jit(solution)/shard_map/ppermute | solution.py:112
  36.9 7.2 %collective-permute-start.13 = (bf16[64,512]{1,0:T(8,128)(2,1)S(1)}, bf16[64,512]{1,0:T(8,128)(2,1)S(1)}, u32[]{:S(2)}, u32[]{:S(2)}) collective-permute-start(bf16[64,512]{1,0:T(8,128)(2,1)S(1)} %collective-permute-done.11.refs_1_), channel_id=1, source_target_pairs={{0,1},{1,0},{2,3},{3,2},{4,5},{5,4},{6,7},{7,6},{8,9},{9,8},{10,11... | collective-permute-start | bytes 196616 | tf_op jit(solution)/shard_map/ppermute | solution.py:127
  36.9 7.7 %collective-permute-start.7 = (bf16[64,512]{1,0:T(8,128)(2,1)S(1)}, bf16[64,512]{1,0:T(8,128)(2,1)S(1)}, u32[]{:S(2)}, u32[]{:S(2)}) collective-permute-start(bf16[64,512]{1,0:T(8,128)(2,1)S(1)} %collective-permute-done.5.refs_1_), channel_id=1, source_target_pairs={{0,1},{1,0},{2,3},{3,2},{4,5},{5,4},{6,7},{7,6},{8,9},{9,8},{10,11... | collective-permute-start | bytes 196616 | tf_op jit(solution)/shard_map/ppermute | solution.py:127
  38.6 4.3 %collective-permute-start.20 = (bf16[64,1792]{1,0:T(8,128)(2,1)S(1)}, bf16[64,1792]{1,0:T(8,128)(2,1)S(1)}, u32[]{:S(2)}, u32[]{:S(2)}) collective-permute-start(bf16[64,1792]{1,0:T(8,128)(2,1)S(1)} %collective-permute-done.18.refs_8_), channel_id=1, source_target_pairs={{0,1},{1,0},{2,3},{3,2},{4,5},{5,4},{6,7},{7,6},{8,9},{9,8},{10,11... | collective-permute-start | bytes 688136 | tf_op jit(solution)/shard_map/ppermute | solution.py:127
  38.6 5.5 %collective-permute-start.12 = (bf16[64,1792]{1,0:T(8,128)(2,1)S(1)}, bf16[64,1792]{1,0:T(8,128)(2,1)S(1)}, u32[]{:S(2)}, u32[]{:S(2)}) collective-permute-start(bf16[64,1792]{1,0:T(8,128)(2,1)S(1)} %collective-permute-done.9.refs_0_), channel_id=1, source_target_pairs={{0,1},{1,0},{2,3},{3,2},{4,5},{5,4},{6,7},{7,6},{8,9},{9,8},{10,11... | collective-permute-start | bytes 688136 | tf_op jit(solution)/shard_map/ppermute | solution.py:127
  40.8 3.8 %collective-permute-start.6 = (bf16[64,1792]{1,0:T(8,128)(2,1)S(1)}, bf16[64,1792]{1,0:T(8,128)(2,1)S(1)}, u32[]{:S(2)}, u32[]{:S(2)}) collective-permute-start(bf16[64,1792]{1,0:T(8,128)(2,1)S(1)} %collective-permute-done.2.refs_0_), channel_id=1, source_target_pairs={{0,1},{1,0},{2,3},{3,2},{4,5},{5,4},{6,7},{7,6},{8,9},{9,8},{10,11... | collective-permute-start | bytes 688136 | tf_op jit(solution)/shard_map/ppermute | solution.py:127
  45.2 6.2 %collective-permute-start.34 = (bf16[136,128]{1,0:T(8,128)(2,1)S(1)}, bf16[136,128]{1,0:T(8,128)(2,1)S(1)}, u32[]{:S(2)}, u32[]{:S(2)}) collective-permute-start(bf16[136,128]{1,0:T(8,128)(2,1)S(1)} %shard_map.95.refs_0_), channel_id=1, source_target_pairs={{0,12},{1,13},{2,14},{3,15},{4,8},{5,9},{6,10},{7,11},{8,4},{9,5},... | collective-permute-start | bytes 104456 | tf_op jit(solution)/shard_map/ppermute | solution.py:23
  47.8 4.3 %collective-permute-start.36 = (bf16[136,128]{1,0:T(8,128)(2,1)S(1)}, bf16[136,128]{1,0:T(8,128)(2,1)S(1)}, u32[]{:S(2)}, u32[]{:S(2)}) collective-permute-start(bf16[136,128]{1,0:T(8,128)(2,1)S(1)} %shard_map.95.refs_0_), channel_id=1, source_target_pairs={{0,4},{1,5},{2,6},{3,7},{4,0},{5,1},{6,2},{7,3},{8,12},{9,13},{10,... | collective-permute-start | bytes 104456 | tf_op jit(solution)/shard_map/ppermute | solution.py:23
  47.9 4.8 %collective-permute-start.30 = (bf16[136,128]{1,0:T(8,128)(2,1)S(1)}, bf16[136,128]{1,0:T(8,128)(2,1)S(1)}, u32[]{:S(2)}, u32[]{:S(2)}) collective-permute-start(bf16[136,128]{1,0:T(8,128)(2,1)S(1)} %shard_map.95.refs_0_), channel_id=1, source_target_pairs={{0,8},{1,9},{2,10},{3,11},{4,12},{5,13},{6,14},{7,15},{8,0},{9,1},... | collective-permute-start | bytes 104456 | tf_op jit(solution)/shard_map/ppermute | solution.py:23
  49.6 4.3 %collective-permute-start.41 = (bf16[136,128]{1,0:T(8,128)(2,1)S(1)}, bf16[136,128]{1,0:T(8,128)(2,1)S(1)}, u32[]{:S(2)}, u32[]{:S(2)}) collective-permute-start(bf16[136,128]{1,0:T(8,128)(2,1)S(1)} %shard_map.95.refs_0_), channel_id=1, source_target_pairs={{0,1},{1,0},{2,3},{3,2},{4,5},{5,4},{6,7},{7,6},{8,9},{9,8},{10,11... | collective-permute-start | bytes 104456 | tf_op jit(solution)/shard_map/ppermute | solution.py:23
  49.6 5.1 %collective-permute-start.33 = (bf16[136,128]{1,0:T(8,128)(2,1)S(1)}, bf16[136,128]{1,0:T(8,128)(2,1)S(1)}, u32[]{:S(2)}, u32[]{:S(2)}) collective-permute-start(bf16[136,128]{1,0:T(8,128)(2,1)S(1)} %shard_map.95.refs_0_), channel_id=1, source_target_pairs={{0,2},{1,3},{2,0},{3,1},{4,6},{5,7},{6,4},{7,5},{8,10},{9,11},{10,... | collective-permute-start | bytes 104456 | tf_op jit(solution)/shard_map/ppermute | solution.py:23
  51.3 4.6 %collective-permute-start.42 = (bf16[136,128]{1,0:T(8,128)(2,1)S(1)}, bf16[136,128]{1,0:T(8,128)(2,1)S(1)}, u32[]{:S(2)}, u32[]{:S(2)}) collective-permute-start(bf16[136,128]{1,0:T(8,128)(2,1)S(1)} %collective-permute-done.34.refs_1_), channel_id=1, source_target_pairs={{0,1},{1,0},{2,3},{3,2},{4,5},{5,4},{6,7},{7,6},{8,9},{9,8},{10,11... | collective-permute-start | bytes 104456 | tf_op jit(solution)/shard_map/ppermute | solution.py:23
  52.2 3.8 %collective-permute-start.43 = (bf16[136,128]{1,0:T(8,128)(2,1)S(1)}, bf16[136,128]{1,0:T(8,128)(2,1)S(1)}, u32[]{:S(2)}, u32[]{:S(2)}) collective-permute-start(bf16[136,128]{1,0:T(8,128)(2,1)S(1)} %collective-permute-done.36.refs_2_), channel_id=1, source_target_pairs={{0,1},{1,0},{2,3},{3,2},{4,5},{5,4},{6,7},{7,6},{8,9},{9,8},{10,11... | collective-permute-start | bytes 104456 | tf_op jit(solution)/shard_map/ppermute | solution.py:23
  52.7 4.3 %collective-permute-start.35 = (bf16[136,128]{1,0:T(8,128)(2,1)S(1)}, bf16[136,128]{1,0:T(8,128)(2,1)S(1)}, u32[]{:S(2)}, u32[]{:S(2)}) collective-permute-start(bf16[136,128]{1,0:T(8,128)(2,1)S(1)} %collective-permute-done.34.refs_1_), channel_id=1, source_target_pairs={{0,2},{1,3},{2,0},{3,1},{4,6},{5,7},{6,4},{7,5},{8,10},{9,11},{10,... | collective-permute-start | bytes 104456 | tf_op jit(solution)/shard_map/ppermute | solution.py:23
  53.9 3.9 %collective-permute-start.37 = (bf16[136,128]{1,0:T(8,128)(2,1)S(1)}, bf16[136,128]{1,0:T(8,128)(2,1)S(1)}, u32[]{:S(2)}, u32[]{:S(2)}) collective-permute-start(bf16[136,128]{1,0:T(8,128)(2,1)S(1)} %collective-permute-done.36.refs_2_), channel_id=1, source_target_pairs={{0,2},{1,3},{2,0},{3,1},{4,6},{5,7},{6,4},{7,5},{8,10},{9,11},{10,... | collective-permute-start | bytes 104456 | tf_op jit(solution)/shard_map/ppermute | solution.py:23
  54.7 3.9 %collective-permute-start.31 = (bf16[136,128]{1,0:T(8,128)(2,1)S(1)}, bf16[136,128]{1,0:T(8,128)(2,1)S(1)}, u32[]{:S(2)}, u32[]{:S(2)}) collective-permute-start(bf16[136,128]{1,0:T(8,128)(2,1)S(1)} %collective-permute-done.30.refs_3_), channel_id=1, source_target_pairs={{0,2},{1,3},{2,0},{3,1},{4,6},{5,7},{6,4},{7,5},{8,10},{9,11},{10,... | collective-permute-start | bytes 104456 | tf_op jit(solution)/shard_map/ppermute | solution.py:23
  56.0 4.4 %collective-permute-start.44 = (bf16[136,128]{1,0:T(8,128)(2,1)S(1)}, bf16[136,128]{1,0:T(8,128)(2,1)S(1)}, u32[]{:S(2)}, u32[]{:S(2)}) collective-permute-start(bf16[136,128]{1,0:T(8,128)(2,1)S(1)} %collective-permute-done.30.refs_3_), channel_id=1, source_target_pairs={{0,1},{1,0},{2,3},{3,2},{4,5},{5,4},{6,7},{7,6},{8,9},{9,8},{10,11... | collective-permute-start | bytes 104456 | tf_op jit(solution)/shard_map/ppermute | solution.py:23
  56.0 4.9 %collective-permute-start.38 = (bf16[136,128]{1,0:T(8,128)(2,1)S(1)}, bf16[136,128]{1,0:T(8,128)(2,1)S(1)}, u32[]{:S(2)}, u32[]{:S(2)}) collective-permute-start(bf16[136,128]{1,0:T(8,128)(2,1)S(1)} %collective-permute-done.33.refs_0_), channel_id=1, source_target_pairs={{0,1},{1,0},{2,3},{3,2},{4,5},{5,4},{6,7},{7,6},{8,9},{9,8},{10,11... | collective-permute-start | bytes 104456 | tf_op jit(solution)/shard_map/ppermute | solution.py:23
  57.0 3.9 %collective-permute-start.39 = (bf16[136,128]{1,0:T(8,128)(2,1)S(1)}, bf16[136,128]{1,0:T(8,128)(2,1)S(1)}, u32[]{:S(2)}, u32[]{:S(2)}) collective-permute-start(bf16[136,128]{1,0:T(8,128)(2,1)S(1)} %collective-permute-done.35.refs_1_), channel_id=1, source_target_pairs={{0,1},{1,0},{2,3},{3,2},{4,5},{5,4},{6,7},{7,6},{8,9},{9,8},{10,11... | collective-permute-start | bytes 104456 | tf_op jit(solution)/shard_map/ppermute | solution.py:23
  57.9 3.0 %collective-permute-start.40 = (bf16[136,128]{1,0:T(8,128)(2,1)S(1)}, bf16[136,128]{1,0:T(8,128)(2,1)S(1)}, u32[]{:S(2)}, u32[]{:S(2)}) collective-permute-start(bf16[136,128]{1,0:T(8,128)(2,1)S(1)} %collective-permute-done.37.refs_2_), channel_id=1, source_target_pairs={{0,1},{1,0},{2,3},{3,2},{4,5},{5,4},{6,7},{7,6},{8,9},{9,8},{10,11... | collective-permute-start | bytes 104456 | tf_op jit(solution)/shard_map/ppermute | solution.py:23
  58.7 2.8 %collective-permute-start.32 = (bf16[136,128]{1,0:T(8,128)(2,1)S(1)}, bf16[136,128]{1,0:T(8,128)(2,1)S(1)}, u32[]{:S(2)}, u32[]{:S(2)}) collective-permute-start(bf16[136,128]{1,0:T(8,128)(2,1)S(1)} %collective-permute-done.31.refs_3_), channel_id=1, source_target_pairs={{0,1},{1,0},{2,3},{3,2},{4,5},{5,4},{6,7},{7,6},{8,9},{9,8},{10,11... | collective-permute-start | bytes 104456 | tf_op jit(solution)/shard_map/ppermute | solution.py:23
  (6 other events, 98.5 us)
